TPU v7x, 32 devices: a whole 2x2x4 slice. The times are simulated.
32 devices in a mesh: group: 4 (over y, core), dp: 2 (over x), mp: 4 (over z).
Axes of the slice: x: 2, y: 2, z: 4, core: 2. Of those that a mesh axis runs over, the one named last changes fastest.
Arguments:
- audio_states: bfloat16 [4, 1024, 1280], P('group', ('dp', 'mp')), may hold values from -6 to 6
- image_states: bfloat16 [4, 1024, 3200], P('group', ('dp', 'mp')), may hold values from -6 to 6
- audio_gain: float32 [1280], replicated, may hold values from 0.1 to 1.9
- image_gain: float32 [3200], replicated, may hold values from 0.1 to 1.9
- audio_proj: bfloat16 [1280, 8192], P('dp', 'mp'), may hold values from -1 to 1
- image_proj: bfloat16 [3200, 8192], P('dp', 'mp'), may hold values from -1 to 1
- block_rows: int32 [2, 2, 4], replicated, may hold values from 1 to 128
- destination: int32 [2, 2, 4], replicated, may hold values from 0 to 3, as said below
- input_gain: float32 [8192], P('mp'), may hold values from 0.1 to 1.9
- kv_weight: bfloat16 [8192, 2048], P('mp'), may hold values from -0.09375 to 0.09375
Outputs:
- key_values: bfloat16 [4, 1024, 2048], P('group', 'dp', 'mp')
- backbone_rows: bfloat16 [4, 1024, 8192], P('group', 'dp', 'mp')
Inputs may be any that keep to these rules, and one draw needn't show every extreme that they name: `destination`: every backbone device receives exactly 2 blocks of each stream; an encoder index of dp sends either none or exactly 1 block of its stream to a backbone device.
All inputs are finite; a program needn't handle non-finite values.
Results may differ from a plain program's by a relative error of at most 0.012.
Values may be sent and summed in bfloat16 or wider, within the bound.
No kernel may reach another device: no remote copies, remote signals or barrier semaphores. Data moves between devices by JAX's collectives and lax.ppermute only.
A program may use at most 128 MiB of HBM per device.

v0:
```python
import jax
import jax.numpy as jnp
from jax import lax
from jax.sharding import PartitionSpec as P

BLOCK = 128
BLOCKS = 4


EPS_LAYER = 1e-05
EPS_ROOT = 1e-06


def layer_norm(values_in, gain_vec):
    values = values_in.astype(jnp.float32)
    center = values - jnp.mean(values, axis=-1, keepdims=True)
    spread = jnp.mean(center * center, axis=-1, keepdims=True)
    return center * lax.rsqrt(spread + EPS_LAYER) * gain_vec


def route_tables(destination, dest_count):
    flat_dest = destination.reshape(-1)
    hit_table = (flat_dest[:, None] == jnp.arange(dest_count, dtype=jnp.int32)[None, :]).astype(
        jnp.int32
    )
    dest_rank = jnp.sum((jnp.cumsum(hit_table, axis=0) - 1) * hit_table, axis=1)
    per_source = hit_table.reshape(-1, BLOCKS, dest_count)
    dest_slot = jnp.sum((jnp.cumsum(per_source, axis=1) - 1) * per_source, axis=2).reshape(-1)
    return (flat_dest, dest_rank, dest_slot)


def send_index(flat_dest, dest_slot, source, targets, capacity):
    row_dest = lax.dynamic_slice_in_dim(flat_dest, source * BLOCKS, BLOCKS)
    row_slot = lax.dynamic_slice_in_dim(dest_slot, source * BLOCKS, BLOCKS)
    wanted_slot = jnp.arange(capacity, dtype=jnp.int32)
    matches = (row_dest[None, None, :] == targets[:, None, None]) & (
        row_slot[None, None, :] == wanted_slot[None, :, None]
    )
    block_ids = jnp.arange(BLOCKS, dtype=jnp.int32)
    picked_index = jnp.sum(matches.astype(jnp.int32) * block_ids[None, None, :], axis=2).reshape(-1)
    present = jnp.any(matches, axis=2).reshape(-1)
    return (picked_index, present)


def route_blocks(blocks, streams, destination, group_id, dp_index):
    dp_count = lax.axis_size("dp")
    dest_count = 2 * dp_count
    capacity = BLOCKS // 4
    flat_dest, dest_rank, dest_slot = route_tables(destination, dest_count)
    serial = jnp.arange(dest_count, dtype=jnp.int32)
    outgoing = []
    for source_blocks, stream in zip(blocks, streams):
        picked_index, present = send_index(
            flat_dest, dest_slot, stream * dp_count + dp_index, serial, capacity
        )
        present = present & (group_id == stream)
        picked = jnp.take(source_blocks, picked_index, axis=0).reshape(dest_count * capacity, -1)
        outgoing.append(jnp.where(present[:, None], picked, jnp.zeros_like(picked)))
    packed = jnp.concatenate(outgoing, axis=1)
    spare_rows = jnp.zeros_like(packed)
    moved_rows = lax.all_to_all(
        jnp.concatenate([spare_rows, packed], axis=0),
        ("group", "dp"),
        split_axis=0,
        concat_axis=0,
        tiled=True,
    )
    arrived = moved_rows[: dest_count * capacity]
    my_index = (group_id - 2) * dp_count + dp_index
    on_backbone = group_id >= 2
    block_count = flat_dest.shape[0]
    source_slot = jnp.arange(block_count, dtype=jnp.int32) // BLOCKS * capacity + dest_slot
    results = []
    offset = 0
    for source_blocks, stream in zip(blocks, streams):
        slot_width = source_blocks[0].size
        columns = arrived[:, offset : offset + slot_width]
        offset = offset + slot_width
        wanted = stream * (BLOCKS // 2) + jnp.arange(BLOCKS // 2, dtype=jnp.int32)
        matches = (flat_dest[None, :] == my_index) & (dest_rank[None, :] == wanted[:, None])
        picked_index = jnp.sum(matches.astype(jnp.int32) * source_slot[None, :], axis=1)
        taken_rows = jnp.take(columns, picked_index, axis=0)
        taken_rows = jnp.where(on_backbone, taken_rows, jnp.zeros_like(taken_rows))
        results.append(taken_rows.reshape((wanted.shape[0],) + source_blocks.shape[1:]))
    return results


def project(audio_rows, image_rows, audio_active, image_active, audio_proj, image_proj):

    def folder(row_block, active, running, shard_part):
        return lax.cond(
            active,
            lambda inner: jnp.dot(row_block, shard_part, preferred_element_type=jnp.float32),
            lambda inner: inner,
            running,
        )

    audio_start = jnp.zeros((audio_rows.shape[0], audio_proj.shape[1]), jnp.float32)
    image_start = jnp.zeros((image_rows.shape[0], image_proj.shape[1]), jnp.float32)
    audio_out = folder(
        audio_rows, audio_active, audio_start, lax.all_gather(audio_proj, "dp", axis=0, tiled=True)
    )
    image_out = folder(
        image_rows, image_active, image_start, lax.all_gather(image_proj, "dp", axis=0, tiled=True)
    )
    return (audio_out, image_out)


def shards(
    audio_states,
    image_states,
    audio_gain,
    image_gain,
    audio_proj,
    image_proj,
    block_rows,
    destination,
    input_gain,
    kv_weight,
):
    group_id = lax.axis_index("group")
    dp_index = lax.axis_index("dp")
    mp_index = lax.axis_index("mp")
    mp_count = lax.axis_size("mp")
    share = BLOCK // mp_count
    row_ids = mp_index * share + jnp.arange(share, dtype=jnp.int32)

    def encode(states, gain_vec, stream):
        limits = lax.dynamic_index_in_dim(block_rows[stream], dp_index, 0, keepdims=False)
        keep_rows = (row_ids[None, :] < limits[:, None]).astype(jnp.float32)
        normed = layer_norm(states[0], gain_vec).reshape(BLOCKS, share, -1)
        return (normed * keep_rows[:, :, None]).astype(jnp.bfloat16)

    audio_normed = encode(audio_states, audio_gain, 0)
    image_normed = encode(image_states, image_gain, 1)
    on_backbone = group_id >= 2
    audio_part, image_part = route_blocks(
        (audio_normed, image_normed), (0, 1), destination, group_id, dp_index
    )
    audio_full, image_full = (
        lax.all_gather(audio_part, "mp", axis=1, tiled=True),
        lax.all_gather(image_part, "mp", axis=1, tiled=True),
    )
    audio_out, image_out = project(
        audio_full.reshape(-1, audio_full.shape[2]),
        image_full.reshape(-1, image_full.shape[2]),
        on_backbone,
        on_backbone,
        audio_proj,
        image_proj,
    )
    arrived = (
        jnp.concatenate([audio_out, image_out], axis=0)
        .astype(jnp.bfloat16)
        .reshape(BLOCKS, BLOCK, -1)
    )
    token_rows = arrived.reshape(BLOCKS * BLOCK, -1)
    tokens = token_rows.astype(jnp.float32)
    squares = lax.psum(jnp.sum(tokens * tokens, axis=1), "mp")
    scaled = (tokens * input_gain).astype(jnp.bfloat16)
    partial_value = jnp.dot(scaled, kv_weight, preferred_element_type=jnp.float32)
    summed = lax.psum_scatter(partial_value, "mp", scatter_dimension=1, tiled=True)
    full_width = tokens.shape[1] * mp_count
    result = summed * lax.rsqrt(squares / full_width + EPS_ROOT)[:, None]
    return (result.astype(jnp.bfloat16)[None], token_rows[None])


def solution(mesh):
    in_specs = (
        P("group", ("dp", "mp"), None),
        P("group", ("dp", "mp"), None),
        P(),
        P(),
        P("dp", "mp"),
        P("dp", "mp"),
        P(),
        P(),
        P("mp"),
        P("mp", None),
    )
    out_specs = (P("group", "dp", "mp"), P("group", "dp", "mp"))
    return jax.shard_map(shards, mesh=mesh, in_specs=in_specs, out_specs=out_specs, check_vma=False)
```

profile of v0, /device:TPU:0, one launch (start us, length us, event | category | flops | bytes accessed | tf_op | source)
XLA Modules:
  0.0 409.1 jit_solution(4111425705348617540)
XLA Ops:
  7.3 0.7 all-gather.4.cloned.1.call-update
  8.0 0.4 copy-done
  8.3 0.2 convert_reduce_fusion
  8.5 0.4 fusion.10
  9.2 0.2 select_reduce_fusion
  9.6 0.1 select_reduce_fusion.2
  9.8 0.1 select_reduce_fusion.3
  9.9 0.2 fusion.20
  10.1 0.1 convert_reduce_fusion.1
  10.2 0.2 fusion.12
  10.7 0.4 multiply_convert_fusion
  11.2 0.7 gather_fusion.1
  11.8 0.4 copy.16
  12.4 0.3 multiply_convert_fusion.2
  12.7 0.6 gather_fusion
  13.3 0.3 copy.15
  13.6 0.5 select_select_fusion
  14.0 0.2 select_select_fusion.1
  14.3 4.3 %fusion.5 = bf16[8,1,143360]{2,0,1:T(8,128)(2,1)S(1)} fusion(bf16[4,102400]{1,0:T(4,128)(2,1)S(1)} %select_select_fusion, bf16[4,40960]{1,0:T(4,128)(2,1)S(1)} %select_select_fusion.1), kind=kLoop, calls=%fused_computation.12 | loop fusion | flops 8028160 | bytes 3440640 | tf_op jit(solution)/shard_map/all_to_all | solution.py:61
  18.6 0.5 broadcast.561
  19.1 3.1 reduce.6
  22.2 5.2 %reshape.588 = bf16[8,2,71680]{2,1,0:T(2,128)(2,1)} reshape(bf16[8,143360]{1,0:T(8,128)(2,1)} %reduce.6) | data formatting | bytes 4587520
  27.4 5.2 %all-to-all-start = ((bf16[8,2,71680]{2,1,0:T(2,128)(2,1)}), bf16[8,2,71680]{2,1,0:T(2,128)(2,1)S(1)}, u32[]{:S(2)}, u32[]{:S(2)}) async-start(bf16[8,2,71680]{2,1,0:T(2,128)(2,1)} %reshape.588), calls=%async_computation | async-start | bytes 4587520 | tf_op jit(solution)/shard_map/all_to_all | solution.py:61
  32.8 0.2 select_reduce_fusion.1
  33.0 0.2 fusion.23
  33.2 52.6 %all-to-all-done = bf16[8,2,71680]{2,1,0:T(2,128)(2,1)S(1)} async-done(((bf16[8,2,71680]{2,1,0:T(2,128)(2,1)}), bf16[8,2,71680]{2,1,0:T(2,128)(2,1)S(1)}, u32[]{:S(2)}, u32[]{:S(2)}) %all-to-all-start) | async-done | bytes 2293792 | tf_op jit(solution)/shard_map/all_to_all | solution.py:61
  85.9 4.5 %reshape.589 = bf16[8,1,143360]{2,1,0:T(2,128)(2,1)} reshape(bf16[8,2,71680]{2,1,0:T(2,128)(2,1)S(1)} %all-to-all-done) | data formatting | bytes 4587520
  90.4 4.0 copy.22
  94.4 0.2 slice.28
  94.6 1.1 gather_fusion.3
  95.7 0.9 fusion.14
  96.7 0.7 all-gather.8.cloned.1.call-update
  97.6 0.8 gather_fusion.2
  98.3 0.1 fusion.15
  98.4 18.4 %all_gather.12 = bf16[2,128,1280]{2,1,0:T(8,128)(2,1)S(1)} all-gather(bf16[2,32,1280]{2,1,0:T(8,128)(2,1)S(1)} %fusion.15), channel_id=1, replica_groups=mesh['group'=4,'dp'=2,'mp'=4] {'mp'}, dimensions={1}, use_global_device_ids=true | all-gather | bytes 819200 | tf_op jit(solution)/shard_map/all_gather | solution.py:141
  116.8 0.1 conditional.2
  116.8 0.1 broadcast.491
  117.0 28.7 %all-gather.6.cloned.1.call-done = bf16[2,128,3200]{2,1,0:T(8,128)(2,1)} async-done(((bf16[2,32,3200]{2,1,0:T(8,128)(2,1)}), bf16[2,128,3200]{2,1,0:T(8,128)(2,1)}) %all-gather.6.cloned.1.call-update) | async-done | bytes 1638416 | tf_op jit(solution)/shard_map/all_gather | solution.py:142
  145.7 158.7 %all-gather.8.cloned.1.call-done = bf16[3200,2048]{1,0:T(8,128)(2,1)} async-done(((bf16[1600,2048]{1,0:T(8,128)(2,1)}), bf16[3200,2048]{1,0:T(8,128)(2,1)}) %all-gather.8.cloned.1.call-update) | async-done | bytes 13107216 | tf_op jit(solution)/shard_map/all_gather | solution.py:104
  304.4 0.1 conditional.3
  304.4 0.1 broadcast.492
  304.5 0.6 copy-done.6
  305.1 10.0 %fusion.6 = f32[512,2048]{1,0:T(8,128)} fusion(bf16[2048,2048]{1,0:T(8,128)(2,1)} %param.23, f32[2048]{0:T(1024)S(1)} %copy-done.6, bf16[256,2048]{1,0:T(8,128)(2,1)S(1)} %get-tuple-element.41, bf16[256,2048]{1,0:T(8,128)(2,1)S(1)} %get-tuple-element.40), kind=kOutput, calls=%fused_computation.14 | convolution fusion | flops 4301258752 | bytes 14688256 | tf_op jit(solution)/shard_map/dot_general | solution.py:161
  315.1 0.5 fusion.3
  315.6 11.7 %psum.7 = f32[512]{0:T(512)S(1)} all-reduce(f32[512]{0:T(512)S(1)} %fusion.3), channel_id=1, replica_groups=mesh['group'=4,'dp'=2,'mp'=4] {'mp'}, use_global_device_ids=true, to_apply=%region_20.21 | all-reduce | flops 512 | bytes 4096 | tf_op jit(solution)/shard_map/psum | solution.py:159
  327.3 1.5 pad_maximum_fusion.1
  328.8 71.6 %reduce-scatter.2.cloned.1.call-done = f32[512,512]{1,0:T(8,128)} async-done(((f32[512,2048]{1,0:T(8,128)}), f32[512,512]{1,0:T(8,128)}) %reduce-scatter.2.cloned.1.call-update) | async-done | bytes 1048592 | tf_op jit(solution)/shard_map/reduce_scatter | solution.py:162
  400.4 2.2 fusion.13
  (56 shorter events, 1.4 us)
Async XLA Ops:
  7.2 1.1 copy-start
  7.2 1.8 copy-start.2
  7.2 2.9 copy-start.1
  7.2 3.3 copy-start.5
  7.2 3.5 copy-start.3
  7.2 109.6 %all-gather.4.cloned.1.call-start = ((), (), s32[]{:S(2)}) async-start(), calls=%async_computation.2 | async-start | bytes 7864320 | tf_op jit(solution)/shard_map/all_gather | solution.py:101
  10.7 1.6 copy-start.4
  27.4 58.5 %all-to-all-start = ((bf16[8,2,71680]{2,1,0:T(2,128)(2,1)}), bf16[8,2,71680]{2,1,0:T(2,128)(2,1)S(1)}, u32[]{:S(2)}, u32[]{:S(2)}) async-start(bf16[8,2,71680]{2,1,0:T(2,128)(2,1)} %reshape.588), calls=%async_computation | async-start | bytes 4587520 | tf_op jit(solution)/shard_map/all_to_all | solution.py:61
  32.6 113.1 %all-gather.6.cloned.1.call-start = ((), (), s32[]{:S(2)}) async-start(), calls=%async_computation.3 | async-start | bytes 2048000 | tf_op jit(solution)/shard_map/all_gather | solution.py:142
  96.6 207.8 %all-gather.8.cloned.1.call-start = ((), (), s32[]{:S(2)}) async-start(), calls=%async_computation.4 | async-start | bytes 19660800 | tf_op jit(solution)/shard_map/all_gather | solution.py:104
  97.4 303.0 %reduce-scatter.2.cloned.1.call-start = ((), (), s32[]{:S(2)}) async-start(), calls=%async_computation.5 | async-start | bytes 5242880 | tf_op jit(solution)/shard_map/reduce_scatter | solution.py:162
  304.4 0.7 copy-start.6
Sparse Core Ops, SparseCore 0:
  9.6 95.8 all-gather.3
  107.6 38.0 all-gather.5
  147.3 157.0 all-gather.7
  315.3 85.0 reduce-scatter.1
where the time goes:
time: 409 us
  waiting for transfers between devices  313 us (77%)
  blocking collectives  30.1 us (7%)
  local copies, waits for them, and re-layouts  20.1 us (5%)
  other arithmetic  16.3 us (4%)
  between operations  14.1 us (3%)
  matrix products  10 us (2%)
  starting transfers between devices  5.39 us (1%)
    all_gather x1, waiting for transfers between devices, project(): lax.all_gather(image_proj, 'dp', axis=0, tiled=True)  159 us
    reduce_scatter x1, waiting for transfers between devices, shards(): lax.psum_scatter(partial_value, 'mp', scatter_dimension=1, tiled=True)  71.6 us
    all_to_all x1, waiting for transfers between devices, route_blocks(): lax.all_to_all(jnp.concatenate([spare_rows, packed], axis=0), ('group', '...  52.6 us
    all_gather x1, waiting for transfers between devices, shards(): lax.all_gather(image_part, 'mp', axis=1, tiled=True)  28.7 us
    all_gather x1, blocking collectives, shards(): lax.all_gather(audio_part, 'mp', axis=1, tiled=True)  18.4 us
    unnamed x19, local copies, waits for them, and re-layouts  15.4 us
    psum x1, blocking collectives, shards(): squares = lax.psum(jnp.sum(tokens * tokens, axis=1), 'mp')  11.7 us
    dot_general x1, matrix products, shards(): jnp.dot(scaled, kv_weight, preferred_element_type=jnp.float32)  10 us
  transfers between devices with their start and end apart: 5, of which 4 were waited for; matrix products, arithmetic and copies ran while one was open for 8% of the time, Pallas kernels for 0%

commit v1 on v0

--- a/solution.py
+++ b/solution.py
@@ -1,7 +1,12 @@
+import functools
+
 import jax
 import jax.numpy as jnp
 from jax import lax
+from jax.experimental import pallas as pl
+from jax.experimental.pallas import tpu as pltpu
 from jax.sharding import PartitionSpec as P
+
 
 BLOCK = 128
 BLOCKS = 4
@@ -106,7 +111,7 @@
     return (audio_out, image_out)
 
 
-def shards(
+def shards_general(
     audio_states,
     image_states,
     audio_gain,
@@ -165,7 +170,248 @@
     return (result.astype(jnp.bfloat16)[None], token_rows[None])
 
 
+MIB = 1 << 20
+
+
+def smem():
+    return pl.BlockSpec(memory_space=pltpu.SMEM)
+
+
+def vmem():
+    return pl.BlockSpec(memory_space=pltpu.VMEM)
+
+
+def limits_of(mib, flops=0):
+    return dict(
+        compiler_params=pltpu.CompilerParams(vmem_limit_bytes=mib * MIB),
+        cost_estimate=pl.CostEstimate(flops=flops, transcendentals=0, bytes_accessed=0),
+    )
+
+
+def encode_kernel(dp_count, meta, dest, limits, *refs):
+    group, dp, mp = meta[0], meta[1], meta[2]
+    targets = 2 * dp_count
+    inputs, messages = refs[:4], refs[4:]
+    for stream in range(2):
+        states, gain = inputs[2 * stream : 2 * stream + 2]
+        outs = messages[stream * targets : (stream + 1) * targets]
+        share = states.shape[1] // BLOCKS
+        half = outs[0].shape[1]
+
+        @pl.when(group == stream)
+        def _():
+            scale = gain[...].reshape(1, -1)
+            for target in range(targets):
+                block = jnp.int32(0)
+                for b in range(BLOCKS):
+                    block = jnp.where(dest[stream, dp, b] == target, b, block)
+                limit = limits[stream, dp, block]
+                start = pl.multiple_of(block * share, share)
+                values = states[0, pl.ds(start, share), :].astype(jnp.float32)
+                center = values - jnp.mean(values, axis=-1, keepdims=True)
+                spread = jnp.mean(center * center, axis=-1, keepdims=True)
+                normed = center * lax.rsqrt(spread + EPS_LAYER) * scale
+                row = mp * share + lax.broadcasted_iota(jnp.int32, normed.shape, 0)
+                normed = jnp.where(row < limit, normed, 0.0).astype(jnp.bfloat16)
+                c, home = target // dp_count, target % dp_count
+                for k in range(dp_count):
+                    place = 0 if home == k else 1
+                    outs[c * dp_count + k][place * share : (place + 1) * share, :] = normed[
+                        :, k * half : (k + 1) * half
+                    ]
+
+
+def encode(dp_count, meta, dest, limits, streams):
+    arguments, shapes = [], []
+    for states, gain, _ in streams:
+        _, rows, width = states.shape
+        arguments += [states, gain]
+        shape = jax.ShapeDtypeStruct((2 * rows // BLOCKS, width // dp_count), jnp.bfloat16)
+        shapes += [shape] * (2 * dp_count)
+    return pl.pallas_call(
+        functools.partial(encode_kernel, dp_count),
+        out_shape=shapes,
+        in_specs=[smem()] * 3 + [vmem()] * len(arguments),
+        out_specs=[vmem()] * len(shapes),
+        name="encode",
+        **limits_of(8, 1 << 28),
+    )(meta, dest, limits, *arguments)
+
+
+def project_kernel(mp_count, tile, meta, *refs):
+    pieces, weight, keep, send, rows = refs[:mp_count], *refs[mp_count:]
+    share = pieces[0].shape[0] // 2
+    block = share * mp_count
+    for shift in range(mp_count):
+        source = lax.rem(meta[2] + (mp_count - shift), mp_count)
+        start = pl.multiple_of(source * share, share)
+        rows[pl.ds(start, share), :] = pieces[shift][:share, :]
+        rows[pl.ds(block + start, share), :] = pieces[shift][share:, :]
+    for first in range(0, weight.shape[1], tile):
+        out = jnp.dot(
+            rows[...], weight[:, first : first + tile], preferred_element_type=jnp.float32
+        )
+        keep[:, first : first + tile] = out[:block]
+        send[:, first : first + tile] = out[block:].astype(jnp.bfloat16)
+
+
+def project_rows(mp_count, meta, pieces, weight, tile):
+    depth, width = weight.shape
+    rows = pieces[0].shape[0] * mp_count
+    return pl.pallas_call(
+        functools.partial(project_kernel, mp_count, tile),
+        out_shape=[
+            jax.ShapeDtypeStruct((rows // 2, width), jnp.float32),
+            jax.ShapeDtypeStruct((rows // 2, width), jnp.bfloat16),
+        ],
+        in_specs=[smem()] + [vmem()] * (mp_count + 1),
+        out_specs=[vmem()] * 2,
+        scratch_shapes=[pltpu.VMEM((rows, depth), jnp.bfloat16)],
+        name="project",
+        **limits_of(12, 2 * rows * depth * width),
+    )(meta, *pieces, weight)
+
+
+def heads_kernel(mp_count, meta, keep, other, gain, weight, tokens, own, *rest):
+    sends, scaled = rest[:-1], rest[-1]
+    rows, tile = own.shape[0] - 8, own.shape[1]
+    rounded = (keep[...] + other[...].astype(jnp.float32)).astype(jnp.bfloat16)
+    tokens[...] = rounded
+    values = rounded.astype(jnp.float32)
+    scaled[...] = (values * gain[...].reshape(1, -1)).astype(jnp.bfloat16)
+    total = jnp.sum(values * values, axis=1, keepdims=True)
+    turned = jnp.transpose(jnp.broadcast_to(total, (rows, 128)))[:8]
+    high = turned.astype(jnp.bfloat16).astype(jnp.float32)
+    line = lax.broadcasted_iota(jnp.int32, turned.shape, 0)
+    packed = jnp.where(line == 0, high, jnp.where(line == 1, turned - high, 0.0))
+    packed = jnp.concatenate([packed] + [jnp.zeros((8, tile - rows), jnp.float32)], axis=1)
+    for shift in list(range(1, mp_count)) + [0]:
+        chunk = lax.rem(meta[2] + shift, mp_count)
+        columns = pl.ds(pl.multiple_of(chunk * tile, tile), tile)
+        out = jnp.dot(scaled[...], weight[:, columns], preferred_element_type=jnp.float32)
+        if shift:
+            block = jnp.concatenate([out, packed], axis=0)
+            sends[shift - 1][...] = block.astype(jnp.bfloat16)
+        else:
+            own[:rows, :] = out
+            own[rows:, :] = packed
+
+
+def heads(mp_count, meta, keep, other, gain, weight):
+    rows, width = keep.shape
+    tile = weight.shape[1] // mp_count
+    return pl.pallas_call(
+        functools.partial(heads_kernel, mp_count),
+        in_specs=[smem()] + [vmem()] * 4,
+        out_specs=[vmem()] * (1 + mp_count),
+        scratch_shapes=[pltpu.VMEM((rows, width), jnp.bfloat16)],
+        out_shape=[
+            jax.ShapeDtypeStruct((rows, width), jnp.bfloat16),
+            jax.ShapeDtypeStruct((rows + 8, tile), jnp.float32),
+        ]
+        + [jax.ShapeDtypeStruct((rows + 8, tile), jnp.bfloat16)] * (mp_count - 1),
+        name="heads",
+        **limits_of(14, 2 * rows * width * weight.shape[1]),
+    )(meta, keep, other, gain, weight)
+
+
+def finish_kernel(full_width, own, *refs):
+    parts, result = refs[:-1], refs[-1]
+    rows = result.shape[0]
+    total = own[...]
+    for part in parts:
+        total = total + part[...].astype(jnp.float32)
+    square = total[rows : rows + 1, :rows] + total[rows + 1 : rows + 2, :rows]
+    scale = lax.rsqrt(square / full_width + EPS_ROOT)
+    column = jnp.transpose(jnp.broadcast_to(scale, (128, rows)))[:, :1]
+    result[...] = (total[:rows] * column).astype(jnp.bfloat16)
+
+
+def finish(full_width, own, parts):
+    rows, tile = own.shape
+    return pl.pallas_call(
+        functools.partial(finish_kernel, full_width),
+        out_shape=jax.ShapeDtypeStruct((rows - 8, tile), jnp.bfloat16),
+        in_specs=[vmem()] * (1 + len(parts)),
+        out_specs=vmem(),
+        name="finish",
+        **limits_of(4, 1 << 26),
+    )(own, *parts)
+
+
+def shards_direct(
+    audio_states,
+    image_states,
+    audio_gain,
+    image_gain,
+    audio_proj,
+    image_proj,
+    block_rows,
+    destination,
+    input_gain,
+    kv_weight,
+):
+    group = lax.axis_index("group")
+    dp = lax.axis_index("dp")
+    mp = lax.axis_index("mp")
+    dp_count = lax.axis_size("dp")
+    mp_count = lax.axis_size("mp")
+    meta = jnp.stack([group, dp, mp]).astype(jnp.int32)
+    rings = [[(i, (i + shift) % mp_count) for i in range(mp_count)] for shift in range(mp_count)]
+    swap = [(i, (i + 1) % dp_count) for i in range(dp_count)]
+    up = [(0, 2), (1, 3)]
+    on_backbone = group >= 2
+    mine = lax.rem(group, 2) * dp_count + dp
+    full_width = input_gain.shape[0] * mp_count
+    targets = 2 * dp_count
+    streams = (
+        (audio_states, audio_gain, audio_proj),
+        (image_states, image_gain, image_proj),
+    )
+
+    messages = encode(dp_count, meta, destination, block_rows, streams)
+    gathered = []
+    for stream in range(2):
+        piece = None
+        for index in range(targets):
+            c, k = index // dp_count, index % dp_count
+            pairs = [(stream * dp_count + d, (2 * d + c) * dp_count + k) for d in range(dp_count)]
+            moved = lax.ppermute(messages[stream * targets + index], ("group", "dp"), pairs)
+            piece = moved if piece is None else jnp.where(mine == index, moved, piece)
+        pieces = [piece]
+        for shift in range(1, mp_count):
+            pieces.append(lax.ppermute(piece, "mp", rings[shift]))
+        gathered.append(pieces)
+    partial, others = [], []
+    for stream, (_, _, proj) in enumerate(streams):
+        partial.append(project_rows(mp_count, meta, gathered[stream], proj, 512))
+        others.append(lax.ppermute(partial[stream][1], "dp", swap))
+    row_parts, head_parts = [], []
+    for stream in range(2):
+        tokens, own, *sends = heads(
+            mp_count, meta, partial[stream][0], others[stream], input_gain, kv_weight
+        )
+        sums = []
+        for shift, part in enumerate(sends, 1):
+            sums.append(lax.ppermute(part, "mp", rings[shift]))
+        row_parts += [lax.ppermute(tokens, "group", up), tokens]
+        values = finish(full_width, own, sums)
+        head_parts += [lax.ppermute(values, "group", up), values]
+    rows_out = jnp.concatenate(row_parts, axis=0)
+    heads_out = jnp.concatenate(head_parts, axis=0)
+    rows_out = jnp.where(on_backbone, rows_out, jnp.zeros_like(rows_out))
+    heads_out = jnp.where(on_backbone, heads_out, jnp.zeros_like(heads_out))
+    return (heads_out[None], rows_out[None])
+
+
 def solution(mesh):
+    if 2 * mesh.shape["dp"] != BLOCKS:
+        return mapped(shards_general, mesh)
+    layer = lambda *inputs: shards_direct(*inputs)
+    return mapped(layer, mesh)
+
+
+def mapped(shards, mesh):
     in_specs = (
         P("group", ("dp", "mp"), None),
         P("group", ("dp", "mp"), None),

time: 409 us -> 105 us (0.26)
  waiting for transfers between devices: 313 us -> 38.7 us
  starting transfers between devices: 5.39 us -> 43.7 us
  blocking collectives: 30.1 us -> 0 us
  other arithmetic: 16.3 us -> 2.77 us
  between operations: 14.1 us -> 0.9 us
  local copies, waits for them, and re-layouts: 20.1 us -> 9.5 us
  matrix products: 10 us -> 0 us
  Pallas kernels: 0 us -> 9.3 us
    all_gather x3 -> x0, waiting for transfers between devices: 187 us -> none  [the longest x1 159 us: project(): lax.all_gather(image_proj, 'dp', axis=0, tiled=True)]
    reduce_scatter x1 -> x0, waiting for transfers between devices: 71.6 us -> none  [shards(): lax.psum_scatter(partial_value, 'mp', scatter_dimension=1, tiled=True)]
    all_to_all x1 -> x0, waiting for transfers between devices: 52.6 us -> none  [route_blocks(): lax.all_to_all(jnp.concatenate([spare_rows, packed], axis=0), ('group', '...]
    ppermute x0 -> x26, starting transfers between devices: none -> 43.7 us  [the longest x8 12.7 us: shards_direct(): lax.ppermute(messages[stream * targets + index], ('group', 'dp'), pairs)]
    ppermute x0 -> x26, waiting for transfers between devices: none -> 38.7 us  [the longest x6 19.7 us: shards_direct(): pieces.append(lax.ppermute(piece, 'mp', rings[shift]))]
    all_gather x1 -> x0, blocking collectives: 18.4 us -> none  [shards(): lax.all_gather(audio_part, 'mp', axis=1, tiled=True)]
    psum x1 -> x0, blocking collectives: 11.7 us -> none  [shards(): squares = lax.psum(jnp.sum(tokens * tokens, axis=1), 'mp')]
    dot_general x1 -> x0, matrix products: 10 us -> none  [shards(): jnp.dot(scaled, kv_weight, preferred_element_type=jnp.float32)]
  transfers between devices with their start and end apart: 5 -> 26, of which waited for: 4 -> 8; matrix products, arithmetic and copies ran while one was open for 8% -> 1% of each run, Pallas kernels for 0% -> 8%
where the time goes in v1:
time: 105 us
  starting transfers between devices  43.7 us (42%)
  waiting for transfers between devices  38.7 us (37%)
  local copies, waits for them, and re-layouts  9.5 us (9%)
  Pallas kernels  9.3 us (9%)
  other arithmetic  2.77 us (3%)
    ppermute x6, waiting for transfers between devices, shards_direct(): pieces.append(lax.ppermute(piece, 'mp', rings[shift]))  19.7 us
    ppermute x8, starting transfers between devices, shards_direct(): lax.ppermute(messages[stream * targets + index], ('group', 'dp'), pairs)  12.7 us
    ppermute x6, starting transfers between devices, shards_direct(): sums.append(lax.ppermute(part, 'mp', rings[shift]))  12.2 us
    ppermute x6, starting transfers between devices, shards_direct(): pieces.append(lax.ppermute(piece, 'mp', rings[shift]))  10.9 us
    unnamed x20, local copies, waits for them, and re-layouts  9.5 us
    ppermute x2, waiting for transfers between devices, shards_direct(): others.append(lax.ppermute(partial[stream][1], 'dp', swap))  7.27 us
    ppermute x2, waiting for transfers between devices, shards_direct(): head_parts += [lax.ppermute(values, 'group', up), values]  7.01 us
    ppermute x6, waiting for transfers between devices, shards_direct(): sums.append(lax.ppermute(part, 'mp', rings[shift]))  4.66 us
  transfers between devices with their start and end apart: 26, of which 8 were waited for; matrix products, arithmetic and copies ran while one was open for 1% of the time, Pallas kernels for 8%

profile of v1, /device:TPU:0, one launch (start us, length us, event | category | flops | bytes accessed | tf_op | source)
XLA Modules:
  0.0 104.9 jit_solution(1699205016325176890)
XLA Ops:
  0.7 1.1 %copy-done.3 = bf16[1,128,3200]{2,1,0:T(8,128)(2,1)S(1)} copy-done((bf16[1,128,3200]{2,1,0:T(8,128)(2,1)S(1)}, bf16[1,128,3200]{2,1,0:T(8,128)(2,1)}, u32[]{:S(2)}) %copy-start.3) | copy-done | bytes 819224
  1.9 1.0 copy-done.4
  2.8 0.7 copy-done.6
  3.6 0.7 copy-done.7
  4.2 0.7 copy-done.8
  4.9 0.7 copy-done.9
  5.6 0.9 encode.1
  6.5 4.7 %collective-permute-start = (bf16[64,640]{1,0:T(8,128)(2,1)S(1)}, bf16[64,640]{1,0:T(8,128)(2,1)S(1)}, u32[]{:S(2)}, u32[]{:S(2)}) collective-permute-start(bf16[64,640]{1,0:T(8,128)(2,1)S(1)} %get-tuple-element.24), channel_id=1, source_target_pairs={{0,12},{4,28},{1,13},{5,29},{2,14},{6,30},{3,15},{7,31}} | collective-permute-start | bytes 245768 | tf_op jit(solution)/shard_map/ppermute | solution.py:379
  11.2 1.3 %collective-permute-start.1 = (bf16[64,640]{1,0:T(8,128)(2,1)S(1)}, bf16[64,640]{1,0:T(8,128)(2,1)S(1)}, u32[]{:S(2)}, u32[]{:S(2)}) collective-permute-start(bf16[64,640]{1,0:T(8,128)(2,1)S(1)} %get-tuple-element.25), channel_id=1, source_target_pairs={{0,8},{4,24},{1,9},{5,25},{2,10},{6,26},{3,11},{7,27}} | collective-permute-start | bytes 245768 | tf_op jit(solution)/shard_map/ppermute | solution.py:379
  12.5 2.7 %collective-permute-start.2 = (bf16[64,640]{1,0:T(8,128)(2,1)S(1)}, bf16[64,640]{1,0:T(8,128)(2,1)S(1)}, u32[]{:S(2)}, u32[]{:S(2)}) collective-permute-start(bf16[64,640]{1,0:T(8,128)(2,1)S(1)} %get-tuple-element.26), channel_id=1, source_target_pairs={{0,4},{4,20},{1,5},{5,21},{2,6},{6,22},{3,7},{7,23}} | collective-permute-start | bytes 245768 | tf_op jit(solution)/shard_map/ppermute | solution.py:379
  15.3 0.7 collective-permute-start.3
  16.0 0.7 collective-permute-start.12
  16.7 0.7 collective-permute-start.13
  17.4 0.7 collective-permute-start.14
  18.1 1.3 %collective-permute-start.15 = (bf16[64,1600]{1,0:T(8,128)(2,1)S(1)}, bf16[64,1600]{1,0:T(8,128)(2,1)S(1)}, u32[]{:S(2)}, u32[]{:S(2)}) collective-permute-start(bf16[64,1600]{1,0:T(8,128)(2,1)S(1)} %get-tuple-element.37), channel_id=1, source_target_pairs={{8,0},{12,16},{9,1},{13,17},{10,2},{14,18},{11,3},{15,19}} | collective-permute-start | bytes 614408 | tf_op jit(solution)/shard_map/ppermute | solution.py:379
  19.4 3.7 %collective-permute-start.6 = (bf16[64,640]{1,0:T(8,128)(2,1)S(1)}, bf16[64,640]{1,0:T(8,128)(2,1)S(1)}, u32[]{:S(2)}, u32[]{:S(2)}) collective-permute-start(bf16[64,640]{1,0:T(8,128)(2,1)S(1)} %select_select_fusion.1.refs_0_), channel_id=1, source_target_pairs={{0,3},{1,0},{2,1},{3,2},{4,7},{5,4},{6,5},{7,6},{8,11},{9,8},{10,9... | collective-permute-start | bytes 245768 | tf_op jit(solution)/shard_map/ppermute | solution.py:383
  23.2 2.8 %collective-permute-start.18 = (bf16[64,1600]{1,0:T(8,128)(2,1)S(1)}, bf16[64,1600]{1,0:T(8,128)(2,1)S(1)}, u32[]{:S(2)}, u32[]{:S(2)}) collective-permute-start(bf16[64,1600]{1,0:T(8,128)(2,1)S(1)} %select_select_fusion.refs_0_), channel_id=1, source_target_pairs={{0,3},{1,0},{2,1},{3,2},{4,7},{5,4},{6,5},{7,6},{8,11},{9,8},{10,9... | collective-permute-start | bytes 614408 | tf_op jit(solution)/shard_map/ppermute | solution.py:383
  26.0 1.0 collective-permute-start.16
  27.0 1.9 %collective-permute-start.5 = (bf16[64,640]{1,0:T(8,128)(2,1)S(1)}, bf16[64,640]{1,0:T(8,128)(2,1)S(1)}, u32[]{:S(2)}, u32[]{:S(2)}) collective-permute-start(bf16[64,640]{1,0:T(8,128)(2,1)S(1)} %select_select_fusion.1.refs_0_), channel_id=1, source_target_pairs={{0,2},{1,3},{2,0},{3,1},{4,6},{5,7},{6,4},{7,5},{8,10},{9,11},{10,... | collective-permute-start | bytes 245768 | tf_op jit(solution)/shard_map/ppermute | solution.py:383
  28.9 1.5 %collective-permute-start.4 = (bf16[64,640]{1,0:T(8,128)(2,1)S(1)}, bf16[64,640]{1,0:T(8,128)(2,1)S(1)}, u32[]{:S(2)}, u32[]{:S(2)}) collective-permute-start(bf16[64,640]{1,0:T(8,128)(2,1)S(1)} %select_select_fusion.1.refs_0_), channel_id=1, source_target_pairs={{0,1},{1,2},{2,3},{3,0},{4,5},{5,6},{6,7},{7,4},{8,9},{9,10},{10,1... | collective-permute-start | bytes 245768 | tf_op jit(solution)/shard_map/ppermute | solution.py:383
  30.4 19.7 %collective-permute-done.5.refs_2_ = bf16[64,640]{1,0:T(8,128)(2,1)S(1)} collective-permute-done((bf16[64,640]{1,0:T(8,128)(2,1)S(1)}, bf16[64,640]{1,0:T(8,128)(2,1)S(1)}, u32[]{:S(2)}, u32[]{:S(2)}) %collective-permute-start.5) | collective-permute-done | bytes 81952 | tf_op jit(solution)/shard_map/ppermute | solution.py:383
  50.0 1.7 %copy-done.2 = bf16[640,2048]{1,0:T(8,128)(2,1)S(1)} copy-done((bf16[640,2048]{1,0:T(8,128)(2,1)S(1)}, bf16[640,2048]{1,0:T(8,128)(2,1)}, u32[]{:S(2)}) %copy-start.2) | copy-done | bytes 2621464
  51.8 1.5 %project.2 = (f32[128,2048]{1,0:T(8,128)S(1)}, bf16[128,2048]{1,0:T(8,128)(2,1)S(1)}) custom-call(s32[3]{0:T(128)S(1)} %pad_add_fusion.meta, bf16[64,640]{1,0:T(8,128)(2,1)S(1)} %select_select_fusion.1.refs_0_, bf16[64,640]{1,0:T(8,128)(2,1)S(1)} %collective-permute-done.4.refs_1_, bf16[64,640]{1,0:T(8,128)(2,1)S(1)} %collective-permute-done.5.refs_2_, ...), custom_call_target="tpu_custom_call" | custom-call | flops 671088640 | tf_op jit(solution)/shard_map/project/pallas_call | solution.py:261
  53.3 0.9 collective-permute-start.7
  54.3 2.9 %copy-done.1 = bf16[1600,2048]{1,0:T(8,128)(2,1)S(1)} copy-done((bf16[1600,2048]{1,0:T(8,128)(2,1)S(1)}, bf16[1600,2048]{1,0:T(8,128)(2,1)}, u32[]{:S(2)}) %copy-start.1) | copy-done | bytes 6553624
  57.2 2.7 %project.3 = (f32[128,2048]{1,0:T(8,128)S(1)}, bf16[128,2048]{1,0:T(8,128)(2,1)S(1)}) custom-call(s32[3]{0:T(128)S(1)} %pad_add_fusion.meta, bf16[64,1600]{1,0:T(8,128)(2,1)S(1)} %select_select_fusion.refs_0_, bf16[64,1600]{1,0:T(8,128)(2,1)S(1)} %collective-permute-done.16.refs_1_, bf16[64,1600]{1,0:T(8,128)(2,1)S(1)} %collective-permute-done.17.refs_2_, ...), custom_call_target="tpu_custom_call" | custom-call | flops 1677721600 | tf_op jit(solution)/shard_map/project/pallas_call | solution.py:261
  59.9 1.2 %collective-permute-start.19 = (bf16[128,2048]{1,0:T(8,128)(2,1)S(1)}, bf16[128,2048]{1,0:T(8,128)(2,1)S(1)}, u32[]{:S(2)}, u32[]{:S(2)}) collective-permute-start(bf16[128,2048]{1,0:T(8,128)(2,1)S(1)} %get-tuple-element.39), channel_id=1, source_target_pairs={{0,4},{4,0},{1,5},{5,1},{2,6},{6,2},{3,7},{7,3},{8,12},{12,8},{9,1... | collective-permute-start | bytes 1572872 | tf_op jit(solution)/shard_map/ppermute | solution.py:388
  61.1 7.1 %collective-permute-done.7.other = bf16[128,2048]{1,0:T(8,128)(2,1)S(1)} collective-permute-done((bf16[128,2048]{1,0:T(8,128)(2,1)S(1)}, bf16[128,2048]{1,0:T(8,128)(2,1)S(1)}, u32[]{:S(2)}, u32[]{:S(2)}) %collective-permute-start.7) | collective-permute-done | bytes 524320 | tf_op jit(solution)/shard_map/ppermute | solution.py:388
  68.2 1.9 %heads.2 = (bf16[128,2048]{1,0:T(8,128)(2,1)S(1)}, f32[136,512]{1,0:T(8,128)S(1)}, bf16[136,512]{1,0:T(8,128)(2,1)S(1)}, bf16[136,512]{1,0:T(8,128)(2,1)S(1)}, bf16[136,512]{1,0:T(8,128)(2,1)S(1)}) custom-call(s32[3]{0:T(128)S(1)} %pad_add_fusion.meta, f32[128,2048]{1,0:T(8,128)S(1)} %get-tuple-element.28.keep, ...), custom_call_target="tpu_custom_call" | custom-call | flops 1073741824 | tf_op jit(solution)/shard_map/heads/pallas_call | solution.py:303
  70.1 1.1 %collective-permute-start.8 = (bf16[136,512]{1,0:T(8,128)(2,1)S(1)}, bf16[136,512]{1,0:T(8,128)(2,1)S(1)}, u32[]{:S(2)}, u32[]{:S(2)}) collective-permute-start(bf16[136,512]{1,0:T(8,128)(2,1)S(1)} %get-tuple-element.31), channel_id=1, source_target_pairs={{0,1},{1,2},{2,3},{3,0},{4,5},{5,6},{6,7},{7,4},{8,9},{9,10},{10,1... | collective-permute-start | bytes 417800 | tf_op jit(solution)/shard_map/ppermute | solution.py:396
  71.2 2.2 %collective-permute-start.9 = (bf16[136,512]{1,0:T(8,128)(2,1)S(1)}, bf16[136,512]{1,0:T(8,128)(2,1)S(1)}, u32[]{:S(2)}, u32[]{:S(2)}) collective-permute-start(bf16[136,512]{1,0:T(8,128)(2,1)S(1)} %get-tuple-element.32), channel_id=1, source_target_pairs={{0,2},{1,3},{2,0},{3,1},{4,6},{5,7},{6,4},{7,5},{8,10},{9,11},{10,... | collective-permute-start | bytes 417800 | tf_op jit(solution)/shard_map/ppermute | solution.py:396
  73.4 2.7 %collective-permute-start.10 = (bf16[136,512]{1,0:T(8,128)(2,1)S(1)}, bf16[136,512]{1,0:T(8,128)(2,1)S(1)}, u32[]{:S(2)}, u32[]{:S(2)}) collective-permute-start(bf16[136,512]{1,0:T(8,128)(2,1)S(1)} %get-tuple-element.33), channel_id=1, source_target_pairs={{0,3},{1,0},{2,1},{3,2},{4,7},{5,4},{6,5},{7,6},{8,11},{9,8},{10,9... | collective-permute-start | bytes 417800 | tf_op jit(solution)/shard_map/ppermute | solution.py:396
  76.1 1.9 %collective-permute-start.24 = (bf16[128,2048]{1,0:T(8,128)(2,1)S(1)}, bf16[128,2048]{1,0:T(8,128)(2,1)S(1)}, u32[]{:S(2)}, u32[]{:S(2)}) collective-permute-start(bf16[128,2048]{1,0:T(8,128)(2,1)S(1)} %get-tuple-element.44), channel_id=1, source_target_pairs={{0,16},{8,24},{1,17},{9,25},{2,18},{10,26},{3,19},{11,27},{4,20},{... | collective-permute-start | bytes 1572872 | tf_op jit(solution)/shard_map/ppermute | solution.py:397
  78.1 1.9 %heads.3 = (bf16[128,2048]{1,0:T(8,128)(2,1)S(1)}, f32[136,512]{1,0:T(8,128)S(1)}, bf16[136,512]{1,0:T(8,128)(2,1)S(1)}, bf16[136,512]{1,0:T(8,128)(2,1)S(1)}, bf16[136,512]{1,0:T(8,128)(2,1)S(1)}) custom-call(s32[3]{0:T(128)S(1)} %pad_add_fusion.meta, f32[128,2048]{1,0:T(8,128)S(1)} %get-tuple-element.38.keep, ...), custom_call_target="tpu_custom_call" | custom-call | flops 1073741824 | tf_op jit(solution)/shard_map/heads/pallas_call | solution.py:303
  80.0 1.3 %collective-permute-start.25 = (bf16[128,2048]{1,0:T(8,128)(2,1)S(1)}, bf16[128,2048]{1,0:T(8,128)(2,1)S(1)}, u32[]{:S(2)}, u32[]{:S(2)}) collective-permute-start(bf16[128,2048]{1,0:T(8,128)(2,1)S(1)} %get-tuple-element.45), channel_id=1, source_target_pairs={{0,16},{8,24},{1,17},{9,25},{2,18},{10,26},{3,19},{11,27},{4,20},{... | collective-permute-start | bytes 1572872 | tf_op jit(solution)/shard_map/ppermute | solution.py:397
  81.4 1.3 %collective-permute-start.20 = (bf16[136,512]{1,0:T(8,128)(2,1)S(1)}, bf16[136,512]{1,0:T(8,128)(2,1)S(1)}, u32[]{:S(2)}, u32[]{:S(2)}) collective-permute-start(bf16[136,512]{1,0:T(8,128)(2,1)S(1)} %get-tuple-element.41), channel_id=1, source_target_pairs={{0,1},{1,2},{2,3},{3,0},{4,5},{5,6},{6,7},{7,4},{8,9},{9,10},{10,1... | collective-permute-start | bytes 417800 | tf_op jit(solution)/shard_map/ppermute | solution.py:396
  82.7 2.1 %collective-permute-start.21 = (bf16[136,512]{1,0:T(8,128)(2,1)S(1)}, bf16[136,512]{1,0:T(8,128)(2,1)S(1)}, u32[]{:S(2)}, u32[]{:S(2)}) collective-permute-start(bf16[136,512]{1,0:T(8,128)(2,1)S(1)} %get-tuple-element.42), channel_id=1, source_target_pairs={{0,2},{1,3},{2,0},{3,1},{4,6},{5,7},{6,4},{7,5},{8,10},{9,11},{10,... | collective-permute-start | bytes 417800 | tf_op jit(solution)/shard_map/ppermute | solution.py:396
  84.8 2.8 %collective-permute-start.22 = (bf16[136,512]{1,0:T(8,128)(2,1)S(1)}, bf16[136,512]{1,0:T(8,128)(2,1)S(1)}, u32[]{:S(2)}, u32[]{:S(2)}) collective-permute-start(bf16[136,512]{1,0:T(8,128)(2,1)S(1)} %get-tuple-element.43), channel_id=1, source_target_pairs={{0,3},{1,0},{2,1},{3,2},{4,7},{5,4},{6,5},{7,6},{8,11},{9,8},{10,9... | collective-permute-start | bytes 417800 | tf_op jit(solution)/shard_map/ppermute | solution.py:396
  87.6 0.2 finish.2
  87.8 2.1 %collective-permute-done.20.refs_0_ = bf16[136,512]{1,0:T(8,128)(2,1)S(1)} collective-permute-done((bf16[136,512]{1,0:T(8,128)(2,1)S(1)}, bf16[136,512]{1,0:T(8,128)(2,1)S(1)}, u32[]{:S(2)}, u32[]{:S(2)}) %collective-permute-start.20) | collective-permute-done | bytes 139296 | tf_op jit(solution)/shard_map/ppermute | solution.py:396
  89.8 1.3 %collective-permute-start.11 = (bf16[128,512]{1,0:T(8,128)(2,1)S(1)}, bf16[128,512]{1,0:T(8,128)(2,1)S(1)}, u32[]{:S(2)}, u32[]{:S(2)}) collective-permute-start(bf16[128,512]{1,0:T(8,128)(2,1)S(1)} %finish.2), channel_id=1, source_target_pairs={{0,16},{8,24},{1,17},{9,25},{2,18},{10,26},{3,19},{11,27},{4,20},{... | collective-permute-start | bytes 393224 | tf_op jit(solution)/shard_map/ppermute | solution.py:399
  91.1 2.6 %collective-permute-done.21.refs_1_ = bf16[136,512]{1,0:T(8,128)(2,1)S(1)} collective-permute-done((bf16[136,512]{1,0:T(8,128)(2,1)S(1)}, bf16[136,512]{1,0:T(8,128)(2,1)S(1)}, u32[]{:S(2)}, u32[]{:S(2)}) %collective-permute-start.21) | collective-permute-done | bytes 139296 | tf_op jit(solution)/shard_map/ppermute | solution.py:396
  93.7 0.2 finish.3
  93.9 1.3 %collective-permute-start.23 = (bf16[128,512]{1,0:T(8,128)(2,1)S(1)}, bf16[128,512]{1,0:T(8,128)(2,1)S(1)}, u32[]{:S(2)}, u32[]{:S(2)}) collective-permute-start(bf16[128,512]{1,0:T(8,128)(2,1)S(1)} %finish.3), channel_id=1, source_target_pairs={{0,16},{8,24},{1,17},{9,25},{2,18},{10,26},{3,19},{11,27},{4,20},{... | collective-permute-start | bytes 393224 | tf_op jit(solution)/shard_map/ppermute | solution.py:399
  95.2 5.6 %collective-permute-done.11 = bf16[128,512]{1,0:T(8,128)(2,1)S(1)} collective-permute-done((bf16[128,512]{1,0:T(8,128)(2,1)S(1)}, bf16[128,512]{1,0:T(8,128)(2,1)S(1)}, u32[]{:S(2)}, u32[]{:S(2)}) %collective-permute-start.11) | collective-permute-done | bytes 131104 | tf_op jit(solution)/shard_map/ppermute | solution.py:399
  100.8 1.4 %collective-permute-done.23 = bf16[128,512]{1,0:T(8,128)(2,1)S(1)} collective-permute-done((bf16[128,512]{1,0:T(8,128)(2,1)S(1)}, bf16[128,512]{1,0:T(8,128)(2,1)S(1)}, u32[]{:S(2)}, u32[]{:S(2)}) %collective-permute-start.23) | collective-permute-done | bytes 131104 | tf_op jit(solution)/shard_map/ppermute | solution.py:399
  102.2 0.9 maximum_select_fusion.1
  103.1 1.7 %maximum_select_fusion = bf16[1,512,2048]{2,1,0:T(8,128)(2,1)} fusion(bf16[1,128,2048]{2,1,0:T(8,128)(2,1)S(1)} %bitcast.12, bf16[1,128,2048]{2,1,0:T(8,128)(2,1)S(1)} %bitcast.16, bf16[1,128,2048]{2,1,0:T(8,128)(2,1)S(1)} %bitcast.11, bf16[1,128,2048]{2,1,0:T(8,128)(2,1)S(1)} %bitcast.15, pred[]{:T(512)S(6)} %ge.3), kind=kLoop, calls=%fused_computation | loop fusion | flops 9437184 | bytes 4194305 | tf_op jit(solution)/shard_map/jit(_where)/select_n | solution.py:402
  (36 shorter events, 0.4 us)
Async XLA Ops:
  0.7 1.1 %copy-start.3 = (bf16[1,128,3200]{2,1,0:T(8,128)(2,1)S(1)}, bf16[1,128,3200]{2,1,0:T(8,128)(2,1)}, u32[]{:S(2)}) copy-start(bf16[1,128,3200]{2,1,0:T(8,128)(2,1)} %refs_2_.1) | copy-start | bytes 2457604
  1.9 1.0 copy-start.4
  2.8 0.7 copy-start.6
  3.5 0.7 copy-start.7
  4.2 0.7 copy-start.8
  4.9 0.7 copy-start.9
  6.5 10.1 %collective-permute-start = (bf16[64,640]{1,0:T(8,128)(2,1)S(1)}, bf16[64,640]{1,0:T(8,128)(2,1)S(1)}, u32[]{:S(2)}, u32[]{:S(2)}) collective-permute-start(bf16[64,640]{1,0:T(8,128)(2,1)S(1)} %get-tuple-element.24), channel_id=1, source_target_pairs={{0,12},{4,28},{1,13},{5,29},{2,14},{6,30},{3,15},{7,31}} | collective-permute-start | bytes 245768 | tf_op jit(solution)/shard_map/ppermute | solution.py:379
  11.2 6.1 %collective-permute-start.1 = (bf16[64,640]{1,0:T(8,128)(2,1)S(1)}, bf16[64,640]{1,0:T(8,128)(2,1)S(1)}, u32[]{:S(2)}, u32[]{:S(2)}) collective-permute-start(bf16[64,640]{1,0:T(8,128)(2,1)S(1)} %get-tuple-element.25), channel_id=1, source_target_pairs={{0,8},{4,24},{1,9},{5,25},{2,10},{6,26},{3,11},{7,27}} | collective-permute-start | bytes 245768 | tf_op jit(solution)/shard_map/ppermute | solution.py:379
  12.5 5.6 %collective-permute-start.2 = (bf16[64,640]{1,0:T(8,128)(2,1)S(1)}, bf16[64,640]{1,0:T(8,128)(2,1)S(1)}, u32[]{:S(2)}, u32[]{:S(2)}) collective-permute-start(bf16[64,640]{1,0:T(8,128)(2,1)S(1)} %get-tuple-element.26), channel_id=1, source_target_pairs={{0,4},{4,20},{1,5},{5,21},{2,6},{6,22},{3,7},{7,23}} | collective-permute-start | bytes 245768 | tf_op jit(solution)/shard_map/ppermute | solution.py:379
  15.3 4.1 %collective-permute-start.3 = (bf16[64,640]{1,0:T(8,128)(2,1)S(1)}, bf16[64,640]{1,0:T(8,128)(2,1)S(1)}, u32[]{:S(2)}, u32[]{:S(2)}) collective-permute-start(bf16[64,640]{1,0:T(8,128)(2,1)S(1)} %get-tuple-element.27), channel_id=1, source_target_pairs={{0,0},{4,16},{1,1},{5,17},{2,2},{6,18},{3,3},{7,19}} | collective-permute-start | bytes 245768 | tf_op jit(solution)/shard_map/ppermute | solution.py:379
  16.0 7.1 %collective-permute-start.12 = (bf16[64,1600]{1,0:T(8,128)(2,1)S(1)}, bf16[64,1600]{1,0:T(8,128)(2,1)S(1)}, u32[]{:S(2)}, u32[]{:S(2)}) collective-permute-start(bf16[64,1600]{1,0:T(8,128)(2,1)S(1)} %get-tuple-element.34), channel_id=1, source_target_pairs={{8,12},{12,28},{9,13},{13,29},{10,14},{14,30},{11,15},{15,31}} | collective-permute-start | bytes 614408 | tf_op jit(solution)/shard_map/ppermute | solution.py:379
  16.7 6.4 %collective-permute-start.13 = (bf16[64,1600]{1,0:T(8,128)(2,1)S(1)}, bf16[64,1600]{1,0:T(8,128)(2,1)S(1)}, u32[]{:S(2)}, u32[]{:S(2)}) collective-permute-start(bf16[64,1600]{1,0:T(8,128)(2,1)S(1)} %get-tuple-element.35), channel_id=1, source_target_pairs={{8,8},{12,24},{9,9},{13,25},{10,10},{14,26},{11,11},{15,27}} | collective-permute-start | bytes 614408 | tf_op jit(solution)/shard_map/ppermute | solution.py:379
  17.4 5.7 %collective-permute-start.14 = (bf16[64,1600]{1,0:T(8,128)(2,1)S(1)}, bf16[64,1600]{1,0:T(8,128)(2,1)S(1)}, u32[]{:S(2)}, u32[]{:S(2)}) collective-permute-start(bf16[64,1600]{1,0:T(8,128)(2,1)S(1)} %get-tuple-element.36), channel_id=1, source_target_pairs={{8,4},{12,20},{9,5},{13,21},{10,6},{14,22},{11,7},{15,23}} | collective-permute-start | bytes 614408 | tf_op jit(solution)/shard_map/ppermute | solution.py:379
  18.1 5.0 %collective-permute-start.15 = (bf16[64,1600]{1,0:T(8,128)(2,1)S(1)}, bf16[64,1600]{1,0:T(8,128)(2,1)S(1)}, u32[]{:S(2)}, u32[]{:S(2)}) collective-permute-start(bf16[64,1600]{1,0:T(8,128)(2,1)S(1)} %get-tuple-element.37), channel_id=1, source_target_pairs={{8,0},{12,16},{9,1},{13,17},{10,2},{14,18},{11,3},{15,19}} | collective-permute-start | bytes 614408 | tf_op jit(solution)/shard_map/ppermute | solution.py:379
  19.4 9.5 %collective-permute-start.6 = (bf16[64,640]{1,0:T(8,128)(2,1)S(1)}, bf16[64,640]{1,0:T(8,128)(2,1)S(1)}, u32[]{:S(2)}, u32[]{:S(2)}) collective-permute-start(bf16[64,640]{1,0:T(8,128)(2,1)S(1)} %select_select_fusion.1.refs_0_), channel_id=1, source_target_pairs={{0,3},{1,0},{2,1},{3,2},{4,7},{5,4},{6,5},{7,6},{8,11},{9,8},{10,9... | collective-permute-start | bytes 245768 | tf_op jit(solution)/shard_map/ppermute | solution.py:383
  23.2 31.1 %collective-permute-start.18 = (bf16[64,1600]{1,0:T(8,128)(2,1)S(1)}, bf16[64,1600]{1,0:T(8,128)(2,1)S(1)}, u32[]{:S(2)}, u32[]{:S(2)}) collective-permute-start(bf16[64,1600]{1,0:T(8,128)(2,1)S(1)} %select_select_fusion.refs_0_), channel_id=1, source_target_pairs={{0,3},{1,0},{2,1},{3,2},{4,7},{5,4},{6,5},{7,6},{8,11},{9,8},{10,9... | collective-permute-start | bytes 614408 | tf_op jit(solution)/shard_map/ppermute | solution.py:383
  26.0 28.3 %collective-permute-start.17 = (bf16[64,1600]{1,0:T(8,128)(2,1)S(1)}, bf16[64,1600]{1,0:T(8,128)(2,1)S(1)}, u32[]{:S(2)}, u32[]{:S(2)}) collective-permute-start(bf16[64,1600]{1,0:T(8,128)(2,1)S(1)} %select_select_fusion.refs_0_), channel_id=1, source_target_pairs={{0,2},{1,3},{2,0},{3,1},{4,6},{5,7},{6,4},{7,5},{8,10},{9,11},{10,... | collective-permute-start | bytes 614408 | tf_op jit(solution)/shard_map/ppermute | solution.py:383
  26.0 28.3 %collective-permute-start.16 = (bf16[64,1600]{1,0:T(8,128)(2,1)S(1)}, bf16[64,1600]{1,0:T(8,128)(2,1)S(1)}, u32[]{:S(2)}, u32[]{:S(2)}) collective-permute-start(bf16[64,1600]{1,0:T(8,128)(2,1)S(1)} %select_select_fusion.refs_0_), channel_id=1, source_target_pairs={{0,1},{1,2},{2,3},{3,0},{4,5},{5,6},{6,7},{7,4},{8,9},{9,10},{10,1... | collective-permute-start | bytes 614408 | tf_op jit(solution)/shard_map/ppermute | solution.py:383
  27.0 23.0 %collective-permute-start.5 = (bf16[64,640]{1,0:T(8,128)(2,1)S(1)}, bf16[64,640]{1,0:T(8,128)(2,1)S(1)}, u32[]{:S(2)}, u32[]{:S(2)}) collective-permute-start(bf16[64,640]{1,0:T(8,128)(2,1)S(1)} %select_select_fusion.1.refs_0_), channel_id=1, source_target_pairs={{0,2},{1,3},{2,0},{3,1},{4,6},{5,7},{6,4},{7,5},{8,10},{9,11},{10,... | collective-permute-start | bytes 245768 | tf_op jit(solution)/shard_map/ppermute | solution.py:383
  28.9 21.1 %collective-permute-start.4 = (bf16[64,640]{1,0:T(8,128)(2,1)S(1)}, bf16[64,640]{1,0:T(8,128)(2,1)S(1)}, u32[]{:S(2)}, u32[]{:S(2)}) collective-permute-start(bf16[64,640]{1,0:T(8,128)(2,1)S(1)} %select_select_fusion.1.refs_0_), channel_id=1, source_target_pairs={{0,1},{1,2},{2,3},{3,0},{4,5},{5,6},{6,7},{7,4},{8,9},{9,10},{10,1... | collective-permute-start | bytes 245768 | tf_op jit(solution)/shard_map/ppermute | solution.py:383
  50.0 1.7 %copy-start.2 = (bf16[640,2048]{1,0:T(8,128)(2,1)S(1)}, bf16[640,2048]{1,0:T(8,128)(2,1)}, u32[]{:S(2)}) copy-start(bf16[640,2048]{1,0:T(8,128)(2,1)} %refs_4_.2) | copy-start | bytes 7864324
  51.8 16.4 %copy-start = (bf16[2048,2048]{1,0:T(8,128)(2,1)S(1)}, bf16[2048,2048]{1,0:T(8,128)(2,1)}, u32[]{:S(2)}) copy-start(bf16[2048,2048]{1,0:T(8,128)(2,1)} %weight.3) | copy-start | bytes 25165828
  53.3 14.9 %collective-permute-start.7 = (bf16[128,2048]{1,0:T(8,128)(2,1)S(1)}, bf16[128,2048]{1,0:T(8,128)(2,1)S(1)}, u32[]{:S(2)}, u32[]{:S(2)}) collective-permute-start(bf16[128,2048]{1,0:T(8,128)(2,1)S(1)} %get-tuple-element.29), channel_id=1, source_target_pairs={{0,4},{4,0},{1,5},{5,1},{2,6},{6,2},{3,7},{7,3},{8,12},{12,8},{9,1... | collective-permute-start | bytes 1572872 | tf_op jit(solution)/shard_map/ppermute | solution.py:388
  54.3 2.9 %copy-start.1 = (bf16[1600,2048]{1,0:T(8,128)(2,1)S(1)}, bf16[1600,2048]{1,0:T(8,128)(2,1)}, u32[]{:S(2)}) copy-start(bf16[1600,2048]{1,0:T(8,128)(2,1)} %refs_4_.3) | copy-start | bytes 19660804
  57.2 11.0 %copy-start.5 = (f32[2048]{0:T(1024)S(1)}, f32[2048]{0:T(1024)}, u32[]{:S(2)}) copy-start(f32[2048]{0:T(1024)} %gain.3) | copy-start | bytes 24580
  59.9 18.3 %collective-permute-start.19 = (bf16[128,2048]{1,0:T(8,128)(2,1)S(1)}, bf16[128,2048]{1,0:T(8,128)(2,1)S(1)}, u32[]{:S(2)}, u32[]{:S(2)}) collective-permute-start(bf16[128,2048]{1,0:T(8,128)(2,1)S(1)} %get-tuple-element.39), channel_id=1, source_target_pairs={{0,4},{4,0},{1,5},{5,1},{2,6},{6,2},{3,7},{7,3},{8,12},{12,8},{9,1... | collective-permute-start | bytes 1572872 | tf_op jit(solution)/shard_map/ppermute | solution.py:388
  70.1 11.3 %collective-permute-start.8 = (bf16[136,512]{1,0:T(8,128)(2,1)S(1)}, bf16[136,512]{1,0:T(8,128)(2,1)S(1)}, u32[]{:S(2)}, u32[]{:S(2)}) collective-permute-start(bf16[136,512]{1,0:T(8,128)(2,1)S(1)} %get-tuple-element.31), channel_id=1, source_target_pairs={{0,1},{1,2},{2,3},{3,0},{4,5},{5,6},{6,7},{7,4},{8,9},{9,10},{10,1... | collective-permute-start | bytes 417800 | tf_op jit(solution)/shard_map/ppermute | solution.py:396
  71.2 11.5 %collective-permute-start.9 = (bf16[136,512]{1,0:T(8,128)(2,1)S(1)}, bf16[136,512]{1,0:T(8,128)(2,1)S(1)}, u32[]{:S(2)}, u32[]{:S(2)}) collective-permute-start(bf16[136,512]{1,0:T(8,128)(2,1)S(1)} %get-tuple-element.32), channel_id=1, source_target_pairs={{0,2},{1,3},{2,0},{3,1},{4,6},{5,7},{6,4},{7,5},{8,10},{9,11},{10,... | collective-permute-start | bytes 417800 | tf_op jit(solution)/shard_map/ppermute | solution.py:396
  73.4 11.3 %collective-permute-start.10 = (bf16[136,512]{1,0:T(8,128)(2,1)S(1)}, bf16[136,512]{1,0:T(8,128)(2,1)S(1)}, u32[]{:S(2)}, u32[]{:S(2)}) collective-permute-start(bf16[136,512]{1,0:T(8,128)(2,1)S(1)} %get-tuple-element.33), channel_id=1, source_target_pairs={{0,3},{1,0},{2,1},{3,2},{4,7},{5,4},{6,5},{7,6},{8,11},{9,8},{10,9... | collective-permute-start | bytes 417800 | tf_op jit(solution)/shard_map/ppermute | solution.py:396
  76.1 27.0 %collective-permute-start.24 = (bf16[128,2048]{1,0:T(8,128)(2,1)S(1)}, bf16[128,2048]{1,0:T(8,128)(2,1)S(1)}, u32[]{:S(2)}, u32[]{:S(2)}) collective-permute-start(bf16[128,2048]{1,0:T(8,128)(2,1)S(1)} %get-tuple-element.44), channel_id=1, source_target_pairs={{0,16},{8,24},{1,17},{9,25},{2,18},{10,26},{3,19},{11,27},{4,20},{... | collective-permute-start | bytes 1572872 | tf_op jit(solution)/shard_map/ppermute | solution.py:397
  80.0 23.1 %collective-permute-start.25 = (bf16[128,2048]{1,0:T(8,128)(2,1)S(1)}, bf16[128,2048]{1,0:T(8,128)(2,1)S(1)}, u32[]{:S(2)}, u32[]{:S(2)}) collective-permute-start(bf16[128,2048]{1,0:T(8,128)(2,1)S(1)} %get-tuple-element.45), channel_id=1, source_target_pairs={{0,16},{8,24},{1,17},{9,25},{2,18},{10,26},{3,19},{11,27},{4,20},{... | collective-permute-start | bytes 1572872 | tf_op jit(solution)/shard_map/ppermute | solution.py:397
  81.4 8.5 %collective-permute-start.20 = (bf16[136,512]{1,0:T(8,128)(2,1)S(1)}, bf16[136,512]{1,0:T(8,128)(2,1)S(1)}, u32[]{:S(2)}, u32[]{:S(2)}) collective-permute-start(bf16[136,512]{1,0:T(8,128)(2,1)S(1)} %get-tuple-element.41), channel_id=1, source_target_pairs={{0,1},{1,2},{2,3},{3,0},{4,5},{5,6},{6,7},{7,4},{8,9},{9,10},{10,1... | collective-permute-start | bytes 417800 | tf_op jit(solution)/shard_map/ppermute | solution.py:396
  82.7 11.0 %collective-permute-start.21 = (bf16[136,512]{1,0:T(8,128)(2,1)S(1)}, bf16[136,512]{1,0:T(8,128)(2,1)S(1)}, u32[]{:S(2)}, u32[]{:S(2)}) collective-permute-start(bf16[136,512]{1,0:T(8,128)(2,1)S(1)} %get-tuple-element.42), channel_id=1, source_target_pairs={{0,2},{1,3},{2,0},{3,1},{4,6},{5,7},{6,4},{7,5},{8,10},{9,11},{10,... | collective-permute-start | bytes 417800 | tf_op jit(solution)/shard_map/ppermute | solution.py:396
  84.8 9.0 %collective-permute-start.22 = (bf16[136,512]{1,0:T(8,128)(2,1)S(1)}, bf16[136,512]{1,0:T(8,128)(2,1)S(1)}, u32[]{:S(2)}, u32[]{:S(2)}) collective-permute-start(bf16[136,512]{1,0:T(8,128)(2,1)S(1)} %get-tuple-element.43), channel_id=1, source_target_pairs={{0,3},{1,0},{2,1},{3,2},{4,7},{5,4},{6,5},{7,6},{8,11},{9,8},{10,9... | collective-permute-start | bytes 417800 | tf_op jit(solution)/shard_map/ppermute | solution.py:396
  89.8 11.0 %collective-permute-start.11 = (bf16[128,512]{1,0:T(8,128)(2,1)S(1)}, bf16[128,512]{1,0:T(8,128)(2,1)S(1)}, u32[]{:S(2)}, u32[]{:S(2)}) collective-permute-start(bf16[128,512]{1,0:T(8,128)(2,1)S(1)} %finish.2), channel_id=1, source_target_pairs={{0,16},{8,24},{1,17},{9,25},{2,18},{10,26},{3,19},{11,27},{4,20},{... | collective-permute-start | bytes 393224 | tf_op jit(solution)/shard_map/ppermute | solution.py:399
  93.9 8.3 %collective-permute-start.23 = (bf16[128,512]{1,0:T(8,128)(2,1)S(1)}, bf16[128,512]{1,0:T(8,128)(2,1)S(1)}, u32[]{:S(2)}, u32[]{:S(2)}) collective-permute-start(bf16[128,512]{1,0:T(8,128)(2,1)S(1)} %finish.3), channel_id=1, source_target_pairs={{0,16},{8,24},{1,17},{9,25},{2,18},{10,26},{3,19},{11,27},{4,20},{... | collective-permute-start | bytes 393224 | tf_op jit(solution)/shard_map/ppermute | solution.py:399

commit v2 on v1

--- a/solution.py
+++ b/solution.py
@@ -181,6 +181,14 @@
     return pl.BlockSpec(memory_space=pltpu.VMEM)
 
 
+def hbm():
+    return pl.BlockSpec(memory_space=pltpu.HBM)
+
+
+def in_hbm(arrays):
+    return [pltpu.with_memory_space_constraint(x, pltpu.HBM) for x in arrays]
+
+
 def limits_of(mib, flops=0):
     return dict(
         compiler_params=pltpu.CompilerParams(vmem_limit_bytes=mib * MIB),
@@ -191,21 +199,37 @@
 def encode_kernel(dp_count, meta, dest, limits, *refs):
     group, dp, mp = meta[0], meta[1], meta[2]
     targets = 2 * dp_count
-    inputs, messages = refs[:4], refs[4:]
+    inputs, messages, scratch = refs[:4], refs[4 : 4 + 2 * targets], refs[4 + 2 * targets :]
+    routes, lives, *places, sems = scratch
     for stream in range(2):
-        states, gain = inputs[2 * stream : 2 * stream + 2]
+        states, gain = places[2 * stream : 2 * stream + 2]
         outs = messages[stream * targets : (stream + 1) * targets]
         share = states.shape[1] // BLOCKS
         half = outs[0].shape[1]
 
         @pl.when(group == stream)
         def _():
+            copies = [
+                pltpu.make_async_copy(source, place, sems.at[i])
+                for i, (source, place) in enumerate(
+                    (
+                        (dest, routes),
+                        (limits, lives),
+                        (inputs[2 * stream], states),
+                        (inputs[2 * stream + 1], gain),
+                    )
+                )
+            ]
+            for copy in copies:
+                copy.start()
+            for copy in copies:
+                copy.wait()
             scale = gain[...].reshape(1, -1)
             for target in range(targets):
                 block = jnp.int32(0)
                 for b in range(BLOCKS):
-                    block = jnp.where(dest[stream, dp, b] == target, b, block)
-                limit = limits[stream, dp, block]
+                    block = jnp.where(routes[stream, dp, b] == target, b, block)
+                limit = lives[stream, dp, block]
                 start = pl.multiple_of(block * share, share)
                 values = states[0, pl.ds(start, share), :].astype(jnp.float32)
                 center = values - jnp.mean(values, axis=-1, keepdims=True)
@@ -223,19 +247,51 @@
 
 def encode(dp_count, meta, dest, limits, streams):
     arguments, shapes = [], []
+    scratch = [pltpu.SMEM(dest.shape, jnp.int32), pltpu.SMEM(limits.shape, jnp.int32)]
     for states, gain, _ in streams:
         _, rows, width = states.shape
         arguments += [states, gain]
+        scratch += [pltpu.VMEM(states.shape, states.dtype), pltpu.VMEM(gain.shape, gain.dtype)]
         shape = jax.ShapeDtypeStruct((2 * rows // BLOCKS, width // dp_count), jnp.bfloat16)
         shapes += [shape] * (2 * dp_count)
     return pl.pallas_call(
         functools.partial(encode_kernel, dp_count),
         out_shape=shapes,
-        in_specs=[smem()] * 3 + [vmem()] * len(arguments),
+        in_specs=[smem()] + [hbm()] * (2 + len(arguments)),
         out_specs=[vmem()] * len(shapes),
+        scratch_shapes=scratch + [pltpu.SemaphoreType.DMA((4,))],
         name="encode",
         **limits_of(8, 1 << 28),
-    )(meta, dest, limits, *arguments)
+    )(meta, *in_hbm([dest, limits, *arguments]))
+
+
+def fetch_kernel(cuts, *refs):
+    count = len(cuts)
+    sources, places, sems = refs[:count], refs[count : 2 * count], refs[2 * count]
+    copies = []
+    for source, place, pieces in zip(sources, places, cuts):
+        depth = source.shape[0] // pieces
+        for i in range(pieces):
+            part = pl.ds(i * depth, depth)
+            copies.append(
+                pltpu.make_async_copy(source.at[part], place.at[part], sems.at[len(copies)])
+            )
+    for copy in copies:
+        copy.start()
+    for copy in copies:
+        copy.wait()
+
+
+def fetch(weights, cuts):
+    return pl.pallas_call(
+        functools.partial(fetch_kernel, cuts),
+        out_shape=[pltpu.VMEM(x.shape, x.dtype) for x in weights],
+        in_specs=[hbm()] * len(weights),
+        out_specs=[vmem()] * len(weights),
+        scratch_shapes=[pltpu.SemaphoreType.DMA((sum(cuts),))],
+        name="fetch",
+        **limits_of(12, 1 << 28),
+    )(*in_hbm(weights))
 
 
 def project_kernel(mp_count, tile, meta, *refs):
@@ -382,8 +438,9 @@
         for shift in range(1, mp_count):
             pieces.append(lax.ppermute(piece, "mp", rings[shift]))
         gathered.append(pieces)
+    weights = fetch([audio_proj, image_proj], (2, 5))
     partial, others = [], []
-    for stream, (_, _, proj) in enumerate(streams):
+    for stream, proj in enumerate(weights):
         partial.append(project_rows(mp_count, meta, gathered[stream], proj, 512))
         others.append(lax.ppermute(partial[stream][1], "dp", swap))
     row_parts, head_parts = [], []
@@ -398,8 +455,8 @@
         values = finish(full_width, own, sums)
         head_parts += [lax.ppermute(values, "group", up), values]
     rows_out = jnp.concatenate(row_parts, axis=0)
+    rows_out = jnp.where(on_backbone, rows_out, jnp.zeros_like(rows_out))
     heads_out = jnp.concatenate(head_parts, axis=0)
-    rows_out = jnp.where(on_backbone, rows_out, jnp.zeros_like(rows_out))
     heads_out = jnp.where(on_backbone, heads_out, jnp.zeros_like(heads_out))
     return (heads_out[None], rows_out[None])
 

time: 105 us -> 100 us (0.952)
  local copies, waits for them, and re-layouts: 9.5 us -> 0.01 us
  Pallas kernels: 9.3 us -> 14.1 us
    unnamed x20 -> x6, local copies, waits for them, and re-layouts: 9.5 us -> 0.01 us
    ppermute x6, waiting for transfers between devices: 19.7 us -> 15.8 us  [shards_direct(): pieces.append(lax.ppermute(piece, 'mp', rings[shift]))]
    pallas_call x0 -> x1, Pallas kernels: none -> 3.84 us  [fetch(): pl.pallas_call(functools.partial(fetch_kernel, cuts), out_shape=[pltpu.VM...]
    ppermute x2, waiting for transfers between devices: 7.27 us -> 10 us  [shards_direct(): others.append(lax.ppermute(partial[stream][1], 'dp', swap))]
  transfers between devices with their start and end apart: 26 -> 26, of which waited for: 8 -> 7; matrix products, arithmetic and copies ran while one was open for 1% -> 1% of each run, Pallas kernels for 8% -> 12%
where the time goes in v2:
time: 100 us
  starting transfers between devices  44 us (44%)
  waiting for transfers between devices  38.2 us (38%)
  Pallas kernels  14.1 us (14%)
  other arithmetic  2.77 us (3%)
    ppermute x6, waiting for transfers between devices, shards_direct(): pieces.append(lax.ppermute(piece, 'mp', rings[shift]))  15.8 us
    ppermute x6, starting transfers between devices, shards_direct(): sums.append(lax.ppermute(part, 'mp', rings[shift]))  13 us
    ppermute x8, starting transfers between devices, shards_direct(): lax.ppermute(messages[stream * targets + index], ('group', 'dp'), pairs)  11.7 us
    ppermute x6, starting transfers between devices, shards_direct(): pieces.append(lax.ppermute(piece, 'mp', rings[shift]))  10.9 us
    ppermute x2, waiting for transfers between devices, shards_direct(): others.append(lax.ppermute(partial[stream][1], 'dp', swap))  10 us
    ppermute x2, waiting for transfers between devices, shards_direct(): head_parts += [lax.ppermute(values, 'group', up), values]  7.79 us
    ppermute x6, waiting for transfers between devices, shards_direct(): sums.append(lax.ppermute(part, 'mp', rings[shift]))  4.47 us
    pallas_call x2, Pallas kernels, project_rows(): pl.pallas_call(functools.partial(project_kernel, mp_count, tile), out_sha...  4.23 us
  transfers between devices with their start and end apart: 26, of which 7 were waited for; matrix products, arithmetic and copies ran while one was open for 1% of the time, Pallas kernels for 12%

profile of v2, /device:TPU:0, one launch (start us, length us, event | category | flops | bytes accessed | tf_op | source)
XLA Modules:
  0.0 100.0 jit_solution(5577285988216545857)
XLA Ops:
  0.6 0.1 pad_add_fusion.meta
  0.7 1.8 %encode.1 = (bf16[64,640]{1,0:T(8,128)(2,1)S(1)}, bf16[64,640]{1,0:T(8,128)(2,1)S(1)}, bf16[64,640]{1,0:T(8,128)(2,1)S(1)}, bf16[64,640]{1,0:T(8,128)(2,1)S(1)},...) custom-call(s32[3]{0:T(128)S(1)} %pad_add_fusion.meta, ...), custom_call_target="tpu_custom_call" | custom-call | flops 268435456 | tf_op jit(solution)/shard_map/encode/pallas_call | solution.py:257
  2.6 4.8 %collective-permute-start = (bf16[64,640]{1,0:T(8,128)(2,1)S(1)}, bf16[64,640]{1,0:T(8,128)(2,1)S(1)}, u32[]{:S(2)}, u32[]{:S(2)}) collective-permute-start(bf16[64,640]{1,0:T(8,128)(2,1)S(1)} %get-tuple-element.26), channel_id=1, source_target_pairs={{0,12},{4,28},{1,13},{5,29},{2,14},{6,30},{3,15},{7,31}} | collective-permute-start | bytes 245768 | tf_op jit(solution)/shard_map/ppermute | solution.py:435
  7.4 1.3 %collective-permute-start.1 = (bf16[64,640]{1,0:T(8,128)(2,1)S(1)}, bf16[64,640]{1,0:T(8,128)(2,1)S(1)}, u32[]{:S(2)}, u32[]{:S(2)}) collective-permute-start(bf16[64,640]{1,0:T(8,128)(2,1)S(1)} %get-tuple-element.27), channel_id=1, source_target_pairs={{0,8},{4,24},{1,9},{5,25},{2,10},{6,26},{3,11},{7,27}} | collective-permute-start | bytes 245768 | tf_op jit(solution)/shard_map/ppermute | solution.py:435
  8.7 1.7 %collective-permute-start.2 = (bf16[64,640]{1,0:T(8,128)(2,1)S(1)}, bf16[64,640]{1,0:T(8,128)(2,1)S(1)}, u32[]{:S(2)}, u32[]{:S(2)}) collective-permute-start(bf16[64,640]{1,0:T(8,128)(2,1)S(1)} %get-tuple-element.28), channel_id=1, source_target_pairs={{0,4},{4,20},{1,5},{5,21},{2,6},{6,22},{3,7},{7,23}} | collective-permute-start | bytes 245768 | tf_op jit(solution)/shard_map/ppermute | solution.py:435
  10.4 0.7 collective-permute-start.3
  11.0 0.7 collective-permute-start.12
  11.7 0.0 collective-permute-done
  11.8 0.7 collective-permute-start.13
  12.4 0.7 collective-permute-start.14
  13.1 0.1 collective-permute-done.2
  13.2 1.3 %collective-permute-start.15 = (bf16[64,1600]{1,0:T(8,128)(2,1)S(1)}, bf16[64,1600]{1,0:T(8,128)(2,1)S(1)}, u32[]{:S(2)}, u32[]{:S(2)}) collective-permute-start(bf16[64,1600]{1,0:T(8,128)(2,1)S(1)} %get-tuple-element.40), channel_id=1, source_target_pairs={{8,0},{12,16},{9,1},{13,17},{10,2},{14,18},{11,3},{15,19}} | collective-permute-start | bytes 614408 | tf_op jit(solution)/shard_map/ppermute | solution.py:435
  14.5 0.0 collective-permute-done.3
  14.5 3.7 %collective-permute-start.6 = (bf16[64,640]{1,0:T(8,128)(2,1)S(1)}, bf16[64,640]{1,0:T(8,128)(2,1)S(1)}, u32[]{:S(2)}, u32[]{:S(2)}) collective-permute-start(bf16[64,640]{1,0:T(8,128)(2,1)S(1)} %select_select_fusion.1.refs_0_), channel_id=1, source_target_pairs={{0,3},{1,0},{2,1},{3,2},{4,7},{5,4},{6,5},{7,6},{8,11},{9,8},{10,9... | collective-permute-start | bytes 245768 | tf_op jit(solution)/shard_map/ppermute | solution.py:439
  18.2 0.0 collective-permute-done.12
  18.2 0.0 collective-permute-done.15
  18.2 2.8 %collective-permute-start.18 = (bf16[64,1600]{1,0:T(8,128)(2,1)S(1)}, bf16[64,1600]{1,0:T(8,128)(2,1)S(1)}, u32[]{:S(2)}, u32[]{:S(2)}) collective-permute-start(bf16[64,1600]{1,0:T(8,128)(2,1)S(1)} %select_select_fusion.refs_0_), channel_id=1, source_target_pairs={{0,3},{1,0},{2,1},{3,2},{4,7},{5,4},{6,5},{7,6},{8,11},{9,8},{10,9... | collective-permute-start | bytes 614408 | tf_op jit(solution)/shard_map/ppermute | solution.py:439
  21.1 1.0 %collective-permute-start.16 = (bf16[64,1600]{1,0:T(8,128)(2,1)S(1)}, bf16[64,1600]{1,0:T(8,128)(2,1)S(1)}, u32[]{:S(2)}, u32[]{:S(2)}) collective-permute-start(bf16[64,1600]{1,0:T(8,128)(2,1)S(1)} %select_select_fusion.refs_0_), channel_id=1, source_target_pairs={{0,1},{1,2},{2,3},{3,0},{4,5},{5,6},{6,7},{7,4},{8,9},{9,10},{10,1... | collective-permute-start | bytes 614408 | tf_op jit(solution)/shard_map/ppermute | solution.py:439
  22.1 1.9 %collective-permute-start.5 = (bf16[64,640]{1,0:T(8,128)(2,1)S(1)}, bf16[64,640]{1,0:T(8,128)(2,1)S(1)}, u32[]{:S(2)}, u32[]{:S(2)}) collective-permute-start(bf16[64,640]{1,0:T(8,128)(2,1)S(1)} %select_select_fusion.1.refs_0_), channel_id=1, source_target_pairs={{0,2},{1,3},{2,0},{3,1},{4,6},{5,7},{6,4},{7,5},{8,10},{9,11},{10,... | collective-permute-start | bytes 245768 | tf_op jit(solution)/shard_map/ppermute | solution.py:439
  24.0 1.5 %collective-permute-start.4 = (bf16[64,640]{1,0:T(8,128)(2,1)S(1)}, bf16[64,640]{1,0:T(8,128)(2,1)S(1)}, u32[]{:S(2)}, u32[]{:S(2)}) collective-permute-start(bf16[64,640]{1,0:T(8,128)(2,1)S(1)} %select_select_fusion.1.refs_0_), channel_id=1, source_target_pairs={{0,1},{1,2},{2,3},{3,0},{4,5},{5,6},{6,7},{7,4},{8,9},{9,10},{10,1... | collective-permute-start | bytes 245768 | tf_op jit(solution)/shard_map/ppermute | solution.py:439
  25.5 3.8 %fetch.1 = (bf16[640,2048]{1,0:T(8,128)(2,1)S(1)}, bf16[1600,2048]{1,0:T(8,128)(2,1)S(1)}) custom-call(bf16[640,2048]{1,0:T(8,128)(2,1)} %refs_0_.3, bf16[1600,2048]{1,0:T(8,128)(2,1)} %refs_1_.3), custom_call_target="tpu_custom_call" | custom-call | flops 268435456 | tf_op jit(solution)/shard_map/fetch/pallas_call | solution.py:286
  29.3 15.8 %collective-permute-done.5.refs_2_ = bf16[64,640]{1,0:T(8,128)(2,1)S(1)} collective-permute-done((bf16[64,640]{1,0:T(8,128)(2,1)S(1)}, bf16[64,640]{1,0:T(8,128)(2,1)S(1)}, u32[]{:S(2)}, u32[]{:S(2)}) %collective-permute-start.5) | collective-permute-done | bytes 81952 | tf_op jit(solution)/shard_map/ppermute | solution.py:439
  45.1 1.5 %project.2 = (f32[128,2048]{1,0:T(8,128)S(1)}, bf16[128,2048]{1,0:T(8,128)(2,1)S(1)}) custom-call(s32[3]{0:T(128)S(1)} %pad_add_fusion.meta, bf16[64,640]{1,0:T(8,128)(2,1)S(1)} %select_select_fusion.1.refs_0_, bf16[64,640]{1,0:T(8,128)(2,1)S(1)} %collective-permute-done.4.refs_1_, bf16[64,640]{1,0:T(8,128)(2,1)S(1)} %collective-permute-done.5.refs_2_, ...), custom_call_target="tpu_custom_call" | custom-call | flops 671088640 | tf_op jit(solution)/shard_map/project/pallas_call | solution.py:317
  46.7 0.0 copy-start
  46.7 1.1 %collective-permute-start.7 = (bf16[128,2048]{1,0:T(8,128)(2,1)S(1)}, bf16[128,2048]{1,0:T(8,128)(2,1)S(1)}, u32[]{:S(2)}, u32[]{:S(2)}) collective-permute-start(bf16[128,2048]{1,0:T(8,128)(2,1)S(1)} %get-tuple-element.32), channel_id=1, source_target_pairs={{0,4},{4,0},{1,5},{5,1},{2,6},{6,2},{3,7},{7,3},{8,12},{12,8},{9,1... | collective-permute-start | bytes 1572872 | tf_op jit(solution)/shard_map/ppermute | solution.py:445
  47.8 2.7 %project.3 = (f32[128,2048]{1,0:T(8,128)S(1)}, bf16[128,2048]{1,0:T(8,128)(2,1)S(1)}) custom-call(s32[3]{0:T(128)S(1)} %pad_add_fusion.meta, bf16[64,1600]{1,0:T(8,128)(2,1)S(1)} %select_select_fusion.refs_0_, bf16[64,1600]{1,0:T(8,128)(2,1)S(1)} %collective-permute-done.16.refs_1_, bf16[64,1600]{1,0:T(8,128)(2,1)S(1)} %collective-permute-done.17.refs_2_, ...), custom_call_target="tpu_custom_call" | custom-call | flops 1677721600 | tf_op jit(solution)/shard_map/project/pallas_call | solution.py:317
  50.5 1.0 %collective-permute-start.19 = (bf16[128,2048]{1,0:T(8,128)(2,1)S(1)}, bf16[128,2048]{1,0:T(8,128)(2,1)S(1)}, u32[]{:S(2)}, u32[]{:S(2)}) collective-permute-start(bf16[128,2048]{1,0:T(8,128)(2,1)S(1)} %get-tuple-element.43), channel_id=1, source_target_pairs={{0,4},{4,0},{1,5},{5,1},{2,6},{6,2},{3,7},{7,3},{8,12},{12,8},{9,1... | collective-permute-start | bytes 1572872 | tf_op jit(solution)/shard_map/ppermute | solution.py:445
  51.5 10.0 %collective-permute-done.7.other = bf16[128,2048]{1,0:T(8,128)(2,1)S(1)} collective-permute-done((bf16[128,2048]{1,0:T(8,128)(2,1)S(1)}, bf16[128,2048]{1,0:T(8,128)(2,1)S(1)}, u32[]{:S(2)}, u32[]{:S(2)}) %collective-permute-start.7) | collective-permute-done | bytes 524320 | tf_op jit(solution)/shard_map/ppermute | solution.py:445
  61.6 1.9 %heads.2 = (bf16[128,2048]{1,0:T(8,128)(2,1)S(1)}, f32[136,512]{1,0:T(8,128)S(1)}, bf16[136,512]{1,0:T(8,128)(2,1)S(1)}, bf16[136,512]{1,0:T(8,128)(2,1)S(1)}, bf16[136,512]{1,0:T(8,128)(2,1)S(1)}) custom-call(s32[3]{0:T(128)S(1)} %pad_add_fusion.meta, f32[128,2048]{1,0:T(8,128)S(1)} %get-tuple-element.31.keep, ...), custom_call_target="tpu_custom_call" | custom-call | flops 1073741824 | tf_op jit(solution)/shard_map/heads/pallas_call | solution.py:359
  63.5 1.1 %collective-permute-start.8 = (bf16[136,512]{1,0:T(8,128)(2,1)S(1)}, bf16[136,512]{1,0:T(8,128)(2,1)S(1)}, u32[]{:S(2)}, u32[]{:S(2)}) collective-permute-start(bf16[136,512]{1,0:T(8,128)(2,1)S(1)} %get-tuple-element.34), channel_id=1, source_target_pairs={{0,1},{1,2},{2,3},{3,0},{4,5},{5,6},{6,7},{7,4},{8,9},{9,10},{10,1... | collective-permute-start | bytes 417800 | tf_op jit(solution)/shard_map/ppermute | solution.py:453
  64.6 2.2 %collective-permute-start.9 = (bf16[136,512]{1,0:T(8,128)(2,1)S(1)}, bf16[136,512]{1,0:T(8,128)(2,1)S(1)}, u32[]{:S(2)}, u32[]{:S(2)}) collective-permute-start(bf16[136,512]{1,0:T(8,128)(2,1)S(1)} %get-tuple-element.35), channel_id=1, source_target_pairs={{0,2},{1,3},{2,0},{3,1},{4,6},{5,7},{6,4},{7,5},{8,10},{9,11},{10,... | collective-permute-start | bytes 417800 | tf_op jit(solution)/shard_map/ppermute | solution.py:453
  66.8 2.7 %collective-permute-start.10 = (bf16[136,512]{1,0:T(8,128)(2,1)S(1)}, bf16[136,512]{1,0:T(8,128)(2,1)S(1)}, u32[]{:S(2)}, u32[]{:S(2)}) collective-permute-start(bf16[136,512]{1,0:T(8,128)(2,1)S(1)} %get-tuple-element.36), channel_id=1, source_target_pairs={{0,3},{1,0},{2,1},{3,2},{4,7},{5,4},{6,5},{7,6},{8,11},{9,8},{10,9... | collective-permute-start | bytes 417800 | tf_op jit(solution)/shard_map/ppermute | solution.py:453
  69.5 2.3 %collective-permute-start.24 = (bf16[128,2048]{1,0:T(8,128)(2,1)S(1)}, bf16[128,2048]{1,0:T(8,128)(2,1)S(1)}, u32[]{:S(2)}, u32[]{:S(2)}) collective-permute-start(bf16[128,2048]{1,0:T(8,128)(2,1)S(1)} %get-tuple-element.48), channel_id=1, source_target_pairs={{0,16},{8,24},{1,17},{9,25},{2,18},{10,26},{3,19},{11,27},{4,20},{... | collective-permute-start | bytes 1572872 | tf_op jit(solution)/shard_map/ppermute | solution.py:454
  71.8 1.9 %heads.3 = (bf16[128,2048]{1,0:T(8,128)(2,1)S(1)}, f32[136,512]{1,0:T(8,128)S(1)}, bf16[136,512]{1,0:T(8,128)(2,1)S(1)}, bf16[136,512]{1,0:T(8,128)(2,1)S(1)}, bf16[136,512]{1,0:T(8,128)(2,1)S(1)}) custom-call(s32[3]{0:T(128)S(1)} %pad_add_fusion.meta, f32[128,2048]{1,0:T(8,128)S(1)} %get-tuple-element.42.keep, ...), custom_call_target="tpu_custom_call" | custom-call | flops 1073741824 | tf_op jit(solution)/shard_map/heads/pallas_call | solution.py:359
  73.7 1.3 %collective-permute-start.25 = (bf16[128,2048]{1,0:T(8,128)(2,1)S(1)}, bf16[128,2048]{1,0:T(8,128)(2,1)S(1)}, u32[]{:S(2)}, u32[]{:S(2)}) collective-permute-start(bf16[128,2048]{1,0:T(8,128)(2,1)S(1)} %get-tuple-element.49), channel_id=1, source_target_pairs={{0,16},{8,24},{1,17},{9,25},{2,18},{10,26},{3,19},{11,27},{4,20},{... | collective-permute-start | bytes 1572872 | tf_op jit(solution)/shard_map/ppermute | solution.py:454
  75.0 2.2 %collective-permute-start.20 = (bf16[136,512]{1,0:T(8,128)(2,1)S(1)}, bf16[136,512]{1,0:T(8,128)(2,1)S(1)}, u32[]{:S(2)}, u32[]{:S(2)}) collective-permute-start(bf16[136,512]{1,0:T(8,128)(2,1)S(1)} %get-tuple-element.45), channel_id=1, source_target_pairs={{0,1},{1,2},{2,3},{3,0},{4,5},{5,6},{6,7},{7,4},{8,9},{9,10},{10,1... | collective-permute-start | bytes 417800 | tf_op jit(solution)/shard_map/ppermute | solution.py:453
  77.2 2.0 %collective-permute-start.21 = (bf16[136,512]{1,0:T(8,128)(2,1)S(1)}, bf16[136,512]{1,0:T(8,128)(2,1)S(1)}, u32[]{:S(2)}, u32[]{:S(2)}) collective-permute-start(bf16[136,512]{1,0:T(8,128)(2,1)S(1)} %get-tuple-element.46), channel_id=1, source_target_pairs={{0,2},{1,3},{2,0},{3,1},{4,6},{5,7},{6,4},{7,5},{8,10},{9,11},{10,... | collective-permute-start | bytes 417800 | tf_op jit(solution)/shard_map/ppermute | solution.py:453
  79.2 2.8 %collective-permute-start.22 = (bf16[136,512]{1,0:T(8,128)(2,1)S(1)}, bf16[136,512]{1,0:T(8,128)(2,1)S(1)}, u32[]{:S(2)}, u32[]{:S(2)}) collective-permute-start(bf16[136,512]{1,0:T(8,128)(2,1)S(1)} %get-tuple-element.47), channel_id=1, source_target_pairs={{0,3},{1,0},{2,1},{3,2},{4,7},{5,4},{6,5},{7,6},{8,11},{9,8},{10,9... | collective-permute-start | bytes 417800 | tf_op jit(solution)/shard_map/ppermute | solution.py:453
  82.1 0.2 finish.2
  82.3 0.5 collective-permute-done.20.refs_0_
  82.8 1.3 %collective-permute-start.11 = (bf16[128,512]{1,0:T(8,128)(2,1)S(1)}, bf16[128,512]{1,0:T(8,128)(2,1)S(1)}, u32[]{:S(2)}, u32[]{:S(2)}) collective-permute-start(bf16[128,512]{1,0:T(8,128)(2,1)S(1)} %finish.2), channel_id=1, source_target_pairs={{0,16},{8,24},{1,17},{9,25},{2,18},{10,26},{3,19},{11,27},{4,20},{... | collective-permute-start | bytes 393224 | tf_op jit(solution)/shard_map/ppermute | solution.py:456
  84.1 4.0 %collective-permute-done.21.refs_1_ = bf16[136,512]{1,0:T(8,128)(2,1)S(1)} collective-permute-done((bf16[136,512]{1,0:T(8,128)(2,1)S(1)}, bf16[136,512]{1,0:T(8,128)(2,1)S(1)}, u32[]{:S(2)}, u32[]{:S(2)}) %collective-permute-start.21) | collective-permute-done | bytes 139296 | tf_op jit(solution)/shard_map/ppermute | solution.py:453
  88.0 0.2 finish.3
  88.2 1.3 %collective-permute-start.23 = (bf16[128,512]{1,0:T(8,128)(2,1)S(1)}, bf16[128,512]{1,0:T(8,128)(2,1)S(1)}, u32[]{:S(2)}, u32[]{:S(2)}) collective-permute-start(bf16[128,512]{1,0:T(8,128)(2,1)S(1)} %finish.3), channel_id=1, source_target_pairs={{0,16},{8,24},{1,17},{9,25},{2,18},{10,26},{3,19},{11,27},{4,20},{... | collective-permute-start | bytes 393224 | tf_op jit(solution)/shard_map/ppermute | solution.py:456
  89.5 6.4 %collective-permute-done.11 = bf16[128,512]{1,0:T(8,128)(2,1)S(1)} collective-permute-done((bf16[128,512]{1,0:T(8,128)(2,1)S(1)}, bf16[128,512]{1,0:T(8,128)(2,1)S(1)}, u32[]{:S(2)}, u32[]{:S(2)}) %collective-permute-start.11) | collective-permute-done | bytes 131104 | tf_op jit(solution)/shard_map/ppermute | solution.py:456
  95.9 1.4 %collective-permute-done.23 = bf16[128,512]{1,0:T(8,128)(2,1)S(1)} collective-permute-done((bf16[128,512]{1,0:T(8,128)(2,1)S(1)}, bf16[128,512]{1,0:T(8,128)(2,1)S(1)}, u32[]{:S(2)}, u32[]{:S(2)}) %collective-permute-start.23) | collective-permute-done | bytes 131104 | tf_op jit(solution)/shard_map/ppermute | solution.py:456
  97.3 0.9 maximum_select_fusion.1
  98.2 1.7 %maximum_select_fusion = bf16[1,512,2048]{2,1,0:T(8,128)(2,1)} fusion(bf16[1,128,2048]{2,1,0:T(8,128)(2,1)S(1)} %bitcast.14, bf16[1,128,2048]{2,1,0:T(8,128)(2,1)S(1)} %bitcast.18, bf16[1,128,2048]{2,1,0:T(8,128)(2,1)S(1)} %bitcast.13, bf16[1,128,2048]{2,1,0:T(8,128)(2,1)S(1)} %bitcast.17, pred[]{:T(512)S(6)} %ge.3), kind=kLoop, calls=%fused_computation | loop fusion | flops 9437184 | bytes 4194305 | tf_op jit(solution)/shard_map/jit(_where)/select_n | solution.py:458
  (24 shorter events, 0.1 us)
Async XLA Ops:
  2.6 9.2 %collective-permute-start = (bf16[64,640]{1,0:T(8,128)(2,1)S(1)}, bf16[64,640]{1,0:T(8,128)(2,1)S(1)}, u32[]{:S(2)}, u32[]{:S(2)}) collective-permute-start(bf16[64,640]{1,0:T(8,128)(2,1)S(1)} %get-tuple-element.26), channel_id=1, source_target_pairs={{0,12},{4,28},{1,13},{5,29},{2,14},{6,30},{3,15},{7,31}} | collective-permute-start | bytes 245768 | tf_op jit(solution)/shard_map/ppermute | solution.py:435
  7.4 5.0 %collective-permute-start.1 = (bf16[64,640]{1,0:T(8,128)(2,1)S(1)}, bf16[64,640]{1,0:T(8,128)(2,1)S(1)}, u32[]{:S(2)}, u32[]{:S(2)}) collective-permute-start(bf16[64,640]{1,0:T(8,128)(2,1)S(1)} %get-tuple-element.27), channel_id=1, source_target_pairs={{0,8},{4,24},{1,9},{5,25},{2,10},{6,26},{3,11},{7,27}} | collective-permute-start | bytes 245768 | tf_op jit(solution)/shard_map/ppermute | solution.py:435
  8.7 4.5 %collective-permute-start.2 = (bf16[64,640]{1,0:T(8,128)(2,1)S(1)}, bf16[64,640]{1,0:T(8,128)(2,1)S(1)}, u32[]{:S(2)}, u32[]{:S(2)}) collective-permute-start(bf16[64,640]{1,0:T(8,128)(2,1)S(1)} %get-tuple-element.28), channel_id=1, source_target_pairs={{0,4},{4,20},{1,5},{5,21},{2,6},{6,22},{3,7},{7,23}} | collective-permute-start | bytes 245768 | tf_op jit(solution)/shard_map/ppermute | solution.py:435
  10.4 4.1 %collective-permute-start.3 = (bf16[64,640]{1,0:T(8,128)(2,1)S(1)}, bf16[64,640]{1,0:T(8,128)(2,1)S(1)}, u32[]{:S(2)}, u32[]{:S(2)}) collective-permute-start(bf16[64,640]{1,0:T(8,128)(2,1)S(1)} %get-tuple-element.29), channel_id=1, source_target_pairs={{0,0},{4,16},{1,1},{5,17},{2,2},{6,18},{3,3},{7,19}} | collective-permute-start | bytes 245768 | tf_op jit(solution)/shard_map/ppermute | solution.py:435
  11.0 7.1 %collective-permute-start.12 = (bf16[64,1600]{1,0:T(8,128)(2,1)S(1)}, bf16[64,1600]{1,0:T(8,128)(2,1)S(1)}, u32[]{:S(2)}, u32[]{:S(2)}) collective-permute-start(bf16[64,1600]{1,0:T(8,128)(2,1)S(1)} %get-tuple-element.37), channel_id=1, source_target_pairs={{8,12},{12,28},{9,13},{13,29},{10,14},{14,30},{11,15},{15,31}} | collective-permute-start | bytes 614408 | tf_op jit(solution)/shard_map/ppermute | solution.py:435
  11.8 6.4 %collective-permute-start.13 = (bf16[64,1600]{1,0:T(8,128)(2,1)S(1)}, bf16[64,1600]{1,0:T(8,128)(2,1)S(1)}, u32[]{:S(2)}, u32[]{:S(2)}) collective-permute-start(bf16[64,1600]{1,0:T(8,128)(2,1)S(1)} %get-tuple-element.38), channel_id=1, source_target_pairs={{8,8},{12,24},{9,9},{13,25},{10,10},{14,26},{11,11},{15,27}} | collective-permute-start | bytes 614408 | tf_op jit(solution)/shard_map/ppermute | solution.py:435
  12.4 5.7 %collective-permute-start.14 = (bf16[64,1600]{1,0:T(8,128)(2,1)S(1)}, bf16[64,1600]{1,0:T(8,128)(2,1)S(1)}, u32[]{:S(2)}, u32[]{:S(2)}) collective-permute-start(bf16[64,1600]{1,0:T(8,128)(2,1)S(1)} %get-tuple-element.39), channel_id=1, source_target_pairs={{8,4},{12,20},{9,5},{13,21},{10,6},{14,22},{11,7},{15,23}} | collective-permute-start | bytes 614408 | tf_op jit(solution)/shard_map/ppermute | solution.py:435
  13.2 5.0 %collective-permute-start.15 = (bf16[64,1600]{1,0:T(8,128)(2,1)S(1)}, bf16[64,1600]{1,0:T(8,128)(2,1)S(1)}, u32[]{:S(2)}, u32[]{:S(2)}) collective-permute-start(bf16[64,1600]{1,0:T(8,128)(2,1)S(1)} %get-tuple-element.40), channel_id=1, source_target_pairs={{8,0},{12,16},{9,1},{13,17},{10,2},{14,18},{11,3},{15,19}} | collective-permute-start | bytes 614408 | tf_op jit(solution)/shard_map/ppermute | solution.py:435
  14.5 9.5 %collective-permute-start.6 = (bf16[64,640]{1,0:T(8,128)(2,1)S(1)}, bf16[64,640]{1,0:T(8,128)(2,1)S(1)}, u32[]{:S(2)}, u32[]{:S(2)}) collective-permute-start(bf16[64,640]{1,0:T(8,128)(2,1)S(1)} %select_select_fusion.1.refs_0_), channel_id=1, source_target_pairs={{0,3},{1,0},{2,1},{3,2},{4,7},{5,4},{6,5},{7,6},{8,11},{9,8},{10,9... | collective-permute-start | bytes 245768 | tf_op jit(solution)/shard_map/ppermute | solution.py:439
  18.2 29.6 %collective-permute-start.18 = (bf16[64,1600]{1,0:T(8,128)(2,1)S(1)}, bf16[64,1600]{1,0:T(8,128)(2,1)S(1)}, u32[]{:S(2)}, u32[]{:S(2)}) collective-permute-start(bf16[64,1600]{1,0:T(8,128)(2,1)S(1)} %select_select_fusion.refs_0_), channel_id=1, source_target_pairs={{0,3},{1,0},{2,1},{3,2},{4,7},{5,4},{6,5},{7,6},{8,11},{9,8},{10,9... | collective-permute-start | bytes 614408 | tf_op jit(solution)/shard_map/ppermute | solution.py:439
  21.1 26.7 %collective-permute-start.17 = (bf16[64,1600]{1,0:T(8,128)(2,1)S(1)}, bf16[64,1600]{1,0:T(8,128)(2,1)S(1)}, u32[]{:S(2)}, u32[]{:S(2)}) collective-permute-start(bf16[64,1600]{1,0:T(8,128)(2,1)S(1)} %select_select_fusion.refs_0_), channel_id=1, source_target_pairs={{0,2},{1,3},{2,0},{3,1},{4,6},{5,7},{6,4},{7,5},{8,10},{9,11},{10,... | collective-permute-start | bytes 614408 | tf_op jit(solution)/shard_map/ppermute | solution.py:439
  21.1 26.7 %collective-permute-start.16 = (bf16[64,1600]{1,0:T(8,128)(2,1)S(1)}, bf16[64,1600]{1,0:T(8,128)(2,1)S(1)}, u32[]{:S(2)}, u32[]{:S(2)}) collective-permute-start(bf16[64,1600]{1,0:T(8,128)(2,1)S(1)} %select_select_fusion.refs_0_), channel_id=1, source_target_pairs={{0,1},{1,2},{2,3},{3,0},{4,5},{5,6},{6,7},{7,4},{8,9},{9,10},{10,1... | collective-permute-start | bytes 614408 | tf_op jit(solution)/shard_map/ppermute | solution.py:439
  22.1 23.0 %collective-permute-start.5 = (bf16[64,640]{1,0:T(8,128)(2,1)S(1)}, bf16[64,640]{1,0:T(8,128)(2,1)S(1)}, u32[]{:S(2)}, u32[]{:S(2)}) collective-permute-start(bf16[64,640]{1,0:T(8,128)(2,1)S(1)} %select_select_fusion.1.refs_0_), channel_id=1, source_target_pairs={{0,2},{1,3},{2,0},{3,1},{4,6},{5,7},{6,4},{7,5},{8,10},{9,11},{10,... | collective-permute-start | bytes 245768 | tf_op jit(solution)/shard_map/ppermute | solution.py:439
  24.0 21.1 %collective-permute-start.4 = (bf16[64,640]{1,0:T(8,128)(2,1)S(1)}, bf16[64,640]{1,0:T(8,128)(2,1)S(1)}, u32[]{:S(2)}, u32[]{:S(2)}) collective-permute-start(bf16[64,640]{1,0:T(8,128)(2,1)S(1)} %select_select_fusion.1.refs_0_), channel_id=1, source_target_pairs={{0,1},{1,2},{2,3},{3,0},{4,5},{5,6},{6,7},{7,4},{8,9},{9,10},{10,1... | collective-permute-start | bytes 245768 | tf_op jit(solution)/shard_map/ppermute | solution.py:439
  25.5 36.1 %slice-start = ((s8[8388608]{0:T(1024)(128)(4,1)}), s8[4194304]{0:T(1024)(128)(4,1)S(1)}, s32[]{:S(2)}) async-start(s8[8388608]{0:T(1024)(128)(4,1)} %bitcast.11), calls=%async_computation | async-start | bytes 8388608
  45.1 16.4 %slice-start.1 = ((s8[8388608]{0:T(1024)(128)(4,1)}), s8[4194304]{0:T(1024)(128)(4,1)S(1)}, s32[]{:S(2)}) async-start(s8[8388608]{0:T(1024)(128)(4,1)} %bitcast.11), calls=%async_computation.1 | async-start | bytes 8388608
  46.7 14.9 %copy-start = (f32[2048]{0:T(1024)S(1)}, f32[2048]{0:T(1024)}, u32[]{:S(2)}) copy-start(f32[2048]{0:T(1024)} %gain.3) | copy-start | bytes 24580
  46.7 14.9 %collective-permute-start.7 = (bf16[128,2048]{1,0:T(8,128)(2,1)S(1)}, bf16[128,2048]{1,0:T(8,128)(2,1)S(1)}, u32[]{:S(2)}, u32[]{:S(2)}) collective-permute-start(bf16[128,2048]{1,0:T(8,128)(2,1)S(1)} %get-tuple-element.32), channel_id=1, source_target_pairs={{0,4},{4,0},{1,5},{5,1},{2,6},{6,2},{3,7},{7,3},{8,12},{12,8},{9,1... | collective-permute-start | bytes 1572872 | tf_op jit(solution)/shard_map/ppermute | solution.py:445
  50.5 21.3 %collective-permute-start.19 = (bf16[128,2048]{1,0:T(8,128)(2,1)S(1)}, bf16[128,2048]{1,0:T(8,128)(2,1)S(1)}, u32[]{:S(2)}, u32[]{:S(2)}) collective-permute-start(bf16[128,2048]{1,0:T(8,128)(2,1)S(1)} %get-tuple-element.43), channel_id=1, source_target_pairs={{0,4},{4,0},{1,5},{5,1},{2,6},{6,2},{3,7},{7,3},{8,12},{12,8},{9,1... | collective-permute-start | bytes 1572872 | tf_op jit(solution)/shard_map/ppermute | solution.py:445
  63.5 11.6 %collective-permute-start.8 = (bf16[136,512]{1,0:T(8,128)(2,1)S(1)}, bf16[136,512]{1,0:T(8,128)(2,1)S(1)}, u32[]{:S(2)}, u32[]{:S(2)}) collective-permute-start(bf16[136,512]{1,0:T(8,128)(2,1)S(1)} %get-tuple-element.34), channel_id=1, source_target_pairs={{0,1},{1,2},{2,3},{3,0},{4,5},{5,6},{6,7},{7,4},{8,9},{9,10},{10,1... | collective-permute-start | bytes 417800 | tf_op jit(solution)/shard_map/ppermute | solution.py:453
  64.6 12.6 %collective-permute-start.9 = (bf16[136,512]{1,0:T(8,128)(2,1)S(1)}, bf16[136,512]{1,0:T(8,128)(2,1)S(1)}, u32[]{:S(2)}, u32[]{:S(2)}) collective-permute-start(bf16[136,512]{1,0:T(8,128)(2,1)S(1)} %get-tuple-element.35), channel_id=1, source_target_pairs={{0,2},{1,3},{2,0},{3,1},{4,6},{5,7},{6,4},{7,5},{8,10},{9,11},{10,... | collective-permute-start | bytes 417800 | tf_op jit(solution)/shard_map/ppermute | solution.py:453
  66.8 12.5 %collective-permute-start.10 = (bf16[136,512]{1,0:T(8,128)(2,1)S(1)}, bf16[136,512]{1,0:T(8,128)(2,1)S(1)}, u32[]{:S(2)}, u32[]{:S(2)}) collective-permute-start(bf16[136,512]{1,0:T(8,128)(2,1)S(1)} %get-tuple-element.36), channel_id=1, source_target_pairs={{0,3},{1,0},{2,1},{3,2},{4,7},{5,4},{6,5},{7,6},{8,11},{9,8},{10,9... | collective-permute-start | bytes 417800 | tf_op jit(solution)/shard_map/ppermute | solution.py:453
  69.5 28.7 %collective-permute-start.24 = (bf16[128,2048]{1,0:T(8,128)(2,1)S(1)}, bf16[128,2048]{1,0:T(8,128)(2,1)S(1)}, u32[]{:S(2)}, u32[]{:S(2)}) collective-permute-start(bf16[128,2048]{1,0:T(8,128)(2,1)S(1)} %get-tuple-element.48), channel_id=1, source_target_pairs={{0,16},{8,24},{1,17},{9,25},{2,18},{10,26},{3,19},{11,27},{4,20},{... | collective-permute-start | bytes 1572872 | tf_op jit(solution)/shard_map/ppermute | solution.py:454
  73.7 24.5 %collective-permute-start.25 = (bf16[128,2048]{1,0:T(8,128)(2,1)S(1)}, bf16[128,2048]{1,0:T(8,128)(2,1)S(1)}, u32[]{:S(2)}, u32[]{:S(2)}) collective-permute-start(bf16[128,2048]{1,0:T(8,128)(2,1)S(1)} %get-tuple-element.49), channel_id=1, source_target_pairs={{0,16},{8,24},{1,17},{9,25},{2,18},{10,26},{3,19},{11,27},{4,20},{... | collective-permute-start | bytes 1572872 | tf_op jit(solution)/shard_map/ppermute | solution.py:454
  75.0 7.7 %collective-permute-start.20 = (bf16[136,512]{1,0:T(8,128)(2,1)S(1)}, bf16[136,512]{1,0:T(8,128)(2,1)S(1)}, u32[]{:S(2)}, u32[]{:S(2)}) collective-permute-start(bf16[136,512]{1,0:T(8,128)(2,1)S(1)} %get-tuple-element.45), channel_id=1, source_target_pairs={{0,1},{1,2},{2,3},{3,0},{4,5},{5,6},{6,7},{7,4},{8,9},{9,10},{10,1... | collective-permute-start | bytes 417800 | tf_op jit(solution)/shard_map/ppermute | solution.py:453
  77.2 10.8 %collective-permute-start.21 = (bf16[136,512]{1,0:T(8,128)(2,1)S(1)}, bf16[136,512]{1,0:T(8,128)(2,1)S(1)}, u32[]{:S(2)}, u32[]{:S(2)}) collective-permute-start(bf16[136,512]{1,0:T(8,128)(2,1)S(1)} %get-tuple-element.46), channel_id=1, source_target_pairs={{0,2},{1,3},{2,0},{3,1},{4,6},{5,7},{6,4},{7,5},{8,10},{9,11},{10,... | collective-permute-start | bytes 417800 | tf_op jit(solution)/shard_map/ppermute | solution.py:453
  79.2 8.8 %collective-permute-start.22 = (bf16[136,512]{1,0:T(8,128)(2,1)S(1)}, bf16[136,512]{1,0:T(8,128)(2,1)S(1)}, u32[]{:S(2)}, u32[]{:S(2)}) collective-permute-start(bf16[136,512]{1,0:T(8,128)(2,1)S(1)} %get-tuple-element.47), channel_id=1, source_target_pairs={{0,3},{1,0},{2,1},{3,2},{4,7},{5,4},{6,5},{7,6},{8,11},{9,8},{10,9... | collective-permute-start | bytes 417800 | tf_op jit(solution)/shard_map/ppermute | solution.py:453
  82.8 13.1 %collective-permute-start.11 = (bf16[128,512]{1,0:T(8,128)(2,1)S(1)}, bf16[128,512]{1,0:T(8,128)(2,1)S(1)}, u32[]{:S(2)}, u32[]{:S(2)}) collective-permute-start(bf16[128,512]{1,0:T(8,128)(2,1)S(1)} %finish.2), channel_id=1, source_target_pairs={{0,16},{8,24},{1,17},{9,25},{2,18},{10,26},{3,19},{11,27},{4,20},{... | collective-permute-start | bytes 393224 | tf_op jit(solution)/shard_map/ppermute | solution.py:456
  88.2 9.1 %collective-permute-start.23 = (bf16[128,512]{1,0:T(8,128)(2,1)S(1)}, bf16[128,512]{1,0:T(8,128)(2,1)S(1)}, u32[]{:S(2)}, u32[]{:S(2)}) collective-permute-start(bf16[128,512]{1,0:T(8,128)(2,1)S(1)} %finish.3), channel_id=1, source_target_pairs={{0,16},{8,24},{1,17},{9,25},{2,18},{10,26},{3,19},{11,27},{4,20},{... | collective-permute-start | bytes 393224 | tf_op jit(solution)/shard_map/ppermute | solution.py:456

commit v3 on v2

--- a/solution.py
+++ b/solution.py
@@ -438,15 +438,16 @@
         for shift in range(1, mp_count):
             pieces.append(lax.ppermute(piece, "mp", rings[shift]))
         gathered.append(pieces)
-    weights = fetch([audio_proj, image_proj], (2, 5))
     partial, others = [], []
-    for stream, proj in enumerate(weights):
+    for stream, (_, _, proj) in enumerate(streams):
+        wanted = [proj] if stream == 0 else [proj, kv_weight]
+        proj, *heads_weight = fetch(wanted, (4,) * len(wanted))
         partial.append(project_rows(mp_count, meta, gathered[stream], proj, 512))
         others.append(lax.ppermute(partial[stream][1], "dp", swap))
     row_parts, head_parts = [], []
     for stream in range(2):
         tokens, own, *sends = heads(
-            mp_count, meta, partial[stream][0], others[stream], input_gain, kv_weight
+            mp_count, meta, partial[stream][0], others[stream], input_gain, heads_weight[0]
         )
         sums = []
         for shift, part in enumerate(sends, 1):

time: 100 us -> 97.9 us (0.979)
  starting transfers between devices: 44 us -> 39.8 us
  Pallas kernels: 14.1 us -> 17.4 us
  waiting for transfers between devices: 38.2 us -> 36.7 us
    ppermute x6, waiting for transfers between devices: 15.8 us -> 11.2 us  [shards_direct(): pieces.append(lax.ppermute(piece, 'mp', rings[shift]))]
    ppermute x6, starting transfers between devices: 13 us -> 9.51 us  [shards_direct(): sums.append(lax.ppermute(part, 'mp', rings[shift]))]
    pallas_call x1 -> x2, Pallas kernels: 3.84 us -> 7.13 us  [fetch(): pl.pallas_call(functools.partial(fetch_kernel, cuts), out_shape=[pltpu.VM...]
    ppermute x2, waiting for transfers between devices: 10 us -> 11.9 us  [shards_direct(): others.append(lax.ppermute(partial[stream][1], 'dp', swap))]
    ppermute x2, waiting for transfers between devices: 7.79 us -> 6.25 us  [shards_direct(): head_parts += [lax.ppermute(values, 'group', up), values]]
    ppermute x6, waiting for transfers between devices: 4.47 us -> 5.98 us  [shards_direct(): sums.append(lax.ppermute(part, 'mp', rings[shift]))]
    ppermute x8, waiting for transfers between devices: 0.07 us -> 1.29 us  [shards_direct(): lax.ppermute(messages[stream * targets + index], ('group', 'dp'), pairs)]
  transfers between devices with their start and end apart: 26 -> 26, of which waited for: 7 -> 9; matrix products, arithmetic and copies ran while one was open for 1% -> 1% of each run, Pallas kernels for 12% -> 16%
where the time goes in v3:
time: 97.9 us; the launch traced here: 97.5 us
  starting transfers between devices  39.8 us (41%)
  waiting for transfers between devices  36.7 us (37%)
  Pallas kernels  17.4 us (18%)
  other arithmetic  2.77 us (3%)
    ppermute x2, waiting for transfers between devices, shards_direct(): others.append(lax.ppermute(partial[stream][1], 'dp', swap))  11.9 us
    ppermute x8, starting transfers between devices, shards_direct(): lax.ppermute(messages[stream * targets + index], ('group', 'dp'), pairs)  11.7 us
    ppermute x6, waiting for transfers between devices, shards_direct(): pieces.append(lax.ppermute(piece, 'mp', rings[shift]))  11.2 us
    ppermute x6, starting transfers between devices, shards_direct(): pieces.append(lax.ppermute(piece, 'mp', rings[shift]))  10.2 us
    ppermute x6, starting transfers between devices, shards_direct(): sums.append(lax.ppermute(part, 'mp', rings[shift]))  9.51 us
    pallas_call x2, Pallas kernels, fetch(): pl.pallas_call(functools.partial(fetch_kernel, cuts), out_shape=[pltpu.VM...  7.13 us
    ppermute x2, waiting for transfers between devices, shards_direct(): head_parts += [lax.ppermute(values, 'group', up), values]  6.25 us
    ppermute x6, waiting for transfers between devices, shards_direct(): sums.append(lax.ppermute(part, 'mp', rings[shift]))  5.98 us
  transfers between devices with their start and end apart: 26, of which 9 were waited for; matrix products, arithmetic and copies ran while one was open for 1% of the time, Pallas kernels for 16%

profile of v3, /device:TPU:0, one launch (start us, length us, event | category | flops | bytes accessed | tf_op | source)
XLA Modules:
  0.0 97.5 jit_solution(13948653482964689658)
XLA Ops:
  0.6 0.1 pad_add_fusion.meta
  0.7 1.8 %encode.1 = (bf16[64,640]{1,0:T(8,128)(2,1)S(1)}, bf16[64,640]{1,0:T(8,128)(2,1)S(1)}, bf16[64,640]{1,0:T(8,128)(2,1)S(1)}, bf16[64,640]{1,0:T(8,128)(2,1)S(1)},...) custom-call(s32[3]{0:T(128)S(1)} %pad_add_fusion.meta, ...), custom_call_target="tpu_custom_call" | custom-call | flops 268435456 | tf_op jit(solution)/shard_map/encode/pallas_call | solution.py:257
  2.6 4.8 %collective-permute-start = (bf16[64,640]{1,0:T(8,128)(2,1)S(1)}, bf16[64,640]{1,0:T(8,128)(2,1)S(1)}, u32[]{:S(2)}, u32[]{:S(2)}) collective-permute-start(bf16[64,640]{1,0:T(8,128)(2,1)S(1)} %get-tuple-element.26), channel_id=1, source_target_pairs={{0,12},{4,28},{1,13},{5,29},{2,14},{6,30},{3,15},{7,31}} | collective-permute-start | bytes 245768 | tf_op jit(solution)/shard_map/ppermute | solution.py:435
  7.4 1.3 %collective-permute-start.1 = (bf16[64,640]{1,0:T(8,128)(2,1)S(1)}, bf16[64,640]{1,0:T(8,128)(2,1)S(1)}, u32[]{:S(2)}, u32[]{:S(2)}) collective-permute-start(bf16[64,640]{1,0:T(8,128)(2,1)S(1)} %get-tuple-element.27), channel_id=1, source_target_pairs={{0,8},{4,24},{1,9},{5,25},{2,10},{6,26},{3,11},{7,27}} | collective-permute-start | bytes 245768 | tf_op jit(solution)/shard_map/ppermute | solution.py:435
  8.7 1.7 %collective-permute-start.2 = (bf16[64,640]{1,0:T(8,128)(2,1)S(1)}, bf16[64,640]{1,0:T(8,128)(2,1)S(1)}, u32[]{:S(2)}, u32[]{:S(2)}) collective-permute-start(bf16[64,640]{1,0:T(8,128)(2,1)S(1)} %get-tuple-element.28), channel_id=1, source_target_pairs={{0,4},{4,20},{1,5},{5,21},{2,6},{6,22},{3,7},{7,23}} | collective-permute-start | bytes 245768 | tf_op jit(solution)/shard_map/ppermute | solution.py:435
  10.4 0.7 collective-permute-start.3
  11.0 0.7 collective-permute-start.12
  11.8 0.7 collective-permute-start.13
  12.4 0.7 collective-permute-start.14
  13.1 0.1 collective-permute-done.2
  13.2 1.3 %collective-permute-start.15 = (bf16[64,1600]{1,0:T(8,128)(2,1)S(1)}, bf16[64,1600]{1,0:T(8,128)(2,1)S(1)}, u32[]{:S(2)}, u32[]{:S(2)}) collective-permute-start(bf16[64,1600]{1,0:T(8,128)(2,1)S(1)} %get-tuple-element.40), channel_id=1, source_target_pairs={{8,0},{12,16},{9,1},{13,17},{10,2},{14,18},{11,3},{15,19}} | collective-permute-start | bytes 614408 | tf_op jit(solution)/shard_map/ppermute | solution.py:435
  14.5 1.6 %collective-permute-start.4 = (bf16[64,640]{1,0:T(8,128)(2,1)S(1)}, bf16[64,640]{1,0:T(8,128)(2,1)S(1)}, u32[]{:S(2)}, u32[]{:S(2)}) collective-permute-start(bf16[64,640]{1,0:T(8,128)(2,1)S(1)} %select_select_fusion.1.refs_0_), channel_id=1, source_target_pairs={{0,1},{1,2},{2,3},{3,0},{4,5},{5,6},{6,7},{7,4},{8,9},{9,10},{10,1... | collective-permute-start | bytes 245768 | tf_op jit(solution)/shard_map/ppermute | solution.py:439
  16.2 1.2 %collective-permute-done.15 = bf16[64,1600]{1,0:T(8,128)(2,1)S(1)} collective-permute-done((bf16[64,1600]{1,0:T(8,128)(2,1)S(1)}, bf16[64,1600]{1,0:T(8,128)(2,1)S(1)}, u32[]{:S(2)}, u32[]{:S(2)}) %collective-permute-start.15) | collective-permute-done | bytes 204832 | tf_op jit(solution)/shard_map/ppermute | solution.py:435
  17.4 1.6 %collective-permute-start.16 = (bf16[64,1600]{1,0:T(8,128)(2,1)S(1)}, bf16[64,1600]{1,0:T(8,128)(2,1)S(1)}, u32[]{:S(2)}, u32[]{:S(2)}) collective-permute-start(bf16[64,1600]{1,0:T(8,128)(2,1)S(1)} %select_select_fusion.refs_0_), channel_id=1, source_target_pairs={{0,1},{1,2},{2,3},{3,0},{4,5},{5,6},{6,7},{7,4},{8,9},{9,10},{10,1... | collective-permute-start | bytes 614408 | tf_op jit(solution)/shard_map/ppermute | solution.py:439
  19.0 2.6 %collective-permute-start.17 = (bf16[64,1600]{1,0:T(8,128)(2,1)S(1)}, bf16[64,1600]{1,0:T(8,128)(2,1)S(1)}, u32[]{:S(2)}, u32[]{:S(2)}) collective-permute-start(bf16[64,1600]{1,0:T(8,128)(2,1)S(1)} %select_select_fusion.refs_0_), channel_id=1, source_target_pairs={{0,2},{1,3},{2,0},{3,1},{4,6},{5,7},{6,4},{7,5},{8,10},{9,11},{10,... | collective-permute-start | bytes 614408 | tf_op jit(solution)/shard_map/ppermute | solution.py:439
  21.6 1.3 %collective-permute-start.18 = (bf16[64,1600]{1,0:T(8,128)(2,1)S(1)}, bf16[64,1600]{1,0:T(8,128)(2,1)S(1)}, u32[]{:S(2)}, u32[]{:S(2)}) collective-permute-start(bf16[64,1600]{1,0:T(8,128)(2,1)S(1)} %select_select_fusion.refs_0_), channel_id=1, source_target_pairs={{0,3},{1,0},{2,1},{3,2},{4,7},{5,4},{6,5},{7,6},{8,11},{9,8},{10,9... | collective-permute-start | bytes 614408 | tf_op jit(solution)/shard_map/ppermute | solution.py:439
  23.0 0.3 collective-permute-start.5
  23.3 2.7 %collective-permute-start.6 = (bf16[64,640]{1,0:T(8,128)(2,1)S(1)}, bf16[64,640]{1,0:T(8,128)(2,1)S(1)}, u32[]{:S(2)}, u32[]{:S(2)}) collective-permute-start(bf16[64,640]{1,0:T(8,128)(2,1)S(1)} %select_select_fusion.1.refs_0_), channel_id=1, source_target_pairs={{0,3},{1,0},{2,1},{3,2},{4,7},{5,4},{6,5},{7,6},{8,11},{9,8},{10,9... | collective-permute-start | bytes 245768 | tf_op jit(solution)/shard_map/ppermute | solution.py:439
  26.0 1.7 %fetch.2.refs_4_ = bf16[640,2048]{1,0:T(8,128)(2,1)S(1)} custom-call(bf16[640,2048]{1,0:T(8,128)(2,1)} %refs_0_.4), custom_call_target="tpu_custom_call" | custom-call | flops 268435456 | tf_op jit(solution)/shard_map/fetch/pallas_call | solution.py:286
  27.7 5.4 %fetch.3 = (bf16[1600,2048]{1,0:T(8,128)(2,1)S(1)}, bf16[2048,2048]{1,0:T(8,128)(2,1)S(1)}) custom-call(bf16[1600,2048]{1,0:T(8,128)(2,1)} %refs_0_.5, bf16[2048,2048]{1,0:T(8,128)(2,1)} %refs_1_.3), custom_call_target="tpu_custom_call" | custom-call | flops 268435456 | tf_op jit(solution)/shard_map/fetch/pallas_call | solution.py:286
  33.2 11.2 %collective-permute-done.5.refs_2_ = bf16[64,640]{1,0:T(8,128)(2,1)S(1)} collective-permute-done((bf16[64,640]{1,0:T(8,128)(2,1)S(1)}, bf16[64,640]{1,0:T(8,128)(2,1)S(1)}, u32[]{:S(2)}, u32[]{:S(2)}) %collective-permute-start.5) | collective-permute-done | bytes 81952 | tf_op jit(solution)/shard_map/ppermute | solution.py:439
  44.4 1.5 %project.2 = (f32[128,2048]{1,0:T(8,128)S(1)}, bf16[128,2048]{1,0:T(8,128)(2,1)S(1)}) custom-call(s32[3]{0:T(128)S(1)} %pad_add_fusion.meta, bf16[64,640]{1,0:T(8,128)(2,1)S(1)} %select_select_fusion.1.refs_0_, bf16[64,640]{1,0:T(8,128)(2,1)S(1)} %collective-permute-done.4.refs_1_, bf16[64,640]{1,0:T(8,128)(2,1)S(1)} %collective-permute-done.5.refs_2_, ...), custom_call_target="tpu_custom_call" | custom-call | flops 671088640 | tf_op jit(solution)/shard_map/project/pallas_call | solution.py:317
  45.9 0.0 copy-start
  45.9 0.5 collective-permute-start.7
  46.4 2.7 %project.3 = (f32[128,2048]{1,0:T(8,128)S(1)}, bf16[128,2048]{1,0:T(8,128)(2,1)S(1)}) custom-call(s32[3]{0:T(128)S(1)} %pad_add_fusion.meta, bf16[64,1600]{1,0:T(8,128)(2,1)S(1)} %select_select_fusion.refs_0_, bf16[64,1600]{1,0:T(8,128)(2,1)S(1)} %collective-permute-done.16.refs_1_, bf16[64,1600]{1,0:T(8,128)(2,1)S(1)} %collective-permute-done.17.refs_2_, ...), custom_call_target="tpu_custom_call" | custom-call | flops 1677721600 | tf_op jit(solution)/shard_map/project/pallas_call | solution.py:317
  49.1 1.6 %collective-permute-start.19 = (bf16[128,2048]{1,0:T(8,128)(2,1)S(1)}, bf16[128,2048]{1,0:T(8,128)(2,1)S(1)}, u32[]{:S(2)}, u32[]{:S(2)}) collective-permute-start(bf16[128,2048]{1,0:T(8,128)(2,1)S(1)} %get-tuple-element.43), channel_id=1, source_target_pairs={{0,4},{4,0},{1,5},{5,1},{2,6},{6,2},{3,7},{7,3},{8,12},{12,8},{9,1... | collective-permute-start | bytes 1572872 | tf_op jit(solution)/shard_map/ppermute | solution.py:446
  50.8 10.0 %collective-permute-done.7.other = bf16[128,2048]{1,0:T(8,128)(2,1)S(1)} collective-permute-done((bf16[128,2048]{1,0:T(8,128)(2,1)S(1)}, bf16[128,2048]{1,0:T(8,128)(2,1)S(1)}, u32[]{:S(2)}, u32[]{:S(2)}) %collective-permute-start.7) | collective-permute-done | bytes 524320 | tf_op jit(solution)/shard_map/ppermute | solution.py:446
  60.8 1.9 %heads.2 = (bf16[128,2048]{1,0:T(8,128)(2,1)S(1)}, f32[136,512]{1,0:T(8,128)S(1)}, bf16[136,512]{1,0:T(8,128)(2,1)S(1)}, bf16[136,512]{1,0:T(8,128)(2,1)S(1)}, bf16[136,512]{1,0:T(8,128)(2,1)S(1)}) custom-call(s32[3]{0:T(128)S(1)} %pad_add_fusion.meta, f32[128,2048]{1,0:T(8,128)S(1)} %get-tuple-element.30.keep, ...), custom_call_target="tpu_custom_call" | custom-call | flops 1073741824 | tf_op jit(solution)/shard_map/heads/pallas_call | solution.py:359
  62.7 2.3 %collective-permute-start.8 = (bf16[136,512]{1,0:T(8,128)(2,1)S(1)}, bf16[136,512]{1,0:T(8,128)(2,1)S(1)}, u32[]{:S(2)}, u32[]{:S(2)}) collective-permute-start(bf16[136,512]{1,0:T(8,128)(2,1)S(1)} %get-tuple-element.34), channel_id=1, source_target_pairs={{0,1},{1,2},{2,3},{3,0},{4,5},{5,6},{6,7},{7,4},{8,9},{9,10},{10,1... | collective-permute-start | bytes 417800 | tf_op jit(solution)/shard_map/ppermute | solution.py:454
  65.0 1.5 %collective-permute-start.9 = (bf16[136,512]{1,0:T(8,128)(2,1)S(1)}, bf16[136,512]{1,0:T(8,128)(2,1)S(1)}, u32[]{:S(2)}, u32[]{:S(2)}) collective-permute-start(bf16[136,512]{1,0:T(8,128)(2,1)S(1)} %get-tuple-element.35), channel_id=1, source_target_pairs={{0,2},{1,3},{2,0},{3,1},{4,6},{5,7},{6,4},{7,5},{8,10},{9,11},{10,... | collective-permute-start | bytes 417800 | tf_op jit(solution)/shard_map/ppermute | solution.py:454
  66.5 0.9 collective-permute-start.10
  67.4 1.7 %collective-permute-start.24 = (bf16[128,2048]{1,0:T(8,128)(2,1)S(1)}, bf16[128,2048]{1,0:T(8,128)(2,1)S(1)}, u32[]{:S(2)}, u32[]{:S(2)}) collective-permute-start(bf16[128,2048]{1,0:T(8,128)(2,1)S(1)} %get-tuple-element.48), channel_id=1, source_target_pairs={{0,16},{8,24},{1,17},{9,25},{2,18},{10,26},{3,19},{11,27},{4,20},{... | collective-permute-start | bytes 1572872 | tf_op jit(solution)/shard_map/ppermute | solution.py:455
  69.1 1.9 %collective-permute-done.19.other = bf16[128,2048]{1,0:T(8,128)(2,1)S(1)} collective-permute-done((bf16[128,2048]{1,0:T(8,128)(2,1)S(1)}, bf16[128,2048]{1,0:T(8,128)(2,1)S(1)}, u32[]{:S(2)}, u32[]{:S(2)}) %collective-permute-start.19) | collective-permute-done | bytes 524320 | tf_op jit(solution)/shard_map/ppermute | solution.py:446
  71.0 1.9 %heads.3 = (bf16[128,2048]{1,0:T(8,128)(2,1)S(1)}, f32[136,512]{1,0:T(8,128)S(1)}, bf16[136,512]{1,0:T(8,128)(2,1)S(1)}, bf16[136,512]{1,0:T(8,128)(2,1)S(1)}, bf16[136,512]{1,0:T(8,128)(2,1)S(1)}) custom-call(s32[3]{0:T(128)S(1)} %pad_add_fusion.meta, f32[128,2048]{1,0:T(8,128)S(1)} %get-tuple-element.42.keep, ...), custom_call_target="tpu_custom_call" | custom-call | flops 1073741824 | tf_op jit(solution)/shard_map/heads/pallas_call | solution.py:359
  72.9 1.7 %collective-permute-start.25 = (bf16[128,2048]{1,0:T(8,128)(2,1)S(1)}, bf16[128,2048]{1,0:T(8,128)(2,1)S(1)}, u32[]{:S(2)}, u32[]{:S(2)}) collective-permute-start(bf16[128,2048]{1,0:T(8,128)(2,1)S(1)} %get-tuple-element.49), channel_id=1, source_target_pairs={{0,16},{8,24},{1,17},{9,25},{2,18},{10,26},{3,19},{11,27},{4,20},{... | collective-permute-start | bytes 1572872 | tf_op jit(solution)/shard_map/ppermute | solution.py:455
  74.6 2.4 %collective-permute-start.20 = (bf16[136,512]{1,0:T(8,128)(2,1)S(1)}, bf16[136,512]{1,0:T(8,128)(2,1)S(1)}, u32[]{:S(2)}, u32[]{:S(2)}) collective-permute-start(bf16[136,512]{1,0:T(8,128)(2,1)S(1)} %get-tuple-element.45), channel_id=1, source_target_pairs={{0,1},{1,2},{2,3},{3,0},{4,5},{5,6},{6,7},{7,4},{8,9},{9,10},{10,1... | collective-permute-start | bytes 417800 | tf_op jit(solution)/shard_map/ppermute | solution.py:454
  77.0 0.8 collective-permute-start.21
  77.8 1.6 %collective-permute-start.22 = (bf16[136,512]{1,0:T(8,128)(2,1)S(1)}, bf16[136,512]{1,0:T(8,128)(2,1)S(1)}, u32[]{:S(2)}, u32[]{:S(2)}) collective-permute-start(bf16[136,512]{1,0:T(8,128)(2,1)S(1)} %get-tuple-element.47), channel_id=1, source_target_pairs={{0,3},{1,0},{2,1},{3,2},{4,7},{5,4},{6,5},{7,6},{8,11},{9,8},{10,9... | collective-permute-start | bytes 417800 | tf_op jit(solution)/shard_map/ppermute | solution.py:454
  79.4 0.2 finish.2
  79.6 3.4 %collective-permute-done.20.refs_0_ = bf16[136,512]{1,0:T(8,128)(2,1)S(1)} collective-permute-done((bf16[136,512]{1,0:T(8,128)(2,1)S(1)}, bf16[136,512]{1,0:T(8,128)(2,1)S(1)}, u32[]{:S(2)}, u32[]{:S(2)}) %collective-permute-start.20) | collective-permute-done | bytes 139296 | tf_op jit(solution)/shard_map/ppermute | solution.py:454
  83.1 1.3 %collective-permute-start.11 = (bf16[128,512]{1,0:T(8,128)(2,1)S(1)}, bf16[128,512]{1,0:T(8,128)(2,1)S(1)}, u32[]{:S(2)}, u32[]{:S(2)}) collective-permute-start(bf16[128,512]{1,0:T(8,128)(2,1)S(1)} %finish.2), channel_id=1, source_target_pairs={{0,16},{8,24},{1,17},{9,25},{2,18},{10,26},{3,19},{11,27},{4,20},{... | collective-permute-start | bytes 393224 | tf_op jit(solution)/shard_map/ppermute | solution.py:457
  84.3 2.5 %collective-permute-done.21.refs_1_ = bf16[136,512]{1,0:T(8,128)(2,1)S(1)} collective-permute-done((bf16[136,512]{1,0:T(8,128)(2,1)S(1)}, bf16[136,512]{1,0:T(8,128)(2,1)S(1)}, u32[]{:S(2)}, u32[]{:S(2)}) %collective-permute-start.21) | collective-permute-done | bytes 139296 | tf_op jit(solution)/shard_map/ppermute | solution.py:454
  86.9 0.2 finish.3
  87.1 1.5 %collective-permute-start.23 = (bf16[128,512]{1,0:T(8,128)(2,1)S(1)}, bf16[128,512]{1,0:T(8,128)(2,1)S(1)}, u32[]{:S(2)}, u32[]{:S(2)}) collective-permute-start(bf16[128,512]{1,0:T(8,128)(2,1)S(1)} %finish.3), channel_id=1, source_target_pairs={{0,16},{8,24},{1,17},{9,25},{2,18},{10,26},{3,19},{11,27},{4,20},{... | collective-permute-start | bytes 393224 | tf_op jit(solution)/shard_map/ppermute | solution.py:457
  88.6 4.8 %collective-permute-done.11 = bf16[128,512]{1,0:T(8,128)(2,1)S(1)} collective-permute-done((bf16[128,512]{1,0:T(8,128)(2,1)S(1)}, bf16[128,512]{1,0:T(8,128)(2,1)S(1)}, u32[]{:S(2)}, u32[]{:S(2)}) %collective-permute-start.11) | collective-permute-done | bytes 131104 | tf_op jit(solution)/shard_map/ppermute | solution.py:457
  93.5 1.4 %collective-permute-done.23 = bf16[128,512]{1,0:T(8,128)(2,1)S(1)} collective-permute-done((bf16[128,512]{1,0:T(8,128)(2,1)S(1)}, bf16[128,512]{1,0:T(8,128)(2,1)S(1)}, u32[]{:S(2)}, u32[]{:S(2)}) %collective-permute-start.23) | collective-permute-done | bytes 131104 | tf_op jit(solution)/shard_map/ppermute | solution.py:457
  94.9 0.9 maximum_select_fusion.1
  95.8 1.7 %maximum_select_fusion = bf16[1,512,2048]{2,1,0:T(8,128)(2,1)} fusion(bf16[1,128,2048]{2,1,0:T(8,128)(2,1)S(1)} %bitcast.12, bf16[1,128,2048]{2,1,0:T(8,128)(2,1)S(1)} %bitcast.16, bf16[1,128,2048]{2,1,0:T(8,128)(2,1)S(1)} %bitcast.11, bf16[1,128,2048]{2,1,0:T(8,128)(2,1)S(1)} %bitcast.15, pred[]{:T(512)S(6)} %ge.3), kind=kLoop, calls=%fused_computation | loop fusion | flops 9437184 | bytes 4194305 | tf_op jit(solution)/shard_map/jit(_where)/select_n | solution.py:459
  (20 shorter events, 0.1 us)
Async XLA Ops:
  2.6 9.2 %collective-permute-start = (bf16[64,640]{1,0:T(8,128)(2,1)S(1)}, bf16[64,640]{1,0:T(8,128)(2,1)S(1)}, u32[]{:S(2)}, u32[]{:S(2)}) collective-permute-start(bf16[64,640]{1,0:T(8,128)(2,1)S(1)} %get-tuple-element.26), channel_id=1, source_target_pairs={{0,12},{4,28},{1,13},{5,29},{2,14},{6,30},{3,15},{7,31}} | collective-permute-start | bytes 245768 | tf_op jit(solution)/shard_map/ppermute | solution.py:435
  7.4 5.0 %collective-permute-start.1 = (bf16[64,640]{1,0:T(8,128)(2,1)S(1)}, bf16[64,640]{1,0:T(8,128)(2,1)S(1)}, u32[]{:S(2)}, u32[]{:S(2)}) collective-permute-start(bf16[64,640]{1,0:T(8,128)(2,1)S(1)} %get-tuple-element.27), channel_id=1, source_target_pairs={{0,8},{4,24},{1,9},{5,25},{2,10},{6,26},{3,11},{7,27}} | collective-permute-start | bytes 245768 | tf_op jit(solution)/shard_map/ppermute | solution.py:435
  8.7 4.5 %collective-permute-start.2 = (bf16[64,640]{1,0:T(8,128)(2,1)S(1)}, bf16[64,640]{1,0:T(8,128)(2,1)S(1)}, u32[]{:S(2)}, u32[]{:S(2)}) collective-permute-start(bf16[64,640]{1,0:T(8,128)(2,1)S(1)} %get-tuple-element.28), channel_id=1, source_target_pairs={{0,4},{4,20},{1,5},{5,21},{2,6},{6,22},{3,7},{7,23}} | collective-permute-start | bytes 245768 | tf_op jit(solution)/shard_map/ppermute | solution.py:435
  10.4 4.1 %collective-permute-start.3 = (bf16[64,640]{1,0:T(8,128)(2,1)S(1)}, bf16[64,640]{1,0:T(8,128)(2,1)S(1)}, u32[]{:S(2)}, u32[]{:S(2)}) collective-permute-start(bf16[64,640]{1,0:T(8,128)(2,1)S(1)} %get-tuple-element.29), channel_id=1, source_target_pairs={{0,0},{4,16},{1,1},{5,17},{2,2},{6,18},{3,3},{7,19}} | collective-permute-start | bytes 245768 | tf_op jit(solution)/shard_map/ppermute | solution.py:435
  11.0 5.1 %collective-permute-start.12 = (bf16[64,1600]{1,0:T(8,128)(2,1)S(1)}, bf16[64,1600]{1,0:T(8,128)(2,1)S(1)}, u32[]{:S(2)}, u32[]{:S(2)}) collective-permute-start(bf16[64,1600]{1,0:T(8,128)(2,1)S(1)} %get-tuple-element.37), channel_id=1, source_target_pairs={{8,12},{12,28},{9,13},{13,29},{10,14},{14,30},{11,15},{15,31}} | collective-permute-start | bytes 614408 | tf_op jit(solution)/shard_map/ppermute | solution.py:435
  11.8 4.4 %collective-permute-start.13 = (bf16[64,1600]{1,0:T(8,128)(2,1)S(1)}, bf16[64,1600]{1,0:T(8,128)(2,1)S(1)}, u32[]{:S(2)}, u32[]{:S(2)}) collective-permute-start(bf16[64,1600]{1,0:T(8,128)(2,1)S(1)} %get-tuple-element.38), channel_id=1, source_target_pairs={{8,8},{12,24},{9,9},{13,25},{10,10},{14,26},{11,11},{15,27}} | collective-permute-start | bytes 614408 | tf_op jit(solution)/shard_map/ppermute | solution.py:435
  12.4 3.7 %collective-permute-start.14 = (bf16[64,1600]{1,0:T(8,128)(2,1)S(1)}, bf16[64,1600]{1,0:T(8,128)(2,1)S(1)}, u32[]{:S(2)}, u32[]{:S(2)}) collective-permute-start(bf16[64,1600]{1,0:T(8,128)(2,1)S(1)} %get-tuple-element.39), channel_id=1, source_target_pairs={{8,4},{12,20},{9,5},{13,21},{10,6},{14,22},{11,7},{15,23}} | collective-permute-start | bytes 614408 | tf_op jit(solution)/shard_map/ppermute | solution.py:435
  13.2 4.2 %collective-permute-start.15 = (bf16[64,1600]{1,0:T(8,128)(2,1)S(1)}, bf16[64,1600]{1,0:T(8,128)(2,1)S(1)}, u32[]{:S(2)}, u32[]{:S(2)}) collective-permute-start(bf16[64,1600]{1,0:T(8,128)(2,1)S(1)} %get-tuple-element.40), channel_id=1, source_target_pairs={{8,0},{12,16},{9,1},{13,17},{10,2},{14,18},{11,3},{15,19}} | collective-permute-start | bytes 614408 | tf_op jit(solution)/shard_map/ppermute | solution.py:435
  14.5 8.8 %collective-permute-start.4 = (bf16[64,640]{1,0:T(8,128)(2,1)S(1)}, bf16[64,640]{1,0:T(8,128)(2,1)S(1)}, u32[]{:S(2)}, u32[]{:S(2)}) collective-permute-start(bf16[64,640]{1,0:T(8,128)(2,1)S(1)} %select_select_fusion.1.refs_0_), channel_id=1, source_target_pairs={{0,1},{1,2},{2,3},{3,0},{4,5},{5,6},{6,7},{7,4},{8,9},{9,10},{10,1... | collective-permute-start | bytes 245768 | tf_op jit(solution)/shard_map/ppermute | solution.py:439
  17.4 29.0 %collective-permute-start.16 = (bf16[64,1600]{1,0:T(8,128)(2,1)S(1)}, bf16[64,1600]{1,0:T(8,128)(2,1)S(1)}, u32[]{:S(2)}, u32[]{:S(2)}) collective-permute-start(bf16[64,1600]{1,0:T(8,128)(2,1)S(1)} %select_select_fusion.refs_0_), channel_id=1, source_target_pairs={{0,1},{1,2},{2,3},{3,0},{4,5},{5,6},{6,7},{7,4},{8,9},{9,10},{10,1... | collective-permute-start | bytes 614408 | tf_op jit(solution)/shard_map/ppermute | solution.py:439
  19.0 27.4 %collective-permute-start.17 = (bf16[64,1600]{1,0:T(8,128)(2,1)S(1)}, bf16[64,1600]{1,0:T(8,128)(2,1)S(1)}, u32[]{:S(2)}, u32[]{:S(2)}) collective-permute-start(bf16[64,1600]{1,0:T(8,128)(2,1)S(1)} %select_select_fusion.refs_0_), channel_id=1, source_target_pairs={{0,2},{1,3},{2,0},{3,1},{4,6},{5,7},{6,4},{7,5},{8,10},{9,11},{10,... | collective-permute-start | bytes 614408 | tf_op jit(solution)/shard_map/ppermute | solution.py:439
  21.6 24.8 %collective-permute-start.18 = (bf16[64,1600]{1,0:T(8,128)(2,1)S(1)}, bf16[64,1600]{1,0:T(8,128)(2,1)S(1)}, u32[]{:S(2)}, u32[]{:S(2)}) collective-permute-start(bf16[64,1600]{1,0:T(8,128)(2,1)S(1)} %select_select_fusion.refs_0_), channel_id=1, source_target_pairs={{0,3},{1,0},{2,1},{3,2},{4,7},{5,4},{6,5},{7,6},{8,11},{9,8},{10,9... | collective-permute-start | bytes 614408 | tf_op jit(solution)/shard_map/ppermute | solution.py:439
  23.0 21.4 %collective-permute-start.5 = (bf16[64,640]{1,0:T(8,128)(2,1)S(1)}, bf16[64,640]{1,0:T(8,128)(2,1)S(1)}, u32[]{:S(2)}, u32[]{:S(2)}) collective-permute-start(bf16[64,640]{1,0:T(8,128)(2,1)S(1)} %select_select_fusion.1.refs_0_), channel_id=1, source_target_pairs={{0,2},{1,3},{2,0},{3,1},{4,6},{5,7},{6,4},{7,5},{8,10},{9,11},{10,... | collective-permute-start | bytes 245768 | tf_op jit(solution)/shard_map/ppermute | solution.py:439
  23.3 21.0 %collective-permute-start.6 = (bf16[64,640]{1,0:T(8,128)(2,1)S(1)}, bf16[64,640]{1,0:T(8,128)(2,1)S(1)}, u32[]{:S(2)}, u32[]{:S(2)}) collective-permute-start(bf16[64,640]{1,0:T(8,128)(2,1)S(1)} %select_select_fusion.1.refs_0_), channel_id=1, source_target_pairs={{0,3},{1,0},{2,1},{3,2},{4,7},{5,4},{6,5},{7,6},{8,11},{9,8},{10,9... | collective-permute-start | bytes 245768 | tf_op jit(solution)/shard_map/ppermute | solution.py:439
  45.9 14.9 %copy-start = (f32[2048]{0:T(1024)S(1)}, f32[2048]{0:T(1024)}, u32[]{:S(2)}) copy-start(f32[2048]{0:T(1024)} %gain.3) | copy-start | bytes 24580
  45.9 14.9 %collective-permute-start.7 = (bf16[128,2048]{1,0:T(8,128)(2,1)S(1)}, bf16[128,2048]{1,0:T(8,128)(2,1)S(1)}, u32[]{:S(2)}, u32[]{:S(2)}) collective-permute-start(bf16[128,2048]{1,0:T(8,128)(2,1)S(1)} %get-tuple-element.31), channel_id=1, source_target_pairs={{0,4},{4,0},{1,5},{5,1},{2,6},{6,2},{3,7},{7,3},{8,12},{12,8},{9,1... | collective-permute-start | bytes 1572872 | tf_op jit(solution)/shard_map/ppermute | solution.py:446
  49.1 21.9 %collective-permute-start.19 = (bf16[128,2048]{1,0:T(8,128)(2,1)S(1)}, bf16[128,2048]{1,0:T(8,128)(2,1)S(1)}, u32[]{:S(2)}, u32[]{:S(2)}) collective-permute-start(bf16[128,2048]{1,0:T(8,128)(2,1)S(1)} %get-tuple-element.43), channel_id=1, source_target_pairs={{0,4},{4,0},{1,5},{5,1},{2,6},{6,2},{3,7},{7,3},{8,12},{12,8},{9,1... | collective-permute-start | bytes 1572872 | tf_op jit(solution)/shard_map/ppermute | solution.py:446
  62.7 11.9 %collective-permute-start.8 = (bf16[136,512]{1,0:T(8,128)(2,1)S(1)}, bf16[136,512]{1,0:T(8,128)(2,1)S(1)}, u32[]{:S(2)}, u32[]{:S(2)}) collective-permute-start(bf16[136,512]{1,0:T(8,128)(2,1)S(1)} %get-tuple-element.34), channel_id=1, source_target_pairs={{0,1},{1,2},{2,3},{3,0},{4,5},{5,6},{6,7},{7,4},{8,9},{9,10},{10,1... | collective-permute-start | bytes 417800 | tf_op jit(solution)/shard_map/ppermute | solution.py:454
  65.0 12.0 %collective-permute-start.9 = (bf16[136,512]{1,0:T(8,128)(2,1)S(1)}, bf16[136,512]{1,0:T(8,128)(2,1)S(1)}, u32[]{:S(2)}, u32[]{:S(2)}) collective-permute-start(bf16[136,512]{1,0:T(8,128)(2,1)S(1)} %get-tuple-element.35), channel_id=1, source_target_pairs={{0,2},{1,3},{2,0},{3,1},{4,6},{5,7},{6,4},{7,5},{8,10},{9,11},{10,... | collective-permute-start | bytes 417800 | tf_op jit(solution)/shard_map/ppermute | solution.py:454
  66.5 11.3 %collective-permute-start.10 = (bf16[136,512]{1,0:T(8,128)(2,1)S(1)}, bf16[136,512]{1,0:T(8,128)(2,1)S(1)}, u32[]{:S(2)}, u32[]{:S(2)}) collective-permute-start(bf16[136,512]{1,0:T(8,128)(2,1)S(1)} %get-tuple-element.36), channel_id=1, source_target_pairs={{0,3},{1,0},{2,1},{3,2},{4,7},{5,4},{6,5},{7,6},{8,11},{9,8},{10,9... | collective-permute-start | bytes 417800 | tf_op jit(solution)/shard_map/ppermute | solution.py:454
  67.4 28.4 %collective-permute-start.24 = (bf16[128,2048]{1,0:T(8,128)(2,1)S(1)}, bf16[128,2048]{1,0:T(8,128)(2,1)S(1)}, u32[]{:S(2)}, u32[]{:S(2)}) collective-permute-start(bf16[128,2048]{1,0:T(8,128)(2,1)S(1)} %get-tuple-element.48), channel_id=1, source_target_pairs={{0,16},{8,24},{1,17},{9,25},{2,18},{10,26},{3,19},{11,27},{4,20},{... | collective-permute-start | bytes 1572872 | tf_op jit(solution)/shard_map/ppermute | solution.py:455
  72.9 22.9 %collective-permute-start.25 = (bf16[128,2048]{1,0:T(8,128)(2,1)S(1)}, bf16[128,2048]{1,0:T(8,128)(2,1)S(1)}, u32[]{:S(2)}, u32[]{:S(2)}) collective-permute-start(bf16[128,2048]{1,0:T(8,128)(2,1)S(1)} %get-tuple-element.49), channel_id=1, source_target_pairs={{0,16},{8,24},{1,17},{9,25},{2,18},{10,26},{3,19},{11,27},{4,20},{... | collective-permute-start | bytes 1572872 | tf_op jit(solution)/shard_map/ppermute | solution.py:455
  74.6 8.4 %collective-permute-start.20 = (bf16[136,512]{1,0:T(8,128)(2,1)S(1)}, bf16[136,512]{1,0:T(8,128)(2,1)S(1)}, u32[]{:S(2)}, u32[]{:S(2)}) collective-permute-start(bf16[136,512]{1,0:T(8,128)(2,1)S(1)} %get-tuple-element.45), channel_id=1, source_target_pairs={{0,1},{1,2},{2,3},{3,0},{4,5},{5,6},{6,7},{7,4},{8,9},{9,10},{10,1... | collective-permute-start | bytes 417800 | tf_op jit(solution)/shard_map/ppermute | solution.py:454
  77.0 9.9 %collective-permute-start.21 = (bf16[136,512]{1,0:T(8,128)(2,1)S(1)}, bf16[136,512]{1,0:T(8,128)(2,1)S(1)}, u32[]{:S(2)}, u32[]{:S(2)}) collective-permute-start(bf16[136,512]{1,0:T(8,128)(2,1)S(1)} %get-tuple-element.46), channel_id=1, source_target_pairs={{0,2},{1,3},{2,0},{3,1},{4,6},{5,7},{6,4},{7,5},{8,10},{9,11},{10,... | collective-permute-start | bytes 417800 | tf_op jit(solution)/shard_map/ppermute | solution.py:454
  77.8 9.1 %collective-permute-start.22 = (bf16[136,512]{1,0:T(8,128)(2,1)S(1)}, bf16[136,512]{1,0:T(8,128)(2,1)S(1)}, u32[]{:S(2)}, u32[]{:S(2)}) collective-permute-start(bf16[136,512]{1,0:T(8,128)(2,1)S(1)} %get-tuple-element.47), channel_id=1, source_target_pairs={{0,3},{1,0},{2,1},{3,2},{4,7},{5,4},{6,5},{7,6},{8,11},{9,8},{10,9... | collective-permute-start | bytes 417800 | tf_op jit(solution)/shard_map/ppermute | solution.py:454
  83.1 10.4 %collective-permute-start.11 = (bf16[128,512]{1,0:T(8,128)(2,1)S(1)}, bf16[128,512]{1,0:T(8,128)(2,1)S(1)}, u32[]{:S(2)}, u32[]{:S(2)}) collective-permute-start(bf16[128,512]{1,0:T(8,128)(2,1)S(1)} %finish.2), channel_id=1, source_target_pairs={{0,16},{8,24},{1,17},{9,25},{2,18},{10,26},{3,19},{11,27},{4,20},{... | collective-permute-start | bytes 393224 | tf_op jit(solution)/shard_map/ppermute | solution.py:457
  87.1 7.8 %collective-permute-start.23 = (bf16[128,512]{1,0:T(8,128)(2,1)S(1)}, bf16[128,512]{1,0:T(8,128)(2,1)S(1)}, u32[]{:S(2)}, u32[]{:S(2)}) collective-permute-start(bf16[128,512]{1,0:T(8,128)(2,1)S(1)} %finish.3), channel_id=1, source_target_pairs={{0,16},{8,24},{1,17},{9,25},{2,18},{10,26},{3,19},{11,27},{4,20},{... | collective-permute-start | bytes 393224 | tf_op jit(solution)/shard_map/ppermute | solution.py:457

commit v4 on v3

--- a/solution.py
+++ b/solution.py
@@ -196,16 +196,19 @@
     )
 
 
+def deal_index(stream, c, k, dp_count):
+    return (c if stream == 0 else 1 - c) * dp_count + k
+
+
 def encode_kernel(dp_count, meta, dest, limits, *refs):
     group, dp, mp = meta[0], meta[1], meta[2]
     targets = 2 * dp_count
-    inputs, messages, scratch = refs[:4], refs[4 : 4 + 2 * targets], refs[4 + 2 * targets :]
+    inputs, outs, scratch = refs[:4], refs[4 : 4 + targets], refs[4 + targets :]
     routes, lives, *places, sems = scratch
     for stream in range(2):
         states, gain = places[2 * stream : 2 * stream + 2]
-        outs = messages[stream * targets : (stream + 1) * targets]
         share = states.shape[1] // BLOCKS
-        half = outs[0].shape[1]
+        half = states.shape[2] // dp_count
 
         @pl.when(group == stream)
         def _():
@@ -240,20 +243,20 @@
                 c, home = target // dp_count, target % dp_count
                 for k in range(dp_count):
                     place = 0 if home == k else 1
-                    outs[c * dp_count + k][place * share : (place + 1) * share, :] = normed[
-                        :, k * half : (k + 1) * half
-                    ]
+                    outs[deal_index(stream, c, k, dp_count)][
+                        place * share : (place + 1) * share, :half
+                    ] = normed[:, k * half : (k + 1) * half]
 
 
 def encode(dp_count, meta, dest, limits, streams):
-    arguments, shapes = [], []
+    arguments = []
     scratch = [pltpu.SMEM(dest.shape, jnp.int32), pltpu.SMEM(limits.shape, jnp.int32)]
     for states, gain, _ in streams:
-        _, rows, width = states.shape
         arguments += [states, gain]
         scratch += [pltpu.VMEM(states.shape, states.dtype), pltpu.VMEM(gain.shape, gain.dtype)]
-        shape = jax.ShapeDtypeStruct((2 * rows // BLOCKS, width // dp_count), jnp.bfloat16)
-        shapes += [shape] * (2 * dp_count)
+    rows = streams[0][0].shape[1]
+    half = max(states.shape[2] for states, _, _ in streams) // dp_count
+    shapes = [jax.ShapeDtypeStruct((2 * rows // BLOCKS, half), jnp.bfloat16)] * (2 * dp_count)
     return pl.pallas_call(
         functools.partial(encode_kernel, dp_count),
         out_shape=shapes,
@@ -395,6 +398,69 @@
     )(own, *parts)
 
 
+def place_early_kernel(meta, kept0, kept1, moved0, out, zeros, sems):
+    rows = kept0.shape[0]
+    at = lambda place: out.at[pl.ds(place * rows, rows)]
+
+    @pl.when(meta[0] >= 2)
+    def _():
+        copies = [
+            pltpu.make_async_copy(source, at(place), sems.at[place])
+            for source, place in ((moved0, 0), (kept0, 1), (kept1, 3))
+        ]
+        for copy in copies:
+            copy.start()
+        for copy in copies:
+            copy.wait()
+
+    @pl.when(meta[0] < 2)
+    def _():
+        zeros[...] = jnp.zeros_like(zeros)
+        copies = [
+            pltpu.make_async_copy(zeros, at(place), sems.at[place]) for place in range(BLOCKS)
+        ]
+        for copy in copies:
+            copy.start()
+        for copy in copies:
+            copy.wait()
+
+
+def place_early(meta, kept, moved):
+    rows, width = moved.shape
+    return pl.pallas_call(
+        place_early_kernel,
+        out_shape=pltpu.HBM((BLOCKS * rows, width), moved.dtype),
+        in_specs=[smem()] + [pl.BlockSpec(memory_space=pl.ANY)] * 3,
+        out_specs=hbm(),
+        scratch_shapes=[pltpu.VMEM((rows, width), moved.dtype), pltpu.SemaphoreType.DMA((BLOCKS,))],
+        name="place",
+        **limits_of(4, 1 << 26),
+    )(meta, *kept, moved)
+
+
+def place_late_kernel(meta, moved1, before, out, sem):
+    rows = moved1.shape[0]
+
+    @pl.when(meta[0] >= 2)
+    def _():
+        copy = pltpu.make_async_copy(moved1, out.at[pl.ds(2 * rows, rows)], sem)
+        copy.start()
+        copy.wait()
+
+
+def place_late(meta, moved, rows_out):
+    return pl.pallas_call(
+        place_late_kernel,
+        out_shape=pltpu.HBM(rows_out.shape, rows_out.dtype),
+        in_specs=[smem(), pl.BlockSpec(memory_space=pl.ANY), hbm()],
+        out_specs=hbm(),
+        scratch_shapes=[pltpu.SemaphoreType.DMA],
+        input_output_aliases={2: 0},
+        name="place",
+        **limits_of(4, 1 << 26),
+    )(meta, moved, rows_out)
+
+
 def shards_direct(
     audio_states,
     image_states,
@@ -417,7 +483,6 @@
     swap = [(i, (i + 1) % dp_count) for i in range(dp_count)]
     up = [(0, 2), (1, 3)]
     on_backbone = group >= 2
-    mine = lax.rem(group, 2) * dp_count + dp
     full_width = input_gain.shape[0] * mp_count
     targets = 2 * dp_count
     streams = (
@@ -426,14 +491,18 @@
     )
 
     messages = encode(dp_count, meta, destination, block_rows, streams)
+    dealt = []
+    for index in range(targets):
+        c, k = index // dp_count, index % dp_count
+        pairs = [(d, (2 * d + c) * dp_count + k) for d in range(dp_count)]
+        pairs += [(dp_count + d, (2 * d + 1 - c) * dp_count + k) for d in range(dp_count)]
+        dealt.append(lax.ppermute(messages[index], ("group", "dp"), pairs))
     gathered = []
-    for stream in range(2):
-        piece = None
-        for index in range(targets):
-            c, k = index // dp_count, index % dp_count
-            pairs = [(stream * dp_count + d, (2 * d + c) * dp_count + k) for d in range(dp_count)]
-            moved = lax.ppermute(messages[stream * targets + index], ("group", "dp"), pairs)
-            piece = moved if piece is None else jnp.where(mine == index, moved, piece)
+    for stream, (_, _, proj) in enumerate(streams):
+        mine = deal_index(stream, lax.rem(group, 2), dp, dp_count)
+        piece = dealt[0][:, : proj.shape[0]]
+        for index in range(1, targets):
+            piece = jnp.where(mine == index, dealt[index][:, : proj.shape[0]], piece)
         pieces = [piece]
         for shift in range(1, mp_count):
             pieces.append(lax.ppermute(piece, "mp", rings[shift]))
@@ -444,7 +513,7 @@
         proj, *heads_weight = fetch(wanted, (4,) * len(wanted))
         partial.append(project_rows(mp_count, meta, gathered[stream], proj, 512))
         others.append(lax.ppermute(partial[stream][1], "dp", swap))
-    row_parts, head_parts = [], []
+    kept, moved, head_parts = [], [], []
     for stream in range(2):
         tokens, own, *sends = heads(
             mp_count, meta, partial[stream][0], others[stream], input_gain, heads_weight[0]
@@ -452,11 +521,12 @@
         sums = []
         for shift, part in enumerate(sends, 1):
             sums.append(lax.ppermute(part, "mp", rings[shift]))
-        row_parts += [lax.ppermute(tokens, "group", up), tokens]
+        kept.append(tokens)
+        moved.append(lax.ppermute(tokens, "group", up))
         values = finish(full_width, own, sums)
         head_parts += [lax.ppermute(values, "group", up), values]
-    rows_out = jnp.concatenate(row_parts, axis=0)
-    rows_out = jnp.where(on_backbone, rows_out, jnp.zeros_like(rows_out))
+    rows_out = place_early(meta, kept, moved[0])
+    rows_out = place_late(meta, moved[1], rows_out)
     heads_out = jnp.concatenate(head_parts, axis=0)
     heads_out = jnp.where(on_backbone, heads_out, jnp.zeros_like(heads_out))
     return (heads_out[None], rows_out[None])

time: 97.9 us -> 103 us (1.052)
  waiting for transfers between devices: 36.7 us -> 39.9 us
  Pallas kernels: 17.4 us -> 19.9 us
  other arithmetic: 2.77 us -> 1.02 us
  starting transfers between devices: 39.8 us -> 41.3 us
    ppermute x10 -> x6, waiting for transfers between devices: 1.29 us -> 5.57 us  [the longest x4 5.56 us: shards_direct(): dealt.append(lax.ppermute(messages[index], ('group', 'dp'), pairs))]
    pallas_call x0 -> x2, Pallas kernels: none -> 2.49 us  [the longest x1 1.93 us: place_early(): pl.pallas_call(place_early_kernel, out_shape=pltpu.HBM((BLOCKS * rows, wi...]
    ppermute x10 -> x6, starting transfers between devices: 15.1 us -> 17.4 us  [the longest x4 8.88 us: shards_direct(): dealt.append(lax.ppermute(messages[index], ('group', 'dp'), pairs))]
    ppermute x2, waiting for transfers between devices: 11.9 us -> 9.98 us  [shards_direct(): others.append(lax.ppermute(partial[stream][1], 'dp', swap))]
    select_n x3 -> x2, other arithmetic: 1.82 us -> 0.07 us  [shards_direct(): piece = jnp.where(mine == index, dealt[index][:, :proj.shape[0]], piece)]
    ppermute x6, starting transfers between devices: 10.2 us -> 8.92 us  [shards_direct(): pieces.append(lax.ppermute(piece, 'mp', rings[shift]))]
  transfers between devices with their start and end apart: 26 -> 22, of which waited for: 9 -> 8; matrix products, arithmetic and copies ran while one was open for 1% -> 1% of each run, Pallas kernels for 16% -> 17%
where the time goes in v4:
time: 103 us
  starting transfers between devices  41.3 us (40%)
  waiting for transfers between devices  39.9 us (39%)
  Pallas kernels  19.9 us (19%)
    ppermute x6, waiting for transfers between devices, shards_direct(): pieces.append(lax.ppermute(piece, 'mp', rings[shift]))  12.1 us
    ppermute x2, waiting for transfers between devices, shards_direct(): others.append(lax.ppermute(partial[stream][1], 'dp', swap))  9.98 us
    ppermute x6, starting transfers between devices, shards_direct(): sums.append(lax.ppermute(part, 'mp', rings[shift]))  9.44 us
    ppermute x6, starting transfers between devices, shards_direct(): pieces.append(lax.ppermute(piece, 'mp', rings[shift]))  8.92 us
    ppermute x4, starting transfers between devices, shards_direct(): dealt.append(lax.ppermute(messages[index], ('group', 'dp'), pairs))  8.88 us
    ppermute x2, starting transfers between devices, shards_direct(): moved.append(lax.ppermute(tokens, 'group', up))  8.53 us
    pallas_call x2, Pallas kernels, fetch(): pl.pallas_call(functools.partial(fetch_kernel, cuts), out_shape=[pltpu.VM...  7.13 us
    ppermute x2, waiting for transfers between devices, shards_direct(): head_parts += [lax.ppermute(values, 'group', up), values]  6.23 us
  transfers between devices with their start and end apart: 22, of which 8 were waited for; matrix products, arithmetic and copies ran while one was open for 1% of the time, Pallas kernels for 17%

profile of v4, /device:TPU:0, one launch (start us, length us, event | category | flops | bytes accessed | tf_op | source)
XLA Modules:
  0.0 102.9 jit_solution(18063083345160787684)
XLA Ops:
  0.6 0.1 pad_add_fusion.meta
  0.7 1.8 %encode.1 = (bf16[64,1600]{1,0:T(8,128)(2,1)S(1)}, bf16[64,1600]{1,0:T(8,128)(2,1)S(1)}, bf16[64,1600]{1,0:T(8,128)(2,1)S(1)}, bf16[64,1600]{1,0:T(8,128)(2,1)S(1)}) custom-call(s32[3]{0:T(128)S(1)} %pad_add_fusion.meta, s32[2,2,4]{2,1,0:T(2,128)} %dest.1, s32[2,2,4]{2,1,0:T(2,128)} %limits.1, bf16[1,128,1280]{2,1,0:T(8,128)(2,1)} %refs_0_.3, f32[1280]{0:T(1024)} %refs_1_.2, ...), custom_call_target="tpu_custom_call" | custom-call | flops 268435456 | tf_op jit(solution)/shard_map/encode/pallas_call | solution.py:260
  2.6 4.8 %collective-permute-start = (bf16[64,1600]{1,0:T(8,128)(2,1)S(1)}, bf16[64,1600]{1,0:T(8,128)(2,1)S(1)}, u32[]{:S(2)}, u32[]{:S(2)}) collective-permute-start(bf16[64,1600]{1,0:T(8,128)(2,1)S(1)} %get-tuple-element.22), channel_id=1, source_target_pairs={{0,12},{4,28},{8,4},{12,20},{1,13},{5,29},{9,5},{13,21},{2,14},{6,... | collective-permute-start | bytes 614408 | tf_op jit(solution)/shard_map/ppermute | solution.py:499
  7.4 2.1 %collective-permute-start.1 = (bf16[64,1600]{1,0:T(8,128)(2,1)S(1)}, bf16[64,1600]{1,0:T(8,128)(2,1)S(1)}, u32[]{:S(2)}, u32[]{:S(2)}) collective-permute-start(bf16[64,1600]{1,0:T(8,128)(2,1)S(1)} %get-tuple-element.23), channel_id=1, source_target_pairs={{0,8},{4,24},{8,0},{12,16},{1,9},{5,25},{9,1},{13,17},{2,10},{6,26... | collective-permute-start | bytes 614408 | tf_op jit(solution)/shard_map/ppermute | solution.py:499
  9.5 1.3 %collective-permute-start.2 = (bf16[64,1600]{1,0:T(8,128)(2,1)S(1)}, bf16[64,1600]{1,0:T(8,128)(2,1)S(1)}, u32[]{:S(2)}, u32[]{:S(2)}) collective-permute-start(bf16[64,1600]{1,0:T(8,128)(2,1)S(1)} %get-tuple-element.24), channel_id=1, source_target_pairs={{0,4},{4,20},{8,12},{12,28},{1,5},{5,21},{9,13},{13,29},{2,6},{6,2... | collective-permute-start | bytes 614408 | tf_op jit(solution)/shard_map/ppermute | solution.py:499
  10.8 0.7 collective-permute-start.3
  11.5 1.5 %collective-permute-done = bf16[64,1600]{1,0:T(8,128)(2,1)S(1)} collective-permute-done((bf16[64,1600]{1,0:T(8,128)(2,1)S(1)}, bf16[64,1600]{1,0:T(8,128)(2,1)S(1)}, u32[]{:S(2)}, u32[]{:S(2)}) %collective-permute-start) | collective-permute-done | bytes 204832 | tf_op jit(solution)/shard_map/ppermute | solution.py:499
  13.0 0.0 collective-permute-done.1
  13.0 4.0 %collective-permute-done.2 = bf16[64,1600]{1,0:T(8,128)(2,1)S(1)} collective-permute-done((bf16[64,1600]{1,0:T(8,128)(2,1)S(1)}, bf16[64,1600]{1,0:T(8,128)(2,1)S(1)}, u32[]{:S(2)}, u32[]{:S(2)}) %collective-permute-start.2) | collective-permute-done | bytes 204832 | tf_op jit(solution)/shard_map/ppermute | solution.py:499
  17.1 1.6 %collective-permute-start.4 = (bf16[64,640]{1,0:T(8,128)(2,1)S(1)}, bf16[64,640]{1,0:T(8,128)(2,1)S(1)}, u32[]{:S(2)}, u32[]{:S(2)}) collective-permute-start(bf16[64,640]{1,0:T(8,128)(2,1)S(1)} %fusion.1.refs_0_), channel_id=1, source_target_pairs={{0,1},{1,2},{2,3},{3,0},{4,5},{5,6},{6,7},{7,4},{8,9},{9,10},{10,1... | collective-permute-start | bytes 245768 | tf_op jit(solution)/shard_map/ppermute | solution.py:508
  18.8 1.6 %collective-permute-start.12 = (bf16[64,1600]{1,0:T(8,128)(2,1)S(1)}, bf16[64,1600]{1,0:T(8,128)(2,1)S(1)}, u32[]{:S(2)}, u32[]{:S(2)}) collective-permute-start(bf16[64,1600]{1,0:T(8,128)(2,1)S(1)} %select_select_fusion.refs_0_), channel_id=1, source_target_pairs={{0,1},{1,2},{2,3},{3,0},{4,5},{5,6},{6,7},{7,4},{8,9},{9,10},{10,1... | collective-permute-start | bytes 614408 | tf_op jit(solution)/shard_map/ppermute | solution.py:508
  20.4 1.2 %collective-permute-start.13 = (bf16[64,1600]{1,0:T(8,128)(2,1)S(1)}, bf16[64,1600]{1,0:T(8,128)(2,1)S(1)}, u32[]{:S(2)}, u32[]{:S(2)}) collective-permute-start(bf16[64,1600]{1,0:T(8,128)(2,1)S(1)} %select_select_fusion.refs_0_), channel_id=1, source_target_pairs={{0,2},{1,3},{2,0},{3,1},{4,6},{5,7},{6,4},{7,5},{8,10},{9,11},{10,... | collective-permute-start | bytes 614408 | tf_op jit(solution)/shard_map/ppermute | solution.py:508
  21.6 2.7 %collective-permute-start.14 = (bf16[64,1600]{1,0:T(8,128)(2,1)S(1)}, bf16[64,1600]{1,0:T(8,128)(2,1)S(1)}, u32[]{:S(2)}, u32[]{:S(2)}) collective-permute-start(bf16[64,1600]{1,0:T(8,128)(2,1)S(1)} %select_select_fusion.refs_0_), channel_id=1, source_target_pairs={{0,3},{1,0},{2,1},{3,2},{4,7},{5,4},{6,5},{7,6},{8,11},{9,8},{10,9... | collective-permute-start | bytes 614408 | tf_op jit(solution)/shard_map/ppermute | solution.py:508
  24.3 0.3 collective-permute-start.5
  24.7 0.0 collective-permute-done.4.refs_1_
  24.7 1.4 %collective-permute-start.6 = (bf16[64,640]{1,0:T(8,128)(2,1)S(1)}, bf16[64,640]{1,0:T(8,128)(2,1)S(1)}, u32[]{:S(2)}, u32[]{:S(2)}) collective-permute-start(bf16[64,640]{1,0:T(8,128)(2,1)S(1)} %fusion.1.refs_0_), channel_id=1, source_target_pairs={{0,3},{1,0},{2,1},{3,2},{4,7},{5,4},{6,5},{7,6},{8,11},{9,8},{10,9... | collective-permute-start | bytes 245768 | tf_op jit(solution)/shard_map/ppermute | solution.py:508
  26.1 1.7 %fetch.2.refs_4_ = bf16[640,2048]{1,0:T(8,128)(2,1)S(1)} custom-call(bf16[640,2048]{1,0:T(8,128)(2,1)} %refs_0_.4), custom_call_target="tpu_custom_call" | custom-call | flops 268435456 | tf_op jit(solution)/shard_map/fetch/pallas_call | solution.py:289
  27.8 5.4 %fetch.3 = (bf16[1600,2048]{1,0:T(8,128)(2,1)S(1)}, bf16[2048,2048]{1,0:T(8,128)(2,1)S(1)}) custom-call(bf16[1600,2048]{1,0:T(8,128)(2,1)} %refs_0_.5, bf16[2048,2048]{1,0:T(8,128)(2,1)} %refs_1_.3), custom_call_target="tpu_custom_call" | custom-call | flops 268435456 | tf_op jit(solution)/shard_map/fetch/pallas_call | solution.py:289
  33.2 0.0 copy-start
  33.2 12.1 %collective-permute-done.5.refs_2_ = bf16[64,640]{1,0:T(8,128)(2,1)S(1)} collective-permute-done((bf16[64,640]{1,0:T(8,128)(2,1)S(1)}, bf16[64,640]{1,0:T(8,128)(2,1)S(1)}, u32[]{:S(2)}, u32[]{:S(2)}) %collective-permute-start.5) | collective-permute-done | bytes 81952 | tf_op jit(solution)/shard_map/ppermute | solution.py:508
  45.3 0.0 collective-permute-done.6.refs_3_
  45.3 1.5 %project.2 = (f32[128,2048]{1,0:T(8,128)S(1)}, bf16[128,2048]{1,0:T(8,128)(2,1)S(1)}) custom-call(s32[3]{0:T(128)S(1)} %pad_add_fusion.meta, bf16[64,640]{1,0:T(8,128)(2,1)S(1)} %fusion.1.refs_0_, bf16[64,640]{1,0:T(8,128)(2,1)S(1)} %collective-permute-done.4.refs_1_, bf16[64,640]{1,0:T(8,128)(2,1)S(1)} %collective-permute-done.5.refs_2_, ...), custom_call_target="tpu_custom_call" | custom-call | flops 671088640 | tf_op jit(solution)/shard_map/project/pallas_call | solution.py:320
  46.9 2.5 %collective-permute-start.7 = (bf16[128,2048]{1,0:T(8,128)(2,1)S(1)}, bf16[128,2048]{1,0:T(8,128)(2,1)S(1)}, u32[]{:S(2)}, u32[]{:S(2)}) collective-permute-start(bf16[128,2048]{1,0:T(8,128)(2,1)S(1)} %get-tuple-element.27), channel_id=1, source_target_pairs={{0,4},{4,0},{1,5},{5,1},{2,6},{6,2},{3,7},{7,3},{8,12},{12,8},{9,1... | collective-permute-start | bytes 1572872 | tf_op jit(solution)/shard_map/ppermute | solution.py:515
  49.4 0.0 collective-permute-done.12.refs_1_
  49.4 2.7 %project.3 = (f32[128,2048]{1,0:T(8,128)S(1)}, bf16[128,2048]{1,0:T(8,128)(2,1)S(1)}) custom-call(s32[3]{0:T(128)S(1)} %pad_add_fusion.meta, bf16[64,1600]{1,0:T(8,128)(2,1)S(1)} %select_select_fusion.refs_0_, bf16[64,1600]{1,0:T(8,128)(2,1)S(1)} %collective-permute-done.12.refs_1_, bf16[64,1600]{1,0:T(8,128)(2,1)S(1)} %collective-permute-done.13.refs_2_, ...), custom_call_target="tpu_custom_call" | custom-call | flops 1677721600 | tf_op jit(solution)/shard_map/project/pallas_call | solution.py:320
  52.1 0.1 collective-permute-start.15
  52.2 10.0 %collective-permute-done.7.other = bf16[128,2048]{1,0:T(8,128)(2,1)S(1)} collective-permute-done((bf16[128,2048]{1,0:T(8,128)(2,1)S(1)}, bf16[128,2048]{1,0:T(8,128)(2,1)S(1)}, u32[]{:S(2)}, u32[]{:S(2)}) %collective-permute-start.7) | collective-permute-done | bytes 524320 | tf_op jit(solution)/shard_map/ppermute | solution.py:515
  62.2 1.9 %heads.2 = (bf16[128,2048]{1,0:T(8,128)(2,1)S(1)}, f32[136,512]{1,0:T(8,128)S(1)}, bf16[136,512]{1,0:T(8,128)(2,1)S(1)}, bf16[136,512]{1,0:T(8,128)(2,1)S(1)}, bf16[136,512]{1,0:T(8,128)(2,1)S(1)}) custom-call(s32[3]{0:T(128)S(1)} %pad_add_fusion.meta, f32[128,2048]{1,0:T(8,128)S(1)} %get-tuple-element.26.keep, ...), custom_call_target="tpu_custom_call" | custom-call | flops 1073741824 | tf_op jit(solution)/shard_map/heads/pallas_call | solution.py:362
  64.1 2.2 %collective-permute-start.8 = (bf16[136,512]{1,0:T(8,128)(2,1)S(1)}, bf16[136,512]{1,0:T(8,128)(2,1)S(1)}, u32[]{:S(2)}, u32[]{:S(2)}) collective-permute-start(bf16[136,512]{1,0:T(8,128)(2,1)S(1)} %get-tuple-element.30), channel_id=1, source_target_pairs={{0,1},{1,2},{2,3},{3,0},{4,5},{5,6},{6,7},{7,4},{8,9},{9,10},{10,1... | collective-permute-start | bytes 417800 | tf_op jit(solution)/shard_map/ppermute | solution.py:523
  66.4 1.6 %collective-permute-start.9 = (bf16[136,512]{1,0:T(8,128)(2,1)S(1)}, bf16[136,512]{1,0:T(8,128)(2,1)S(1)}, u32[]{:S(2)}, u32[]{:S(2)}) collective-permute-start(bf16[136,512]{1,0:T(8,128)(2,1)S(1)} %get-tuple-element.31), channel_id=1, source_target_pairs={{0,2},{1,3},{2,0},{3,1},{4,6},{5,7},{6,4},{7,5},{8,10},{9,11},{10,... | collective-permute-start | bytes 417800 | tf_op jit(solution)/shard_map/ppermute | solution.py:523
  68.0 0.8 collective-permute-start.10
  68.8 4.9 %collective-permute-start.21 = (bf16[128,2048]{1,0:T(8,128)(2,1)S(1)}, bf16[128,2048]{1,0:T(8,128)(2,1)S(1)}, u32[]{:S(2)}, u32[]{:S(2)}) collective-permute-start(bf16[128,2048]{1,0:T(8,128)(2,1)S(1)} %get-tuple-element.41.kept0), channel_id=1, source_target_pairs={{0,16},{8,24},{1,17},{9,25},{2,18},{10,26},{3,19},{11,27},{4,20},{... | collective-permute-start | bytes 1572872 | tf_op jit(solution)/shard_map/ppermute | solution.py:525
  73.8 1.9 %heads.3 = (bf16[128,2048]{1,0:T(8,128)(2,1)S(1)}, f32[136,512]{1,0:T(8,128)S(1)}, bf16[136,512]{1,0:T(8,128)(2,1)S(1)}, bf16[136,512]{1,0:T(8,128)(2,1)S(1)}, bf16[136,512]{1,0:T(8,128)(2,1)S(1)}) custom-call(s32[3]{0:T(128)S(1)} %pad_add_fusion.meta, f32[128,2048]{1,0:T(8,128)S(1)} %get-tuple-element.34.keep, ...), custom_call_target="tpu_custom_call" | custom-call | flops 1073741824 | tf_op jit(solution)/shard_map/heads/pallas_call | solution.py:362
  75.7 3.6 %collective-permute-start.20 = (bf16[128,2048]{1,0:T(8,128)(2,1)S(1)}, bf16[128,2048]{1,0:T(8,128)(2,1)S(1)}, u32[]{:S(2)}, u32[]{:S(2)}) collective-permute-start(bf16[128,2048]{1,0:T(8,128)(2,1)S(1)} %get-tuple-element.40.kept1), channel_id=1, source_target_pairs={{0,16},{8,24},{1,17},{9,25},{2,18},{10,26},{3,19},{11,27},{4,20},{... | collective-permute-start | bytes 1572872 | tf_op jit(solution)/shard_map/ppermute | solution.py:525
  79.3 2.3 %collective-permute-start.16 = (bf16[136,512]{1,0:T(8,128)(2,1)S(1)}, bf16[136,512]{1,0:T(8,128)(2,1)S(1)}, u32[]{:S(2)}, u32[]{:S(2)}) collective-permute-start(bf16[136,512]{1,0:T(8,128)(2,1)S(1)} %get-tuple-element.37), channel_id=1, source_target_pairs={{0,1},{1,2},{2,3},{3,0},{4,5},{5,6},{6,7},{7,4},{8,9},{9,10},{10,1... | collective-permute-start | bytes 417800 | tf_op jit(solution)/shard_map/ppermute | solution.py:523
  81.6 0.9 collective-permute-start.17
  82.5 1.5 %collective-permute-start.18 = (bf16[136,512]{1,0:T(8,128)(2,1)S(1)}, bf16[136,512]{1,0:T(8,128)(2,1)S(1)}, u32[]{:S(2)}, u32[]{:S(2)}) collective-permute-start(bf16[136,512]{1,0:T(8,128)(2,1)S(1)} %get-tuple-element.39), channel_id=1, source_target_pairs={{0,3},{1,0},{2,1},{3,2},{4,7},{5,4},{6,5},{7,6},{8,11},{9,8},{10,9... | collective-permute-start | bytes 417800 | tf_op jit(solution)/shard_map/ppermute | solution.py:523
  84.1 0.2 finish.2
  84.3 3.5 %collective-permute-done.16.refs_0_ = bf16[136,512]{1,0:T(8,128)(2,1)S(1)} collective-permute-done((bf16[136,512]{1,0:T(8,128)(2,1)S(1)}, bf16[136,512]{1,0:T(8,128)(2,1)S(1)}, u32[]{:S(2)}, u32[]{:S(2)}) %collective-permute-start.16) | collective-permute-done | bytes 139296 | tf_op jit(solution)/shard_map/ppermute | solution.py:523
  87.7 1.3 %collective-permute-start.11 = (bf16[128,512]{1,0:T(8,128)(2,1)S(1)}, bf16[128,512]{1,0:T(8,128)(2,1)S(1)}, u32[]{:S(2)}, u32[]{:S(2)}) collective-permute-start(bf16[128,512]{1,0:T(8,128)(2,1)S(1)} %finish.2), channel_id=1, source_target_pairs={{0,16},{8,24},{1,17},{9,25},{2,18},{10,26},{3,19},{11,27},{4,20},{... | collective-permute-start | bytes 393224 | tf_op jit(solution)/shard_map/ppermute | solution.py:527
  89.0 2.5 %collective-permute-done.17.refs_1_ = bf16[136,512]{1,0:T(8,128)(2,1)S(1)} collective-permute-done((bf16[136,512]{1,0:T(8,128)(2,1)S(1)}, bf16[136,512]{1,0:T(8,128)(2,1)S(1)}, u32[]{:S(2)}, u32[]{:S(2)}) %collective-permute-start.17) | collective-permute-done | bytes 139296 | tf_op jit(solution)/shard_map/ppermute | solution.py:523
  91.6 0.2 finish.3
  91.8 1.5 %collective-permute-start.19 = (bf16[128,512]{1,0:T(8,128)(2,1)S(1)}, bf16[128,512]{1,0:T(8,128)(2,1)S(1)}, u32[]{:S(2)}, u32[]{:S(2)}) collective-permute-start(bf16[128,512]{1,0:T(8,128)(2,1)S(1)} %finish.3), channel_id=1, source_target_pairs={{0,16},{8,24},{1,17},{9,25},{2,18},{10,26},{3,19},{11,27},{4,20},{... | collective-permute-start | bytes 393224 | tf_op jit(solution)/shard_map/ppermute | solution.py:527
  93.3 4.8 %collective-permute-done.11 = bf16[128,512]{1,0:T(8,128)(2,1)S(1)} collective-permute-done((bf16[128,512]{1,0:T(8,128)(2,1)S(1)}, bf16[128,512]{1,0:T(8,128)(2,1)S(1)}, u32[]{:S(2)}, u32[]{:S(2)}) %collective-permute-start.11) | collective-permute-done | bytes 131104 | tf_op jit(solution)/shard_map/ppermute | solution.py:527
  98.1 1.4 %collective-permute-done.19 = bf16[128,512]{1,0:T(8,128)(2,1)S(1)} collective-permute-done((bf16[128,512]{1,0:T(8,128)(2,1)S(1)}, bf16[128,512]{1,0:T(8,128)(2,1)S(1)}, u32[]{:S(2)}, u32[]{:S(2)}) %collective-permute-start.19) | collective-permute-done | bytes 131104 | tf_op jit(solution)/shard_map/ppermute | solution.py:527
  99.5 0.9 maximum_select_fusion
  100.4 1.9 %place.2.before = bf16[512,2048]{1,0:T(8,128)(2,1)} custom-call(s32[3]{0:T(128)S(1)} %pad_add_fusion.meta, bf16[128,2048]{1,0:T(8,128)(2,1)S(1)} %get-tuple-element.41.kept0, bf16[128,2048]{1,0:T(8,128)(2,1)S(1)} %get-tuple-element.40.kept1, bf16[128,2048]{1,0:T(8,128)(2,1)S(1)} %collective-permute-done.21.moved0), custom_call_target="tpu_custom_call" | custom-call | flops 67108864 | tf_op jit(solution)/shard_map/place/pallas_call | solution.py:430
  102.4 0.6 place.3
  (13 shorter events, 0.1 us)
Async XLA Ops:
  2.6 10.5 %collective-permute-start = (bf16[64,1600]{1,0:T(8,128)(2,1)S(1)}, bf16[64,1600]{1,0:T(8,128)(2,1)S(1)}, u32[]{:S(2)}, u32[]{:S(2)}) collective-permute-start(bf16[64,1600]{1,0:T(8,128)(2,1)S(1)} %get-tuple-element.22), channel_id=1, source_target_pairs={{0,12},{4,28},{8,4},{12,20},{1,13},{5,29},{9,5},{13,21},{2,14},{6,... | collective-permute-start | bytes 614408 | tf_op jit(solution)/shard_map/ppermute | solution.py:499
  7.4 5.6 %collective-permute-start.1 = (bf16[64,1600]{1,0:T(8,128)(2,1)S(1)}, bf16[64,1600]{1,0:T(8,128)(2,1)S(1)}, u32[]{:S(2)}, u32[]{:S(2)}) collective-permute-start(bf16[64,1600]{1,0:T(8,128)(2,1)S(1)} %get-tuple-element.23), channel_id=1, source_target_pairs={{0,8},{4,24},{8,0},{12,16},{1,9},{5,25},{9,1},{13,17},{2,10},{6,26... | collective-permute-start | bytes 614408 | tf_op jit(solution)/shard_map/ppermute | solution.py:499
  9.5 7.6 %collective-permute-start.2 = (bf16[64,1600]{1,0:T(8,128)(2,1)S(1)}, bf16[64,1600]{1,0:T(8,128)(2,1)S(1)}, u32[]{:S(2)}, u32[]{:S(2)}) collective-permute-start(bf16[64,1600]{1,0:T(8,128)(2,1)S(1)} %get-tuple-element.24), channel_id=1, source_target_pairs={{0,4},{4,20},{8,12},{12,28},{1,5},{5,21},{9,13},{13,29},{2,6},{6,2... | collective-permute-start | bytes 614408 | tf_op jit(solution)/shard_map/ppermute | solution.py:499
  10.8 6.3 %collective-permute-start.3 = (bf16[64,1600]{1,0:T(8,128)(2,1)S(1)}, bf16[64,1600]{1,0:T(8,128)(2,1)S(1)}, u32[]{:S(2)}, u32[]{:S(2)}) collective-permute-start(bf16[64,1600]{1,0:T(8,128)(2,1)S(1)} %get-tuple-element.25), channel_id=1, source_target_pairs={{0,0},{4,16},{8,8},{12,24},{1,1},{5,17},{9,9},{13,25},{2,2},{6,18}... | collective-permute-start | bytes 614408 | tf_op jit(solution)/shard_map/ppermute | solution.py:499
  17.1 7.6 %collective-permute-start.4 = (bf16[64,640]{1,0:T(8,128)(2,1)S(1)}, bf16[64,640]{1,0:T(8,128)(2,1)S(1)}, u32[]{:S(2)}, u32[]{:S(2)}) collective-permute-start(bf16[64,640]{1,0:T(8,128)(2,1)S(1)} %fusion.1.refs_0_), channel_id=1, source_target_pairs={{0,1},{1,2},{2,3},{3,0},{4,5},{5,6},{6,7},{7,4},{8,9},{9,10},{10,1... | collective-permute-start | bytes 245768 | tf_op jit(solution)/shard_map/ppermute | solution.py:508
  18.8 30.7 %collective-permute-start.12 = (bf16[64,1600]{1,0:T(8,128)(2,1)S(1)}, bf16[64,1600]{1,0:T(8,128)(2,1)S(1)}, u32[]{:S(2)}, u32[]{:S(2)}) collective-permute-start(bf16[64,1600]{1,0:T(8,128)(2,1)S(1)} %select_select_fusion.refs_0_), channel_id=1, source_target_pairs={{0,1},{1,2},{2,3},{3,0},{4,5},{5,6},{6,7},{7,4},{8,9},{9,10},{10,1... | collective-permute-start | bytes 614408 | tf_op jit(solution)/shard_map/ppermute | solution.py:508
  20.4 29.0 %collective-permute-start.13 = (bf16[64,1600]{1,0:T(8,128)(2,1)S(1)}, bf16[64,1600]{1,0:T(8,128)(2,1)S(1)}, u32[]{:S(2)}, u32[]{:S(2)}) collective-permute-start(bf16[64,1600]{1,0:T(8,128)(2,1)S(1)} %select_select_fusion.refs_0_), channel_id=1, source_target_pairs={{0,2},{1,3},{2,0},{3,1},{4,6},{5,7},{6,4},{7,5},{8,10},{9,11},{10,... | collective-permute-start | bytes 614408 | tf_op jit(solution)/shard_map/ppermute | solution.py:508
  21.6 27.8 %collective-permute-start.14 = (bf16[64,1600]{1,0:T(8,128)(2,1)S(1)}, bf16[64,1600]{1,0:T(8,128)(2,1)S(1)}, u32[]{:S(2)}, u32[]{:S(2)}) collective-permute-start(bf16[64,1600]{1,0:T(8,128)(2,1)S(1)} %select_select_fusion.refs_0_), channel_id=1, source_target_pairs={{0,3},{1,0},{2,1},{3,2},{4,7},{5,4},{6,5},{7,6},{8,11},{9,8},{10,9... | collective-permute-start | bytes 614408 | tf_op jit(solution)/shard_map/ppermute | solution.py:508
  24.3 21.0 %collective-permute-start.5 = (bf16[64,640]{1,0:T(8,128)(2,1)S(1)}, bf16[64,640]{1,0:T(8,128)(2,1)S(1)}, u32[]{:S(2)}, u32[]{:S(2)}) collective-permute-start(bf16[64,640]{1,0:T(8,128)(2,1)S(1)} %fusion.1.refs_0_), channel_id=1, source_target_pairs={{0,2},{1,3},{2,0},{3,1},{4,6},{5,7},{6,4},{7,5},{8,10},{9,11},{10,... | collective-permute-start | bytes 245768 | tf_op jit(solution)/shard_map/ppermute | solution.py:508
  24.7 20.7 %collective-permute-start.6 = (bf16[64,640]{1,0:T(8,128)(2,1)S(1)}, bf16[64,640]{1,0:T(8,128)(2,1)S(1)}, u32[]{:S(2)}, u32[]{:S(2)}) collective-permute-start(bf16[64,640]{1,0:T(8,128)(2,1)S(1)} %fusion.1.refs_0_), channel_id=1, source_target_pairs={{0,3},{1,0},{2,1},{3,2},{4,7},{5,4},{6,5},{7,6},{8,11},{9,8},{10,9... | collective-permute-start | bytes 245768 | tf_op jit(solution)/shard_map/ppermute | solution.py:508
  33.2 29.0 %copy-start = (f32[2048]{0:T(1024)S(1)}, f32[2048]{0:T(1024)}, u32[]{:S(2)}) copy-start(f32[2048]{0:T(1024)} %gain.3) | copy-start | bytes 24580
  46.9 15.3 %collective-permute-start.7 = (bf16[128,2048]{1,0:T(8,128)(2,1)S(1)}, bf16[128,2048]{1,0:T(8,128)(2,1)S(1)}, u32[]{:S(2)}, u32[]{:S(2)}) collective-permute-start(bf16[128,2048]{1,0:T(8,128)(2,1)S(1)} %get-tuple-element.27), channel_id=1, source_target_pairs={{0,4},{4,0},{1,5},{5,1},{2,6},{6,2},{3,7},{7,3},{8,12},{12,8},{9,1... | collective-permute-start | bytes 1572872 | tf_op jit(solution)/shard_map/ppermute | solution.py:515
  52.1 21.6 %collective-permute-start.15 = (bf16[128,2048]{1,0:T(8,128)(2,1)S(1)}, bf16[128,2048]{1,0:T(8,128)(2,1)S(1)}, u32[]{:S(2)}, u32[]{:S(2)}) collective-permute-start(bf16[128,2048]{1,0:T(8,128)(2,1)S(1)} %get-tuple-element.35), channel_id=1, source_target_pairs={{0,4},{4,0},{1,5},{5,1},{2,6},{6,2},{3,7},{7,3},{8,12},{12,8},{9,1... | collective-permute-start | bytes 1572872 | tf_op jit(solution)/shard_map/ppermute | solution.py:515
  64.1 15.1 %collective-permute-start.8 = (bf16[136,512]{1,0:T(8,128)(2,1)S(1)}, bf16[136,512]{1,0:T(8,128)(2,1)S(1)}, u32[]{:S(2)}, u32[]{:S(2)}) collective-permute-start(bf16[136,512]{1,0:T(8,128)(2,1)S(1)} %get-tuple-element.30), channel_id=1, source_target_pairs={{0,1},{1,2},{2,3},{3,0},{4,5},{5,6},{6,7},{7,4},{8,9},{9,10},{10,1... | collective-permute-start | bytes 417800 | tf_op jit(solution)/shard_map/ppermute | solution.py:523
  66.4 15.3 %collective-permute-start.9 = (bf16[136,512]{1,0:T(8,128)(2,1)S(1)}, bf16[136,512]{1,0:T(8,128)(2,1)S(1)}, u32[]{:S(2)}, u32[]{:S(2)}) collective-permute-start(bf16[136,512]{1,0:T(8,128)(2,1)S(1)} %get-tuple-element.31), channel_id=1, source_target_pairs={{0,2},{1,3},{2,0},{3,1},{4,6},{5,7},{6,4},{7,5},{8,10},{9,11},{10,... | collective-permute-start | bytes 417800 | tf_op jit(solution)/shard_map/ppermute | solution.py:523
  68.0 14.6 %collective-permute-start.10 = (bf16[136,512]{1,0:T(8,128)(2,1)S(1)}, bf16[136,512]{1,0:T(8,128)(2,1)S(1)}, u32[]{:S(2)}, u32[]{:S(2)}) collective-permute-start(bf16[136,512]{1,0:T(8,128)(2,1)S(1)} %get-tuple-element.32), channel_id=1, source_target_pairs={{0,3},{1,0},{2,1},{3,2},{4,7},{5,4},{6,5},{7,6},{8,11},{9,8},{10,9... | collective-permute-start | bytes 417800 | tf_op jit(solution)/shard_map/ppermute | solution.py:523
  68.8 31.6 %collective-permute-start.21 = (bf16[128,2048]{1,0:T(8,128)(2,1)S(1)}, bf16[128,2048]{1,0:T(8,128)(2,1)S(1)}, u32[]{:S(2)}, u32[]{:S(2)}) collective-permute-start(bf16[128,2048]{1,0:T(8,128)(2,1)S(1)} %get-tuple-element.41.kept0), channel_id=1, source_target_pairs={{0,16},{8,24},{1,17},{9,25},{2,18},{10,26},{3,19},{11,27},{4,20},{... | collective-permute-start | bytes 1572872 | tf_op jit(solution)/shard_map/ppermute | solution.py:525
  75.7 26.7 %collective-permute-start.20 = (bf16[128,2048]{1,0:T(8,128)(2,1)S(1)}, bf16[128,2048]{1,0:T(8,128)(2,1)S(1)}, u32[]{:S(2)}, u32[]{:S(2)}) collective-permute-start(bf16[128,2048]{1,0:T(8,128)(2,1)S(1)} %get-tuple-element.40.kept1), channel_id=1, source_target_pairs={{0,16},{8,24},{1,17},{9,25},{2,18},{10,26},{3,19},{11,27},{4,20},{... | collective-permute-start | bytes 1572872 | tf_op jit(solution)/shard_map/ppermute | solution.py:525
  79.3 8.4 %collective-permute-start.16 = (bf16[136,512]{1,0:T(8,128)(2,1)S(1)}, bf16[136,512]{1,0:T(8,128)(2,1)S(1)}, u32[]{:S(2)}, u32[]{:S(2)}) collective-permute-start(bf16[136,512]{1,0:T(8,128)(2,1)S(1)} %get-tuple-element.37), channel_id=1, source_target_pairs={{0,1},{1,2},{2,3},{3,0},{4,5},{5,6},{6,7},{7,4},{8,9},{9,10},{10,1... | collective-permute-start | bytes 417800 | tf_op jit(solution)/shard_map/ppermute | solution.py:523
  81.6 9.9 %collective-permute-start.17 = (bf16[136,512]{1,0:T(8,128)(2,1)S(1)}, bf16[136,512]{1,0:T(8,128)(2,1)S(1)}, u32[]{:S(2)}, u32[]{:S(2)}) collective-permute-start(bf16[136,512]{1,0:T(8,128)(2,1)S(1)} %get-tuple-element.38), channel_id=1, source_target_pairs={{0,2},{1,3},{2,0},{3,1},{4,6},{5,7},{6,4},{7,5},{8,10},{9,11},{10,... | collective-permute-start | bytes 417800 | tf_op jit(solution)/shard_map/ppermute | solution.py:523
  82.5 9.0 %collective-permute-start.18 = (bf16[136,512]{1,0:T(8,128)(2,1)S(1)}, bf16[136,512]{1,0:T(8,128)(2,1)S(1)}, u32[]{:S(2)}, u32[]{:S(2)}) collective-permute-start(bf16[136,512]{1,0:T(8,128)(2,1)S(1)} %get-tuple-element.39), channel_id=1, source_target_pairs={{0,3},{1,0},{2,1},{3,2},{4,7},{5,4},{6,5},{7,6},{8,11},{9,8},{10,9... | collective-permute-start | bytes 417800 | tf_op jit(solution)/shard_map/ppermute | solution.py:523
  87.7 10.4 %collective-permute-start.11 = (bf16[128,512]{1,0:T(8,128)(2,1)S(1)}, bf16[128,512]{1,0:T(8,128)(2,1)S(1)}, u32[]{:S(2)}, u32[]{:S(2)}) collective-permute-start(bf16[128,512]{1,0:T(8,128)(2,1)S(1)} %finish.2), channel_id=1, source_target_pairs={{0,16},{8,24},{1,17},{9,25},{2,18},{10,26},{3,19},{11,27},{4,20},{... | collective-permute-start | bytes 393224 | tf_op jit(solution)/shard_map/ppermute | solution.py:527
  91.8 7.8 %collective-permute-start.19 = (bf16[128,512]{1,0:T(8,128)(2,1)S(1)}, bf16[128,512]{1,0:T(8,128)(2,1)S(1)}, u32[]{:S(2)}, u32[]{:S(2)}) collective-permute-start(bf16[128,512]{1,0:T(8,128)(2,1)S(1)} %finish.3), channel_id=1, source_target_pairs={{0,16},{8,24},{1,17},{9,25},{2,18},{10,26},{3,19},{11,27},{4,20},{... | collective-permute-start | bytes 393224 | tf_op jit(solution)/shard_map/ppermute | solution.py:527

commit v5 on v4

--- a/solution.py
+++ b/solution.py
@@ -196,19 +196,16 @@
     )
 
 
-def deal_index(stream, c, k, dp_count):
-    return (c if stream == 0 else 1 - c) * dp_count + k
-
-
 def encode_kernel(dp_count, meta, dest, limits, *refs):
     group, dp, mp = meta[0], meta[1], meta[2]
     targets = 2 * dp_count
-    inputs, outs, scratch = refs[:4], refs[4 : 4 + targets], refs[4 + targets :]
+    inputs, messages, scratch = refs[:4], refs[4 : 4 + 2 * targets], refs[4 + 2 * targets :]
     routes, lives, *places, sems = scratch
     for stream in range(2):
         states, gain = places[2 * stream : 2 * stream + 2]
         share = states.shape[1] // BLOCKS
         half = states.shape[2] // dp_count
+        outs = messages[stream * targets : (stream + 1) * targets]
 
         @pl.when(group == stream)
         def _():
@@ -243,20 +240,20 @@
                 c, home = target // dp_count, target % dp_count
                 for k in range(dp_count):
                     place = 0 if home == k else 1
-                    outs[deal_index(stream, c, k, dp_count)][
-                        place * share : (place + 1) * share, :half
-                    ] = normed[:, k * half : (k + 1) * half]
+                    outs[c * dp_count + k][place * share : (place + 1) * share, :] = normed[
+                        :, k * half : (k + 1) * half
+                    ]
 
 
 def encode(dp_count, meta, dest, limits, streams):
-    arguments = []
+    arguments, shapes = [], []
     scratch = [pltpu.SMEM(dest.shape, jnp.int32), pltpu.SMEM(limits.shape, jnp.int32)]
     for states, gain, _ in streams:
         arguments += [states, gain]
         scratch += [pltpu.VMEM(states.shape, states.dtype), pltpu.VMEM(gain.shape, gain.dtype)]
-    rows = streams[0][0].shape[1]
-    half = max(states.shape[2] for states, _, _ in streams) // dp_count
-    shapes = [jax.ShapeDtypeStruct((2 * rows // BLOCKS, half), jnp.bfloat16)] * (2 * dp_count)
+        _, rows, width = states.shape
+        shape = jax.ShapeDtypeStruct((2 * rows // BLOCKS, width // dp_count), jnp.bfloat16)
+        shapes += [shape] * (2 * dp_count)
     return pl.pallas_call(
         functools.partial(encode_kernel, dp_count),
         out_shape=shapes,
@@ -297,12 +294,46 @@
     )(*in_hbm(weights))
 
 
+def piece_source(mp, shift, mp_count):
+    if mp_count == 4:
+        return mp ^ shift
+    return lax.rem(mp + (mp_count - shift), mp_count)
+
+
+def project_half_kernel(mp_count, tile, half, meta, *refs):
+    pieces, weight, result, rows = refs[:mp_count], *refs[mp_count:]
+    share = pieces[0].shape[0] // 2
+    for shift in range(mp_count):
+        start = pl.multiple_of(piece_source(meta[2], shift, mp_count) * share, share)
+        rows[pl.ds(start, share), :] = pieces[shift][half * share : (half + 1) * share, :]
+    for first in range(0, weight.shape[1], tile):
+        out = jnp.dot(
+            rows[...], weight[:, first : first + tile], preferred_element_type=jnp.float32
+        )
+        result[:, first : first + tile] = out.astype(result.dtype)
+
+
+def project_half(mp_count, meta, pieces, weight, tile, half):
+    depth, width = weight.shape
+    rows = pieces[0].shape[0] * mp_count // 2
+    kind = jnp.bfloat16 if half else jnp.float32
+    return pl.pallas_call(
+        functools.partial(project_half_kernel, mp_count, tile, half),
+        out_shape=jax.ShapeDtypeStruct((rows, width), kind),
+        in_specs=[smem()] + [vmem()] * (mp_count + 1),
+        out_specs=vmem(),
+        scratch_shapes=[pltpu.VMEM((rows, depth), jnp.bfloat16)],
+        name="project",
+        **limits_of(12, 2 * rows * depth * width),
+    )(meta, *pieces, weight)
+
+
 def project_kernel(mp_count, tile, meta, *refs):
     pieces, weight, keep, send, rows = refs[:mp_count], *refs[mp_count:]
     share = pieces[0].shape[0] // 2
     block = share * mp_count
     for shift in range(mp_count):
-        source = lax.rem(meta[2] + (mp_count - shift), mp_count)
+        source = piece_source(meta[2], shift, mp_count)
         start = pl.multiple_of(source * share, share)
         rows[pl.ds(start, share), :] = pieces[shift][:share, :]
         rows[pl.ds(block + start, share), :] = pieces[shift][share:, :]
@@ -480,6 +511,9 @@
     mp_count = lax.axis_size("mp")
     meta = jnp.stack([group, dp, mp]).astype(jnp.int32)
     rings = [[(i, (i + shift) % mp_count) for i in range(mp_count)] for shift in range(mp_count)]
+    spreads = rings
+    if mp_count == 4:
+        spreads = [[(i, i ^ step) for i in range(mp_count)] for step in (0, 1, 2, 1)]
     swap = [(i, (i + 1) % dp_count) for i in range(dp_count)]
     up = [(0, 2), (1, 3)]
     on_backbone = group >= 2
@@ -491,32 +525,35 @@
     )
 
     messages = encode(dp_count, meta, destination, block_rows, streams)
-    dealt = []
-    for index in range(targets):
-        c, k = index // dp_count, index % dp_count
-        pairs = [(d, (2 * d + c) * dp_count + k) for d in range(dp_count)]
-        pairs += [(dp_count + d, (2 * d + 1 - c) * dp_count + k) for d in range(dp_count)]
-        dealt.append(lax.ppermute(messages[index], ("group", "dp"), pairs))
+    mine = lax.rem(group, 2) * dp_count + dp
     gathered = []
-    for stream, (_, _, proj) in enumerate(streams):
-        mine = deal_index(stream, lax.rem(group, 2), dp, dp_count)
-        piece = dealt[0][:, : proj.shape[0]]
-        for index in range(1, targets):
-            piece = jnp.where(mine == index, dealt[index][:, : proj.shape[0]], piece)
+    for stream in range(2):
+        piece = None
+        for index in range(targets):
+            c, k = index // dp_count, index % dp_count
+            pairs = [(stream * dp_count + d, (2 * d + c) * dp_count + k) for d in range(dp_count)]
+            moved = lax.ppermute(messages[stream * targets + index], ("group", "dp"), pairs)
+            piece = moved if piece is None else jnp.where(mine == index, moved, piece)
         pieces = [piece]
         for shift in range(1, mp_count):
-            pieces.append(lax.ppermute(piece, "mp", rings[shift]))
+            sent = pieces[2] if mp_count == 4 and shift == 3 else piece
+            pieces.append(lax.ppermute(sent, "mp", spreads[shift]))
         gathered.append(pieces)
     partial, others = [], []
     for stream, (_, _, proj) in enumerate(streams):
-        wanted = [proj] if stream == 0 else [proj, kv_weight]
-        proj, *heads_weight = fetch(wanted, (4,) * len(wanted))
-        partial.append(project_rows(mp_count, meta, gathered[stream], proj, 512))
-        others.append(lax.ppermute(partial[stream][1], "dp", swap))
+        (proj,) = fetch([proj], (4,))
+        if stream == 0:
+            keep, send = project_rows(mp_count, meta, gathered[stream], proj, 512)
+        else:
+            send = project_half(mp_count, meta, gathered[stream], proj, 512, 1)
+            keep = project_half(mp_count, meta, gathered[stream], proj, 512, 0)
+        partial.append((keep, send))
+        others.append(lax.ppermute(send, "dp", swap))
+    (heads_weight,) = fetch([kv_weight], (8,))
     kept, moved, head_parts = [], [], []
     for stream in range(2):
         tokens, own, *sends = heads(
-            mp_count, meta, partial[stream][0], others[stream], input_gain, heads_weight[0]
+            mp_count, meta, partial[stream][0], others[stream], input_gain, heads_weight
         )
         sums = []
         for shift, part in enumerate(sends, 1):

time: 103 us -> 88.5 us (0.86)
  the two profiles are of different devices: /device:TPU:0 before, /device:TPU:14 now
where the time goes in v5:
time: 88.5 us; the launch traced here: 88.2 us
  starting transfers between devices  35.3 us (40%)
  waiting for transfers between devices  30.1 us (34%)
  Pallas kernels  20.8 us (24%)
  other arithmetic  1.03 us (1%)
  between operations  0.94 us (1%)
    ppermute x6, starting transfers between devices, shards_direct(): sums.append(lax.ppermute(part, 'mp', rings[shift]))  11.8 us
    ppermute x6, waiting for transfers between devices, shards_direct(): pieces.append(lax.ppermute(sent, 'mp', spreads[shift]))  10.5 us
    ppermute x6, waiting for transfers between devices, shards_direct(): sums.append(lax.ppermute(part, 'mp', rings[shift]))  10.4 us
    pallas_call x3, Pallas kernels, fetch(): pl.pallas_call(functools.partial(fetch_kernel, cuts), out_shape=[pltpu.VM...  8.13 us
    ppermute x6, starting transfers between devices, shards_direct(): pieces.append(lax.ppermute(sent, 'mp', spreads[shift]))  7.48 us
    ppermute x8, starting transfers between devices, shards_direct(): lax.ppermute(messages[stream * targets + index], ('group', 'dp'), pairs)  6.59 us
    ppermute x8, waiting for transfers between devices, shards_direct(): lax.ppermute(messages[stream * targets + index], ('group', 'dp'), pairs)  4.63 us
    ppermute x2, waiting for transfers between devices, shards_direct(): head_parts += [lax.ppermute(values, 'group', up), values]  4.3 us
  transfers between devices with their start and end apart: 26, of which 13 were waited for; matrix products, arithmetic and copies ran while one was open for 1% of the time, Pallas kernels for 21%

profile of v5, /device:TPU:14, one launch (start us, length us, event | category | flops | bytes accessed | tf_op | source)
XLA Modules:
  0.0 88.2 jit_solution(3007564037299985140)
XLA Ops:
  0.7 0.6 encode.1
  1.3 0.7 collective-permute-start.12
  2.0 0.7 collective-permute-start.13
  2.7 1.3 %collective-permute-start.14 = (bf16[64,1600]{1,0:T(8,128)(2,1)S(1)}, bf16[64,1600]{1,0:T(8,128)(2,1)S(1)}, u32[]{:S(2)}, u32[]{:S(2)}) collective-permute-start(bf16[64,1600]{1,0:T(8,128)(2,1)S(1)} %get-tuple-element.34), channel_id=1, source_target_pairs={{8,4},{12,20},{9,5},{13,21},{10,6},{14,22},{11,7},{15,23}} | collective-permute-start | bytes 614408 | tf_op jit(solution)/shard_map/ppermute | solution.py:535
  4.0 0.7 collective-permute-start.15
  4.7 0.7 collective-permute-start
  5.4 0.7 collective-permute-start.1
  6.0 1.3 %collective-permute-start.2 = (bf16[64,640]{1,0:T(8,128)(2,1)S(1)}, bf16[64,640]{1,0:T(8,128)(2,1)S(1)}, u32[]{:S(2)}, u32[]{:S(2)}) collective-permute-start(bf16[64,640]{1,0:T(8,128)(2,1)S(1)} %get-tuple-element.24), channel_id=1, source_target_pairs={{0,4},{4,20},{1,5},{5,21},{2,6},{6,22},{3,7},{7,23}} | collective-permute-start | bytes 245768 | tf_op jit(solution)/shard_map/ppermute | solution.py:535
  7.3 4.6 %collective-permute-done.14 = bf16[64,1600]{1,0:T(8,128)(2,1)S(1)} collective-permute-done((bf16[64,1600]{1,0:T(8,128)(2,1)S(1)}, bf16[64,1600]{1,0:T(8,128)(2,1)S(1)}, u32[]{:S(2)}, u32[]{:S(2)}) %collective-permute-start.14) | collective-permute-done | bytes 204832 | tf_op jit(solution)/shard_map/ppermute | solution.py:535
  12.0 0.7 collective-permute-start.3
  12.7 2.7 %collective-permute-start.17 = (bf16[64,1600]{1,0:T(8,128)(2,1)S(1)}, bf16[64,1600]{1,0:T(8,128)(2,1)S(1)}, u32[]{:S(2)}, u32[]{:S(2)}) collective-permute-start(bf16[64,1600]{1,0:T(8,128)(2,1)S(1)} %select_select_fusion.refs_0_), channel_id=1, source_target_pairs={{0,2},{1,3},{2,0},{3,1},{4,6},{5,7},{6,4},{7,5},{8,10},{9,11},{10,... | collective-permute-start | bytes 614408 | tf_op jit(solution)/shard_map/ppermute | solution.py:540
  15.4 1.0 %collective-permute-start.5 = (bf16[64,640]{1,0:T(8,128)(2,1)S(1)}, bf16[64,640]{1,0:T(8,128)(2,1)S(1)}, u32[]{:S(2)}, u32[]{:S(2)}) collective-permute-start(bf16[64,640]{1,0:T(8,128)(2,1)S(1)} %select_select_fusion.1.refs_0_), channel_id=1, source_target_pairs={{0,2},{1,3},{2,0},{3,1},{4,6},{5,7},{6,4},{7,5},{8,10},{9,11},{10,... | collective-permute-start | bytes 245768 | tf_op jit(solution)/shard_map/ppermute | solution.py:540
  16.4 0.4 collective-permute-start.4
  16.8 8.8 %collective-permute-done.5.refs_2_ = bf16[64,640]{1,0:T(8,128)(2,1)S(1)} collective-permute-done((bf16[64,640]{1,0:T(8,128)(2,1)S(1)}, bf16[64,640]{1,0:T(8,128)(2,1)S(1)}, u32[]{:S(2)}, u32[]{:S(2)}) %collective-permute-start.5) | collective-permute-done | bytes 81952 | tf_op jit(solution)/shard_map/ppermute | solution.py:540
  25.7 1.4 %collective-permute-start.6 = (bf16[64,640]{1,0:T(8,128)(2,1)S(1)}, bf16[64,640]{1,0:T(8,128)(2,1)S(1)}, u32[]{:S(2)}, u32[]{:S(2)}) collective-permute-start(bf16[64,640]{1,0:T(8,128)(2,1)S(1)} %collective-permute-done.5.refs_2_), channel_id=1, source_target_pairs={{0,1},{1,0},{2,3},{3,2},{4,5},{5,4},{6,7},{7,6},{8,9},{9,8},{10,11... | collective-permute-start | bytes 245768 | tf_op jit(solution)/shard_map/ppermute | solution.py:540
  27.0 0.7 collective-permute-start.16
  27.7 1.4 %collective-permute-start.18 = (bf16[64,1600]{1,0:T(8,128)(2,1)S(1)}, bf16[64,1600]{1,0:T(8,128)(2,1)S(1)}, u32[]{:S(2)}, u32[]{:S(2)}) collective-permute-start(bf16[64,1600]{1,0:T(8,128)(2,1)S(1)} %collective-permute-done.17.refs_2_), channel_id=1, source_target_pairs={{0,1},{1,0},{2,3},{3,2},{4,5},{5,4},{6,7},{7,6},{8,9},{9,8},{10,11... | collective-permute-start | bytes 614408 | tf_op jit(solution)/shard_map/ppermute | solution.py:540
  29.1 1.7 %fetch.3.refs_4_ = bf16[640,2048]{1,0:T(8,128)(2,1)S(1)} custom-call(bf16[640,2048]{1,0:T(8,128)(2,1)} %refs_0_.5), custom_call_target="tpu_custom_call" | custom-call | flops 268435456 | tf_op jit(solution)/shard_map/fetch/pallas_call | solution.py:286
  31.0 1.5 %project.3 = (f32[128,2048]{1,0:T(8,128)S(1)}, bf16[128,2048]{1,0:T(8,128)(2,1)S(1)}) custom-call(s32[3]{0:T(128)S(1)} %pad_add_fusion.meta, bf16[64,640]{1,0:T(8,128)(2,1)S(1)} %select_select_fusion.1.refs_0_, bf16[64,640]{1,0:T(8,128)(2,1)S(1)} %collective-permute-done.4.refs_1_, bf16[64,640]{1,0:T(8,128)(2,1)S(1)} %collective-permute-done.5.refs_2_, ...), custom_call_target="tpu_custom_call" | custom-call | flops 671088640 | tf_op jit(solution)/shard_map/project/pallas_call | solution.py:351
  32.5 2.1 %collective-permute-start.7 = (bf16[128,2048]{1,0:T(8,128)(2,1)S(1)}, bf16[128,2048]{1,0:T(8,128)(2,1)S(1)}, u32[]{:S(2)}, u32[]{:S(2)}) collective-permute-start(bf16[128,2048]{1,0:T(8,128)(2,1)S(1)} %get-tuple-element.27), channel_id=1, source_target_pairs={{0,4},{4,0},{1,5},{5,1},{2,6},{6,2},{3,7},{7,3},{8,12},{12,8},{9,1... | collective-permute-start | bytes 1572872 | tf_op jit(solution)/shard_map/ppermute | solution.py:551
  34.7 2.9 %fetch.5.refs_4_ = bf16[1600,2048]{1,0:T(8,128)(2,1)S(1)} custom-call(bf16[1600,2048]{1,0:T(8,128)(2,1)} %refs_0_.7), custom_call_target="tpu_custom_call" | custom-call | flops 268435456 | tf_op jit(solution)/shard_map/fetch/pallas_call | solution.py:286
  37.6 1.5 %collective-permute-done.18.refs_3_ = bf16[64,1600]{1,0:T(8,128)(2,1)S(1)} collective-permute-done((bf16[64,1600]{1,0:T(8,128)(2,1)S(1)}, bf16[64,1600]{1,0:T(8,128)(2,1)S(1)}, u32[]{:S(2)}, u32[]{:S(2)}) %collective-permute-start.18) | collective-permute-done | bytes 204832 | tf_op jit(solution)/shard_map/ppermute | solution.py:540
  39.1 1.7 %project.5 = bf16[128,2048]{1,0:T(8,128)(2,1)S(1)} custom-call(s32[3]{0:T(128)S(1)} %pad_add_fusion.meta, bf16[64,1600]{1,0:T(8,128)(2,1)S(1)} %select_select_fusion.refs_0_, bf16[64,1600]{1,0:T(8,128)(2,1)S(1)} %collective-permute-done.16.refs_1_, bf16[64,1600]{1,0:T(8,128)(2,1)S(1)} %collective-permute-done.17.refs_2_, ...), custom_call_target="tpu_custom_call" | custom-call | flops 838860800 | tf_op jit(solution)/shard_map/project/pallas_call | solution.py:320
  40.8 2.1 %collective-permute-start.19 = (bf16[128,2048]{1,0:T(8,128)(2,1)S(1)}, bf16[128,2048]{1,0:T(8,128)(2,1)S(1)}, u32[]{:S(2)}, u32[]{:S(2)}) collective-permute-start(bf16[128,2048]{1,0:T(8,128)(2,1)S(1)} %project.5), channel_id=1, source_target_pairs={{0,4},{4,0},{1,5},{5,1},{2,6},{6,2},{3,7},{7,3},{8,12},{12,8},{9,1... | collective-permute-start | bytes 1572872 | tf_op jit(solution)/shard_map/ppermute | solution.py:551
  43.0 3.5 %fetch.4.weight = bf16[2048,2048]{1,0:T(8,128)(2,1)S(1)} custom-call(bf16[2048,2048]{1,0:T(8,128)(2,1)} %refs_0_.6), custom_call_target="tpu_custom_call" | custom-call | flops 268435456 | tf_op jit(solution)/shard_map/fetch/pallas_call | solution.py:286
  46.4 0.2 collective-permute-done.7.other
  46.7 1.9 %heads.2 = (bf16[128,2048]{1,0:T(8,128)(2,1)S(1)}, f32[136,512]{1,0:T(8,128)S(1)}, bf16[136,512]{1,0:T(8,128)(2,1)S(1)}, bf16[136,512]{1,0:T(8,128)(2,1)S(1)}, bf16[136,512]{1,0:T(8,128)(2,1)S(1)}) custom-call(s32[3]{0:T(128)S(1)} %pad_add_fusion.meta, f32[128,2048]{1,0:T(8,128)S(1)} %get-tuple-element.26.keep, ...), custom_call_target="tpu_custom_call" | custom-call | flops 1073741824 | tf_op jit(solution)/shard_map/heads/pallas_call | solution.py:393
  48.6 1.3 %collective-permute-start.25 = (bf16[128,2048]{1,0:T(8,128)(2,1)S(1)}, bf16[128,2048]{1,0:T(8,128)(2,1)S(1)}, u32[]{:S(2)}, u32[]{:S(2)}) collective-permute-start(bf16[128,2048]{1,0:T(8,128)(2,1)S(1)} %get-tuple-element.41.kept0), channel_id=1, source_target_pairs={{0,16},{8,24},{1,17},{9,25},{2,18},{10,26},{3,19},{11,27},{4,20},{... | collective-permute-start | bytes 1572872 | tf_op jit(solution)/shard_map/ppermute | solution.py:562
  49.9 1.7 %project.4.keep = f32[128,2048]{1,0:T(8,128)S(1)} custom-call(s32[3]{0:T(128)S(1)} %pad_add_fusion.meta, bf16[64,1600]{1,0:T(8,128)(2,1)S(1)} %select_select_fusion.refs_0_, bf16[64,1600]{1,0:T(8,128)(2,1)S(1)} %collective-permute-done.16.refs_1_, bf16[64,1600]{1,0:T(8,128)(2,1)S(1)} %collective-permute-done.17.refs_2_, ...), custom_call_target="tpu_custom_call" | custom-call | flops 838860800 | tf_op jit(solution)/shard_map/project/pallas_call | solution.py:320
  51.6 3.3 %collective-permute-start.8 = (bf16[136,512]{1,0:T(8,128)(2,1)S(1)}, bf16[136,512]{1,0:T(8,128)(2,1)S(1)}, u32[]{:S(2)}, u32[]{:S(2)}) collective-permute-start(bf16[136,512]{1,0:T(8,128)(2,1)S(1)} %get-tuple-element.29), channel_id=1, source_target_pairs={{0,1},{1,2},{2,3},{3,0},{4,5},{5,6},{6,7},{7,4},{8,9},{9,10},{10,1... | collective-permute-start | bytes 417800 | tf_op jit(solution)/shard_map/ppermute | solution.py:560
  54.8 1.4 %collective-permute-start.9 = (bf16[136,512]{1,0:T(8,128)(2,1)S(1)}, bf16[136,512]{1,0:T(8,128)(2,1)S(1)}, u32[]{:S(2)}, u32[]{:S(2)}) collective-permute-start(bf16[136,512]{1,0:T(8,128)(2,1)S(1)} %get-tuple-element.30), channel_id=1, source_target_pairs={{0,2},{1,3},{2,0},{3,1},{4,6},{5,7},{6,4},{7,5},{8,10},{9,11},{10,... | collective-permute-start | bytes 417800 | tf_op jit(solution)/shard_map/ppermute | solution.py:560
  56.2 0.6 collective-permute-start.10
  56.8 1.9 %heads.3 = (bf16[128,2048]{1,0:T(8,128)(2,1)S(1)}, f32[136,512]{1,0:T(8,128)S(1)}, bf16[136,512]{1,0:T(8,128)(2,1)S(1)}, bf16[136,512]{1,0:T(8,128)(2,1)S(1)}, bf16[136,512]{1,0:T(8,128)(2,1)S(1)}) custom-call(s32[3]{0:T(128)S(1)} %pad_add_fusion.meta, f32[128,2048]{1,0:T(8,128)S(1)} %project.4.keep, bf16[128,2048]{1,0:T(8,128)(2,1)S(1)} %collective-permute-done.19.other, ...), custom_call_target="tpu_custom_call" | custom-call | flops 1073741824 | tf_op jit(solution)/shard_map/heads/pallas_call | solution.py:393
  58.7 1.3 %collective-permute-start.24 = (bf16[128,2048]{1,0:T(8,128)(2,1)S(1)}, bf16[128,2048]{1,0:T(8,128)(2,1)S(1)}, u32[]{:S(2)}, u32[]{:S(2)}) collective-permute-start(bf16[128,2048]{1,0:T(8,128)(2,1)S(1)} %get-tuple-element.40.kept1), channel_id=1, source_target_pairs={{0,16},{8,24},{1,17},{9,25},{2,18},{10,26},{3,19},{11,27},{4,20},{... | collective-permute-start | bytes 1572872 | tf_op jit(solution)/shard_map/ppermute | solution.py:562
  60.0 3.5 %collective-permute-done.8.refs_0_ = bf16[136,512]{1,0:T(8,128)(2,1)S(1)} collective-permute-done((bf16[136,512]{1,0:T(8,128)(2,1)S(1)}, bf16[136,512]{1,0:T(8,128)(2,1)S(1)}, u32[]{:S(2)}, u32[]{:S(2)}) %collective-permute-start.8) | collective-permute-done | bytes 139296 | tf_op jit(solution)/shard_map/ppermute | solution.py:560
  63.4 2.7 %collective-permute-start.20 = (bf16[136,512]{1,0:T(8,128)(2,1)S(1)}, bf16[136,512]{1,0:T(8,128)(2,1)S(1)}, u32[]{:S(2)}, u32[]{:S(2)}) collective-permute-start(bf16[136,512]{1,0:T(8,128)(2,1)S(1)} %get-tuple-element.37), channel_id=1, source_target_pairs={{0,1},{1,2},{2,3},{3,0},{4,5},{5,6},{6,7},{7,4},{8,9},{9,10},{10,1... | collective-permute-start | bytes 417800 | tf_op jit(solution)/shard_map/ppermute | solution.py:560
  66.1 0.7 collective-permute-done.9.refs_1_
  66.8 3.9 %collective-permute-start.21 = (bf16[136,512]{1,0:T(8,128)(2,1)S(1)}, bf16[136,512]{1,0:T(8,128)(2,1)S(1)}, u32[]{:S(2)}, u32[]{:S(2)}) collective-permute-start(bf16[136,512]{1,0:T(8,128)(2,1)S(1)} %get-tuple-element.38), channel_id=1, source_target_pairs={{0,2},{1,3},{2,0},{3,1},{4,6},{5,7},{6,4},{7,5},{8,10},{9,11},{10,... | collective-permute-start | bytes 417800 | tf_op jit(solution)/shard_map/ppermute | solution.py:560
  70.7 0.3 collective-permute-done.10.refs_2_
  71.2 3.7 %collective-permute-done.20.refs_0_ = bf16[136,512]{1,0:T(8,128)(2,1)S(1)} collective-permute-done((bf16[136,512]{1,0:T(8,128)(2,1)S(1)}, bf16[136,512]{1,0:T(8,128)(2,1)S(1)}, u32[]{:S(2)}, u32[]{:S(2)}) %collective-permute-start.20) | collective-permute-done | bytes 139296 | tf_op jit(solution)/shard_map/ppermute | solution.py:560
  74.9 1.3 %collective-permute-start.11 = (bf16[128,512]{1,0:T(8,128)(2,1)S(1)}, bf16[128,512]{1,0:T(8,128)(2,1)S(1)}, u32[]{:S(2)}, u32[]{:S(2)}) collective-permute-start(bf16[128,512]{1,0:T(8,128)(2,1)S(1)} %finish.2), channel_id=1, source_target_pairs={{0,16},{8,24},{1,17},{9,25},{2,18},{10,26},{3,19},{11,27},{4,20},{... | collective-permute-start | bytes 393224 | tf_op jit(solution)/shard_map/ppermute | solution.py:564
  76.2 0.2 collective-permute-done.21.refs_1_
  76.4 2.0 %collective-permute-done.22.refs_2_ = bf16[136,512]{1,0:T(8,128)(2,1)S(1)} collective-permute-done((bf16[136,512]{1,0:T(8,128)(2,1)S(1)}, bf16[136,512]{1,0:T(8,128)(2,1)S(1)}, u32[]{:S(2)}, u32[]{:S(2)}) %collective-permute-start.22) | collective-permute-done | bytes 139296 | tf_op jit(solution)/shard_map/ppermute | solution.py:560
  78.6 1.3 %collective-permute-start.23 = (bf16[128,512]{1,0:T(8,128)(2,1)S(1)}, bf16[128,512]{1,0:T(8,128)(2,1)S(1)}, u32[]{:S(2)}, u32[]{:S(2)}) collective-permute-start(bf16[128,512]{1,0:T(8,128)(2,1)S(1)} %finish.3), channel_id=1, source_target_pairs={{0,16},{8,24},{1,17},{9,25},{2,18},{10,26},{3,19},{11,27},{4,20},{... | collective-permute-start | bytes 393224 | tf_op jit(solution)/shard_map/ppermute | solution.py:564
  79.9 1.7 %place.2.before = bf16[512,2048]{1,0:T(8,128)(2,1)} custom-call(s32[3]{0:T(128)S(1)} %pad_add_fusion.meta, bf16[128,2048]{1,0:T(8,128)(2,1)S(1)} %get-tuple-element.41.kept0, bf16[128,2048]{1,0:T(8,128)(2,1)S(1)} %get-tuple-element.40.kept1, bf16[128,2048]{1,0:T(8,128)(2,1)S(1)} %collective-permute-done.25.moved0), custom_call_target="tpu_custom_call" | custom-call | flops 67108864 | tf_op jit(solution)/shard_map/place/pallas_call | solution.py:461
  81.8 4.1 %collective-permute-done.23 = bf16[128,512]{1,0:T(8,128)(2,1)S(1)} collective-permute-done((bf16[128,512]{1,0:T(8,128)(2,1)S(1)}, bf16[128,512]{1,0:T(8,128)(2,1)S(1)}, u32[]{:S(2)}, u32[]{:S(2)}) %collective-permute-start.23) | collective-permute-done | bytes 131104 | tf_op jit(solution)/shard_map/ppermute | solution.py:564
  85.9 0.9 %maximum_select_fusion = bf16[1,512,512]{2,1,0:T(8,128)(2,1)} fusion(bf16[1,128,512]{2,1,0:T(8,128)(2,1)S(1)} %bitcast.9, bf16[1,128,512]{2,1,0:T(8,128)(2,1)S(1)} %bitcast.12, bf16[1,128,512]{2,1,0:T(8,128)(2,1)S(1)} %bitcast.8, bf16[1,128,512]{2,1,0:T(8,128)(2,1)S(1)} %bitcast.11, pred[]{:T(512)S(6)} %ge.3), kind=kLoop, calls=%fused_computation | loop fusion | flops 2359296 | bytes 1048577 | tf_op jit(solution)/shard_map/jit(_where)/select_n | solution.py:568
  86.8 1.3 %place.3 = bf16[512,2048]{1,0:T(8,128)(2,1)} custom-call(s32[3]{0:T(128)S(1)} %pad_add_fusion.meta, bf16[128,2048]{1,0:T(8,128)(2,1)S(1)} %collective-permute-done.24.moved1, bf16[512,2048]{1,0:T(8,128)(2,1)} %place.2.before), custom_call_target="tpu_custom_call", output_to_operand_aliasing={{}: (2, {})} | custom-call | flops 67108864 | tf_op jit(solution)/shard_map/place/pallas_call | solution.py:483
  (23 shorter events, 0.9 us)
Async XLA Ops:
  1.3 4.0 %collective-permute-start.12 = (bf16[64,1600]{1,0:T(8,128)(2,1)S(1)}, bf16[64,1600]{1,0:T(8,128)(2,1)S(1)}, u32[]{:S(2)}, u32[]{:S(2)}) collective-permute-start(bf16[64,1600]{1,0:T(8,128)(2,1)S(1)} %get-tuple-element.32), channel_id=1, source_target_pairs={{8,12},{12,28},{9,13},{13,29},{10,14},{14,30},{11,15},{15,31}} | collective-permute-start | bytes 614408 | tf_op jit(solution)/shard_map/ppermute | solution.py:535
  2.0 4.0 %collective-permute-start.13 = (bf16[64,1600]{1,0:T(8,128)(2,1)S(1)}, bf16[64,1600]{1,0:T(8,128)(2,1)S(1)}, u32[]{:S(2)}, u32[]{:S(2)}) collective-permute-start(bf16[64,1600]{1,0:T(8,128)(2,1)S(1)} %get-tuple-element.33), channel_id=1, source_target_pairs={{8,8},{12,24},{9,9},{13,25},{10,10},{14,26},{11,11},{15,27}} | collective-permute-start | bytes 614408 | tf_op jit(solution)/shard_map/ppermute | solution.py:535
  2.7 9.3 %collective-permute-start.14 = (bf16[64,1600]{1,0:T(8,128)(2,1)S(1)}, bf16[64,1600]{1,0:T(8,128)(2,1)S(1)}, u32[]{:S(2)}, u32[]{:S(2)}) collective-permute-start(bf16[64,1600]{1,0:T(8,128)(2,1)S(1)} %get-tuple-element.34), channel_id=1, source_target_pairs={{8,4},{12,20},{9,5},{13,21},{10,6},{14,22},{11,7},{15,23}} | collective-permute-start | bytes 614408 | tf_op jit(solution)/shard_map/ppermute | solution.py:535
  4.0 8.6 %collective-permute-start.15 = (bf16[64,1600]{1,0:T(8,128)(2,1)S(1)}, bf16[64,1600]{1,0:T(8,128)(2,1)S(1)}, u32[]{:S(2)}, u32[]{:S(2)}) collective-permute-start(bf16[64,1600]{1,0:T(8,128)(2,1)S(1)} %get-tuple-element.35), channel_id=1, source_target_pairs={{8,0},{12,16},{9,1},{13,17},{10,2},{14,18},{11,3},{15,19}} | collective-permute-start | bytes 614408 | tf_op jit(solution)/shard_map/ppermute | solution.py:535
  4.7 10.7 %collective-permute-start = (bf16[64,640]{1,0:T(8,128)(2,1)S(1)}, bf16[64,640]{1,0:T(8,128)(2,1)S(1)}, u32[]{:S(2)}, u32[]{:S(2)}) collective-permute-start(bf16[64,640]{1,0:T(8,128)(2,1)S(1)} %get-tuple-element.22), channel_id=1, source_target_pairs={{0,12},{4,28},{1,13},{5,29},{2,14},{6,30},{3,15},{7,31}} | collective-permute-start | bytes 245768 | tf_op jit(solution)/shard_map/ppermute | solution.py:535
  5.4 10.0 %collective-permute-start.1 = (bf16[64,640]{1,0:T(8,128)(2,1)S(1)}, bf16[64,640]{1,0:T(8,128)(2,1)S(1)}, u32[]{:S(2)}, u32[]{:S(2)}) collective-permute-start(bf16[64,640]{1,0:T(8,128)(2,1)S(1)} %get-tuple-element.23), channel_id=1, source_target_pairs={{0,8},{4,24},{1,9},{5,25},{2,10},{6,26},{3,11},{7,27}} | collective-permute-start | bytes 245768 | tf_op jit(solution)/shard_map/ppermute | solution.py:535
  6.0 9.3 %collective-permute-start.2 = (bf16[64,640]{1,0:T(8,128)(2,1)S(1)}, bf16[64,640]{1,0:T(8,128)(2,1)S(1)}, u32[]{:S(2)}, u32[]{:S(2)}) collective-permute-start(bf16[64,640]{1,0:T(8,128)(2,1)S(1)} %get-tuple-element.24), channel_id=1, source_target_pairs={{0,4},{4,20},{1,5},{5,21},{2,6},{6,22},{3,7},{7,23}} | collective-permute-start | bytes 245768 | tf_op jit(solution)/shard_map/ppermute | solution.py:535
  12.0 3.4 %collective-permute-start.3 = (bf16[64,640]{1,0:T(8,128)(2,1)S(1)}, bf16[64,640]{1,0:T(8,128)(2,1)S(1)}, u32[]{:S(2)}, u32[]{:S(2)}) collective-permute-start(bf16[64,640]{1,0:T(8,128)(2,1)S(1)} %get-tuple-element.25), channel_id=1, source_target_pairs={{0,0},{4,16},{1,1},{5,17},{2,2},{6,18},{3,3},{7,19}} | collective-permute-start | bytes 245768 | tf_op jit(solution)/shard_map/ppermute | solution.py:535
  12.7 15.0 %collective-permute-start.17 = (bf16[64,1600]{1,0:T(8,128)(2,1)S(1)}, bf16[64,1600]{1,0:T(8,128)(2,1)S(1)}, u32[]{:S(2)}, u32[]{:S(2)}) collective-permute-start(bf16[64,1600]{1,0:T(8,128)(2,1)S(1)} %select_select_fusion.refs_0_), channel_id=1, source_target_pairs={{0,2},{1,3},{2,0},{3,1},{4,6},{5,7},{6,4},{7,5},{8,10},{9,11},{10,... | collective-permute-start | bytes 614408 | tf_op jit(solution)/shard_map/ppermute | solution.py:540
  15.4 10.3 %collective-permute-start.5 = (bf16[64,640]{1,0:T(8,128)(2,1)S(1)}, bf16[64,640]{1,0:T(8,128)(2,1)S(1)}, u32[]{:S(2)}, u32[]{:S(2)}) collective-permute-start(bf16[64,640]{1,0:T(8,128)(2,1)S(1)} %select_select_fusion.1.refs_0_), channel_id=1, source_target_pairs={{0,2},{1,3},{2,0},{3,1},{4,6},{5,7},{6,4},{7,5},{8,10},{9,11},{10,... | collective-permute-start | bytes 245768 | tf_op jit(solution)/shard_map/ppermute | solution.py:540
  16.4 14.4 %collective-permute-start.4 = (bf16[64,640]{1,0:T(8,128)(2,1)S(1)}, bf16[64,640]{1,0:T(8,128)(2,1)S(1)}, u32[]{:S(2)}, u32[]{:S(2)}) collective-permute-start(bf16[64,640]{1,0:T(8,128)(2,1)S(1)} %select_select_fusion.1.refs_0_), channel_id=1, source_target_pairs={{0,1},{1,0},{2,3},{3,2},{4,5},{5,4},{6,7},{7,6},{8,9},{9,8},{10,11... | collective-permute-start | bytes 245768 | tf_op jit(solution)/shard_map/ppermute | solution.py:540
  25.7 5.3 %collective-permute-start.6 = (bf16[64,640]{1,0:T(8,128)(2,1)S(1)}, bf16[64,640]{1,0:T(8,128)(2,1)S(1)}, u32[]{:S(2)}, u32[]{:S(2)}) collective-permute-start(bf16[64,640]{1,0:T(8,128)(2,1)S(1)} %collective-permute-done.5.refs_2_), channel_id=1, source_target_pairs={{0,1},{1,0},{2,3},{3,2},{4,5},{5,4},{6,7},{7,6},{8,9},{9,8},{10,11... | collective-permute-start | bytes 245768 | tf_op jit(solution)/shard_map/ppermute | solution.py:540
  27.0 10.6 %collective-permute-start.16 = (bf16[64,1600]{1,0:T(8,128)(2,1)S(1)}, bf16[64,1600]{1,0:T(8,128)(2,1)S(1)}, u32[]{:S(2)}, u32[]{:S(2)}) collective-permute-start(bf16[64,1600]{1,0:T(8,128)(2,1)S(1)} %select_select_fusion.refs_0_), channel_id=1, source_target_pairs={{0,1},{1,0},{2,3},{3,2},{4,5},{5,4},{6,7},{7,6},{8,9},{9,8},{10,11... | collective-permute-start | bytes 614408 | tf_op jit(solution)/shard_map/ppermute | solution.py:540
  27.7 11.4 %collective-permute-start.18 = (bf16[64,1600]{1,0:T(8,128)(2,1)S(1)}, bf16[64,1600]{1,0:T(8,128)(2,1)S(1)}, u32[]{:S(2)}, u32[]{:S(2)}) collective-permute-start(bf16[64,1600]{1,0:T(8,128)(2,1)S(1)} %collective-permute-done.17.refs_2_), channel_id=1, source_target_pairs={{0,1},{1,0},{2,3},{3,2},{4,5},{5,4},{6,7},{7,6},{8,9},{9,8},{10,11... | collective-permute-start | bytes 614408 | tf_op jit(solution)/shard_map/ppermute | solution.py:540
  32.5 14.1 %collective-permute-start.7 = (bf16[128,2048]{1,0:T(8,128)(2,1)S(1)}, bf16[128,2048]{1,0:T(8,128)(2,1)S(1)}, u32[]{:S(2)}, u32[]{:S(2)}) collective-permute-start(bf16[128,2048]{1,0:T(8,128)(2,1)S(1)} %get-tuple-element.27), channel_id=1, source_target_pairs={{0,4},{4,0},{1,5},{5,1},{2,6},{6,2},{3,7},{7,3},{8,12},{12,8},{9,1... | collective-permute-start | bytes 1572872 | tf_op jit(solution)/shard_map/ppermute | solution.py:551
  40.8 5.9 %copy-start = (f32[2048]{0:T(1024)S(1)}, f32[2048]{0:T(1024)}, u32[]{:S(2)}) copy-start(f32[2048]{0:T(1024)} %gain.3) | copy-start | bytes 24580
  40.8 16.0 %collective-permute-start.19 = (bf16[128,2048]{1,0:T(8,128)(2,1)S(1)}, bf16[128,2048]{1,0:T(8,128)(2,1)S(1)}, u32[]{:S(2)}, u32[]{:S(2)}) collective-permute-start(bf16[128,2048]{1,0:T(8,128)(2,1)S(1)} %project.5), channel_id=1, source_target_pairs={{0,4},{4,0},{1,5},{5,1},{2,6},{6,2},{3,7},{7,3},{8,12},{12,8},{9,1... | collective-permute-start | bytes 1572872 | tf_op jit(solution)/shard_map/ppermute | solution.py:551
  48.6 31.3 %collective-permute-start.25 = (bf16[128,2048]{1,0:T(8,128)(2,1)S(1)}, bf16[128,2048]{1,0:T(8,128)(2,1)S(1)}, u32[]{:S(2)}, u32[]{:S(2)}) collective-permute-start(bf16[128,2048]{1,0:T(8,128)(2,1)S(1)} %get-tuple-element.41.kept0), channel_id=1, source_target_pairs={{0,16},{8,24},{1,17},{9,25},{2,18},{10,26},{3,19},{11,27},{4,20},{... | collective-permute-start | bytes 1572872 | tf_op jit(solution)/shard_map/ppermute | solution.py:562
  51.6 11.9 %collective-permute-start.8 = (bf16[136,512]{1,0:T(8,128)(2,1)S(1)}, bf16[136,512]{1,0:T(8,128)(2,1)S(1)}, u32[]{:S(2)}, u32[]{:S(2)}) collective-permute-start(bf16[136,512]{1,0:T(8,128)(2,1)S(1)} %get-tuple-element.29), channel_id=1, source_target_pairs={{0,1},{1,2},{2,3},{3,0},{4,5},{5,6},{6,7},{7,4},{8,9},{9,10},{10,1... | collective-permute-start | bytes 417800 | tf_op jit(solution)/shard_map/ppermute | solution.py:560
  54.8 12.0 %collective-permute-start.9 = (bf16[136,512]{1,0:T(8,128)(2,1)S(1)}, bf16[136,512]{1,0:T(8,128)(2,1)S(1)}, u32[]{:S(2)}, u32[]{:S(2)}) collective-permute-start(bf16[136,512]{1,0:T(8,128)(2,1)S(1)} %get-tuple-element.30), channel_id=1, source_target_pairs={{0,2},{1,3},{2,0},{3,1},{4,6},{5,7},{6,4},{7,5},{8,10},{9,11},{10,... | collective-permute-start | bytes 417800 | tf_op jit(solution)/shard_map/ppermute | solution.py:560
  56.2 14.8 %collective-permute-start.10 = (bf16[136,512]{1,0:T(8,128)(2,1)S(1)}, bf16[136,512]{1,0:T(8,128)(2,1)S(1)}, u32[]{:S(2)}, u32[]{:S(2)}) collective-permute-start(bf16[136,512]{1,0:T(8,128)(2,1)S(1)} %get-tuple-element.31), channel_id=1, source_target_pairs={{0,3},{1,0},{2,1},{3,2},{4,7},{5,4},{6,5},{7,6},{8,11},{9,8},{10,9... | collective-permute-start | bytes 417800 | tf_op jit(solution)/shard_map/ppermute | solution.py:560
  58.7 28.1 %collective-permute-start.24 = (bf16[128,2048]{1,0:T(8,128)(2,1)S(1)}, bf16[128,2048]{1,0:T(8,128)(2,1)S(1)}, u32[]{:S(2)}, u32[]{:S(2)}) collective-permute-start(bf16[128,2048]{1,0:T(8,128)(2,1)S(1)} %get-tuple-element.40.kept1), channel_id=1, source_target_pairs={{0,16},{8,24},{1,17},{9,25},{2,18},{10,26},{3,19},{11,27},{4,20},{... | collective-permute-start | bytes 1572872 | tf_op jit(solution)/shard_map/ppermute | solution.py:562
  63.4 11.5 %collective-permute-start.20 = (bf16[136,512]{1,0:T(8,128)(2,1)S(1)}, bf16[136,512]{1,0:T(8,128)(2,1)S(1)}, u32[]{:S(2)}, u32[]{:S(2)}) collective-permute-start(bf16[136,512]{1,0:T(8,128)(2,1)S(1)} %get-tuple-element.37), channel_id=1, source_target_pairs={{0,1},{1,2},{2,3},{3,0},{4,5},{5,6},{6,7},{7,4},{8,9},{9,10},{10,1... | collective-permute-start | bytes 417800 | tf_op jit(solution)/shard_map/ppermute | solution.py:560
  66.8 9.6 %collective-permute-start.21 = (bf16[136,512]{1,0:T(8,128)(2,1)S(1)}, bf16[136,512]{1,0:T(8,128)(2,1)S(1)}, u32[]{:S(2)}, u32[]{:S(2)}) collective-permute-start(bf16[136,512]{1,0:T(8,128)(2,1)S(1)} %get-tuple-element.38), channel_id=1, source_target_pairs={{0,2},{1,3},{2,0},{3,1},{4,6},{5,7},{6,4},{7,5},{8,10},{9,11},{10,... | collective-permute-start | bytes 417800 | tf_op jit(solution)/shard_map/ppermute | solution.py:560
  71.0 7.4 %collective-permute-start.22 = (bf16[136,512]{1,0:T(8,128)(2,1)S(1)}, bf16[136,512]{1,0:T(8,128)(2,1)S(1)}, u32[]{:S(2)}, u32[]{:S(2)}) collective-permute-start(bf16[136,512]{1,0:T(8,128)(2,1)S(1)} %get-tuple-element.39), channel_id=1, source_target_pairs={{0,3},{1,0},{2,1},{3,2},{4,7},{5,4},{6,5},{7,6},{8,11},{9,8},{10,9... | collective-permute-start | bytes 417800 | tf_op jit(solution)/shard_map/ppermute | solution.py:560
  74.9 6.8 %collective-permute-start.11 = (bf16[128,512]{1,0:T(8,128)(2,1)S(1)}, bf16[128,512]{1,0:T(8,128)(2,1)S(1)}, u32[]{:S(2)}, u32[]{:S(2)}) collective-permute-start(bf16[128,512]{1,0:T(8,128)(2,1)S(1)} %finish.2), channel_id=1, source_target_pairs={{0,16},{8,24},{1,17},{9,25},{2,18},{10,26},{3,19},{11,27},{4,20},{... | collective-permute-start | bytes 393224 | tf_op jit(solution)/shard_map/ppermute | solution.py:564
  78.6 7.3 %collective-permute-start.23 = (bf16[128,512]{1,0:T(8,128)(2,1)S(1)}, bf16[128,512]{1,0:T(8,128)(2,1)S(1)}, u32[]{:S(2)}, u32[]{:S(2)}) collective-permute-start(bf16[128,512]{1,0:T(8,128)(2,1)S(1)} %finish.3), channel_id=1, source_target_pairs={{0,16},{8,24},{1,17},{9,25},{2,18},{10,26},{3,19},{11,27},{4,20},{... | collective-permute-start | bytes 393224 | tf_op jit(solution)/shard_map/ppermute | solution.py:564

commit v6 on v5

--- a/solution.py
+++ b/solution.py
@@ -173,8 +173,9 @@
 MIB = 1 << 20
 
 
-def smem():
-    return pl.BlockSpec(memory_space=pltpu.SMEM)
+class Place:
+    def __getitem__(self, axis):
+        return lax.axis_index(("group", "dp", "mp")[axis])
 
 
 def vmem():
@@ -196,7 +197,8 @@
     )
 
 
-def encode_kernel(dp_count, meta, dest, limits, *refs):
+def encode_kernel(dp_count, dest, limits, *refs):
+    meta = Place()
     group, dp, mp = meta[0], meta[1], meta[2]
     targets = 2 * dp_count
     inputs, messages, scratch = refs[:4], refs[4 : 4 + 2 * targets], refs[4 + 2 * targets :]
@@ -215,11 +217,17 @@
                     (
                         (dest, routes),
                         (limits, lives),
-                        (inputs[2 * stream], states),
                         (inputs[2 * stream + 1], gain),
                     )
                 )
             ]
+            for b in range(BLOCKS):
+                part = (0, pl.ds(b * share, share))
+                copies.append(
+                    pltpu.make_async_copy(
+                        inputs[2 * stream].at[part], states.at[part], sems.at[len(copies)]
+                    )
+                )
             for copy in copies:
                 copy.start()
             for copy in copies:
@@ -245,7 +253,7 @@
                     ]
 
 
-def encode(dp_count, meta, dest, limits, streams):
+def encode(dp_count, dest, limits, streams):
     arguments, shapes = [], []
     scratch = [pltpu.SMEM(dest.shape, jnp.int32), pltpu.SMEM(limits.shape, jnp.int32)]
     for states, gain, _ in streams:
@@ -257,12 +265,12 @@
     return pl.pallas_call(
         functools.partial(encode_kernel, dp_count),
         out_shape=shapes,
-        in_specs=[smem()] + [hbm()] * (2 + len(arguments)),
+        in_specs=[hbm()] * (2 + len(arguments)),
         out_specs=[vmem()] * len(shapes),
-        scratch_shapes=scratch + [pltpu.SemaphoreType.DMA((4,))],
+        scratch_shapes=scratch + [pltpu.SemaphoreType.DMA((3 + BLOCKS,))],
         name="encode",
         **limits_of(8, 1 << 28),
-    )(meta, *in_hbm([dest, limits, *arguments]))
+    )(*in_hbm([dest, limits, *arguments]))
 
 
 def fetch_kernel(cuts, *refs):
@@ -300,7 +308,8 @@
     return lax.rem(mp + (mp_count - shift), mp_count)
 
 
-def project_half_kernel(mp_count, tile, half, meta, *refs):
+def project_half_kernel(mp_count, tile, half, *refs):
+    meta = Place()
     pieces, weight, result, rows = refs[:mp_count], *refs[mp_count:]
     share = pieces[0].shape[0] // 2
     for shift in range(mp_count):
@@ -313,22 +322,23 @@
         result[:, first : first + tile] = out.astype(result.dtype)
 
 
-def project_half(mp_count, meta, pieces, weight, tile, half):
+def project_half(mp_count, pieces, weight, tile, half):
     depth, width = weight.shape
     rows = pieces[0].shape[0] * mp_count // 2
     kind = jnp.bfloat16 if half else jnp.float32
     return pl.pallas_call(
         functools.partial(project_half_kernel, mp_count, tile, half),
         out_shape=jax.ShapeDtypeStruct((rows, width), kind),
-        in_specs=[smem()] + [vmem()] * (mp_count + 1),
+        in_specs=[vmem()] * (mp_count + 1),
         out_specs=vmem(),
         scratch_shapes=[pltpu.VMEM((rows, depth), jnp.bfloat16)],
         name="project",
         **limits_of(12, 2 * rows * depth * width),
-    )(meta, *pieces, weight)
-
-
-def project_kernel(mp_count, tile, meta, *refs):
+    )(*pieces, weight)
+
+
+def project_kernel(mp_count, tile, *refs):
+    meta = Place()
     pieces, weight, keep, send, rows = refs[:mp_count], *refs[mp_count:]
     share = pieces[0].shape[0] // 2
     block = share * mp_count
@@ -345,7 +355,7 @@
         send[:, first : first + tile] = out[block:].astype(jnp.bfloat16)
 
 
-def project_rows(mp_count, meta, pieces, weight, tile):
+def project_rows(mp_count, pieces, weight, tile):
     depth, width = weight.shape
     rows = pieces[0].shape[0] * mp_count
     return pl.pallas_call(
@@ -354,15 +364,16 @@
             jax.ShapeDtypeStruct((rows // 2, width), jnp.float32),
             jax.ShapeDtypeStruct((rows // 2, width), jnp.bfloat16),
         ],
-        in_specs=[smem()] + [vmem()] * (mp_count + 1),
+        in_specs=[vmem()] * (mp_count + 1),
         out_specs=[vmem()] * 2,
         scratch_shapes=[pltpu.VMEM((rows, depth), jnp.bfloat16)],
         name="project",
         **limits_of(12, 2 * rows * depth * width),
-    )(meta, *pieces, weight)
-
-
-def heads_kernel(mp_count, meta, keep, other, gain, weight, tokens, own, *rest):
+    )(*pieces, weight)
+
+
+def heads_kernel(mp_count, keep, other, gain, weight, tokens, own, *rest):
+    meta = Place()
     sends, scaled = rest[:-1], rest[-1]
     rows, tile = own.shape[0] - 8, own.shape[1]
     rounded = (keep[...] + other[...].astype(jnp.float32)).astype(jnp.bfloat16)
@@ -387,12 +398,12 @@
             own[rows:, :] = packed
 
 
-def heads(mp_count, meta, keep, other, gain, weight):
+def heads(mp_count, keep, other, gain, weight):
     rows, width = keep.shape
     tile = weight.shape[1] // mp_count
     return pl.pallas_call(
         functools.partial(heads_kernel, mp_count),
-        in_specs=[smem()] + [vmem()] * 4,
+        in_specs=[vmem()] * 4,
         out_specs=[vmem()] * (1 + mp_count),
         scratch_shapes=[pltpu.VMEM((rows, width), jnp.bfloat16)],
         out_shape=[
@@ -402,7 +413,7 @@
         + [jax.ShapeDtypeStruct((rows + 8, tile), jnp.bfloat16)] * (mp_count - 1),
         name="heads",
         **limits_of(14, 2 * rows * width * weight.shape[1]),
-    )(meta, keep, other, gain, weight)
+    )(keep, other, gain, weight)
 
 
 def finish_kernel(full_width, own, *refs):
@@ -429,7 +440,8 @@
     )(own, *parts)
 
 
-def place_early_kernel(meta, kept0, kept1, moved0, out, zeros, sems):
+def place_early_kernel(kept0, kept1, moved0, out, zeros, sems):
+    meta = Place()
     rows = kept0.shape[0]
     at = lambda place: out.at[pl.ds(place * rows, rows)]
 
@@ -456,20 +468,21 @@
             copy.wait()
 
 
-def place_early(meta, kept, moved):
+def place_early(kept, moved):
     rows, width = moved.shape
     return pl.pallas_call(
         place_early_kernel,
         out_shape=pltpu.HBM((BLOCKS * rows, width), moved.dtype),
-        in_specs=[smem()] + [pl.BlockSpec(memory_space=pl.ANY)] * 3,
+        in_specs=[pl.BlockSpec(memory_space=pl.ANY)] * 3,
         out_specs=hbm(),
         scratch_shapes=[pltpu.VMEM((rows, width), moved.dtype), pltpu.SemaphoreType.DMA((BLOCKS,))],
         name="place",
         **limits_of(4, 1 << 26),
-    )(meta, *kept, moved)
-
-
-def place_late_kernel(meta, moved1, before, out, sem):
+    )(*kept, moved)
+
+
+def place_late_kernel(moved1, before, out, sem):
+    meta = Place()
     rows = moved1.shape[0]
 
     @pl.when(meta[0] >= 2)
@@ -479,17 +492,17 @@
         copy.wait()
 
 
-def place_late(meta, moved, rows_out):
+def place_late(moved, rows_out):
     return pl.pallas_call(
         place_late_kernel,
         out_shape=pltpu.HBM(rows_out.shape, rows_out.dtype),
-        in_specs=[smem(), pl.BlockSpec(memory_space=pl.ANY), hbm()],
+        in_specs=[pl.BlockSpec(memory_space=pl.ANY), hbm()],
         out_specs=hbm(),
         scratch_shapes=[pltpu.SemaphoreType.DMA],
-        input_output_aliases={2: 0},
+        input_output_aliases={1: 0},
         name="place",
         **limits_of(4, 1 << 26),
-    )(meta, moved, rows_out)
+    )(moved, rows_out)
 
 
 def shards_direct(
@@ -506,10 +519,8 @@
 ):
     group = lax.axis_index("group")
     dp = lax.axis_index("dp")
-    mp = lax.axis_index("mp")
     dp_count = lax.axis_size("dp")
     mp_count = lax.axis_size("mp")
-    meta = jnp.stack([group, dp, mp]).astype(jnp.int32)
     rings = [[(i, (i + shift) % mp_count) for i in range(mp_count)] for shift in range(mp_count)]
     spreads = rings
     if mp_count == 4:
@@ -524,7 +535,7 @@
         (image_states, image_gain, image_proj),
     )
 
-    messages = encode(dp_count, meta, destination, block_rows, streams)
+    messages = encode(dp_count, destination, block_rows, streams)
     mine = lax.rem(group, 2) * dp_count + dp
     gathered = []
     for stream in range(2):
@@ -543,17 +554,17 @@
     for stream, (_, _, proj) in enumerate(streams):
         (proj,) = fetch([proj], (4,))
         if stream == 0:
-            keep, send = project_rows(mp_count, meta, gathered[stream], proj, 512)
+            keep, send = project_rows(mp_count, gathered[stream], proj, 512)
         else:
-            send = project_half(mp_count, meta, gathered[stream], proj, 512, 1)
-            keep = project_half(mp_count, meta, gathered[stream], proj, 512, 0)
+            send = project_half(mp_count, gathered[stream], proj, 512, 1)
+            keep = project_half(mp_count, gathered[stream], proj, 512, 0)
         partial.append((keep, send))
         others.append(lax.ppermute(send, "dp", swap))
     (heads_weight,) = fetch([kv_weight], (8,))
     kept, moved, head_parts = [], [], []
     for stream in range(2):
         tokens, own, *sends = heads(
-            mp_count, meta, partial[stream][0], others[stream], input_gain, heads_weight
+            mp_count, partial[stream][0], others[stream], input_gain, heads_weight
         )
         sums = []
         for shift, part in enumerate(sends, 1):
@@ -562,8 +573,8 @@
         moved.append(lax.ppermute(tokens, "group", up))
         values = finish(full_width, own, sums)
         head_parts += [lax.ppermute(values, "group", up), values]
-    rows_out = place_early(meta, kept, moved[0])
-    rows_out = place_late(meta, moved[1], rows_out)
+    rows_out = place_early(kept, moved[0])
+    rows_out = place_late(moved[1], rows_out)
     heads_out = jnp.concatenate(head_parts, axis=0)
     heads_out = jnp.where(on_backbone, heads_out, jnp.zeros_like(heads_out))
     return (heads_out[None], rows_out[None])

time: 88.5 us -> 85.9 us (0.971)
  the two profiles are of different devices: /device:TPU:14 before, /device:TPU:0 now
where the time goes in v6:
time: 85.9 us; the launch traced here: 84.7 us
  starting transfers between devices  44.2 us (51%)
  waiting for transfers between devices  21.4 us (25%)
  Pallas kernels  17.2 us (20%)
  between operations  0.98 us (1%)
  other arithmetic  0.95 us (1%)
    ppermute x8, starting transfers between devices, shards_direct(): lax.ppermute(messages[stream * targets + index], ('group', 'dp'), pairs)  14 us
    ppermute x6, waiting for transfers between devices, shards_direct(): pieces.append(lax.ppermute(sent, 'mp', spreads[shift]))  11.4 us
    ppermute x6, starting transfers between devices, shards_direct(): sums.append(lax.ppermute(part, 'mp', rings[shift]))  9.81 us
    ppermute x6, starting transfers between devices, shards_direct(): pieces.append(lax.ppermute(sent, 'mp', spreads[shift]))  8.19 us
    pallas_call x3, Pallas kernels, fetch(): pl.pallas_call(functools.partial(fetch_kernel, cuts), out_shape=[pltpu.VM...  8.13 us
    ppermute x6, waiting for transfers between devices, shards_direct(): sums.append(lax.ppermute(part, 'mp', rings[shift]))  6.65 us
    ppermute x2, starting transfers between devices, shards_direct(): head_parts += [lax.ppermute(values, 'group', up), values]  5.47 us
    ppermute x2, starting transfers between devices, shards_direct(): moved.append(lax.ppermute(tokens, 'group', up))  4.01 us
  transfers between devices with their start and end apart: 26, of which 7 were waited for; matrix products, arithmetic and copies ran while one was open for 1% of the time, Pallas kernels for 19%

profile of v6, /device:TPU:0, one launch (start us, length us, event | category | flops | bytes accessed | tf_op | source)
XLA Modules:
  0.0 84.7 jit_solution(17253134289328006406)
XLA Ops:
  0.6 1.4 %encode.1 = (bf16[64,640]{1,0:T(8,128)(2,1)S(1)}, bf16[64,640]{1,0:T(8,128)(2,1)S(1)}, bf16[64,640]{1,0:T(8,128)(2,1)S(1)}, bf16[64,640]{1,0:T(8,128)(2,1)S(1)},...) custom-call(s32[2,2,4]{2,1,0:T(2,128)} %dest.1, ...), custom_call_target="tpu_custom_call" | custom-call | flops 268435456 | tf_op jit(solution)/shard_map/encode/pallas_call | solution.py:265
  2.0 0.7 collective-permute-start.12
  2.7 0.7 collective-permute-start.13
  3.4 0.7 collective-permute-start.14
  4.1 1.3 %collective-permute-start.15 = (bf16[64,1600]{1,0:T(8,128)(2,1)S(1)}, bf16[64,1600]{1,0:T(8,128)(2,1)S(1)}, u32[]{:S(2)}, u32[]{:S(2)}) collective-permute-start(bf16[64,1600]{1,0:T(8,128)(2,1)S(1)} %get-tuple-element.35), channel_id=1, source_target_pairs={{8,0},{12,16},{9,1},{13,17},{10,2},{14,18},{11,3},{15,19}} | collective-permute-start | bytes 614408 | tf_op jit(solution)/shard_map/ppermute | solution.py:546
  5.4 7.4 %collective-permute-start = (bf16[64,640]{1,0:T(8,128)(2,1)S(1)}, bf16[64,640]{1,0:T(8,128)(2,1)S(1)}, u32[]{:S(2)}, u32[]{:S(2)}) collective-permute-start(bf16[64,640]{1,0:T(8,128)(2,1)S(1)} %get-tuple-element.22), channel_id=1, source_target_pairs={{0,12},{4,28},{1,13},{5,29},{2,14},{6,30},{3,15},{7,31}} | collective-permute-start | bytes 245768 | tf_op jit(solution)/shard_map/ppermute | solution.py:546
  12.8 1.3 %collective-permute-start.1 = (bf16[64,640]{1,0:T(8,128)(2,1)S(1)}, bf16[64,640]{1,0:T(8,128)(2,1)S(1)}, u32[]{:S(2)}, u32[]{:S(2)}) collective-permute-start(bf16[64,640]{1,0:T(8,128)(2,1)S(1)} %get-tuple-element.23), channel_id=1, source_target_pairs={{0,8},{4,24},{1,9},{5,25},{2,10},{6,26},{3,11},{7,27}} | collective-permute-start | bytes 245768 | tf_op jit(solution)/shard_map/ppermute | solution.py:546
  14.1 0.0 collective-permute-done.13
  14.1 1.3 %collective-permute-start.2 = (bf16[64,640]{1,0:T(8,128)(2,1)S(1)}, bf16[64,640]{1,0:T(8,128)(2,1)S(1)}, u32[]{:S(2)}, u32[]{:S(2)}) collective-permute-start(bf16[64,640]{1,0:T(8,128)(2,1)S(1)} %get-tuple-element.24), channel_id=1, source_target_pairs={{0,4},{4,20},{1,5},{5,21},{2,6},{6,22},{3,7},{7,23}} | collective-permute-start | bytes 245768 | tf_op jit(solution)/shard_map/ppermute | solution.py:546
  15.4 0.7 collective-permute-start.3
  16.1 0.0 collective-permute-done.15
  16.2 2.7 %collective-permute-start.17 = (bf16[64,1600]{1,0:T(8,128)(2,1)S(1)}, bf16[64,1600]{1,0:T(8,128)(2,1)S(1)}, u32[]{:S(2)}, u32[]{:S(2)}) collective-permute-start(bf16[64,1600]{1,0:T(8,128)(2,1)S(1)} %select_select_fusion.refs_0_), channel_id=1, source_target_pairs={{0,2},{1,3},{2,0},{3,1},{4,6},{5,7},{6,4},{7,5},{8,10},{9,11},{10,... | collective-permute-start | bytes 614408 | tf_op jit(solution)/shard_map/ppermute | solution.py:551
  18.9 1.3 %collective-permute-start.5 = (bf16[64,640]{1,0:T(8,128)(2,1)S(1)}, bf16[64,640]{1,0:T(8,128)(2,1)S(1)}, u32[]{:S(2)}, u32[]{:S(2)}) collective-permute-start(bf16[64,640]{1,0:T(8,128)(2,1)S(1)} %select_select_fusion.1.refs_0_), channel_id=1, source_target_pairs={{0,2},{1,3},{2,0},{3,1},{4,6},{5,7},{6,4},{7,5},{8,10},{9,11},{10,... | collective-permute-start | bytes 245768 | tf_op jit(solution)/shard_map/ppermute | solution.py:551
  20.1 1.6 %collective-permute-start.4 = (bf16[64,640]{1,0:T(8,128)(2,1)S(1)}, bf16[64,640]{1,0:T(8,128)(2,1)S(1)}, u32[]{:S(2)}, u32[]{:S(2)}) collective-permute-start(bf16[64,640]{1,0:T(8,128)(2,1)S(1)} %select_select_fusion.1.refs_0_), channel_id=1, source_target_pairs={{0,1},{1,0},{2,3},{3,2},{4,5},{5,4},{6,7},{7,6},{8,9},{9,8},{10,11... | collective-permute-start | bytes 245768 | tf_op jit(solution)/shard_map/ppermute | solution.py:551
  21.7 8.3 %collective-permute-done.5.refs_2_ = bf16[64,640]{1,0:T(8,128)(2,1)S(1)} collective-permute-done((bf16[64,640]{1,0:T(8,128)(2,1)S(1)}, bf16[64,640]{1,0:T(8,128)(2,1)S(1)}, u32[]{:S(2)}, u32[]{:S(2)}) %collective-permute-start.5) | collective-permute-done | bytes 81952 | tf_op jit(solution)/shard_map/ppermute | solution.py:551
  30.0 0.7 collective-permute-start.6
  30.7 1.4 %collective-permute-start.16 = (bf16[64,1600]{1,0:T(8,128)(2,1)S(1)}, bf16[64,1600]{1,0:T(8,128)(2,1)S(1)}, u32[]{:S(2)}, u32[]{:S(2)}) collective-permute-start(bf16[64,1600]{1,0:T(8,128)(2,1)S(1)} %select_select_fusion.refs_0_), channel_id=1, source_target_pairs={{0,1},{1,0},{2,3},{3,2},{4,5},{5,4},{6,7},{7,6},{8,9},{9,8},{10,11... | collective-permute-start | bytes 614408 | tf_op jit(solution)/shard_map/ppermute | solution.py:551
  32.0 0.7 collective-permute-start.18
  32.7 1.7 %fetch.3.refs_4_ = bf16[640,2048]{1,0:T(8,128)(2,1)S(1)} custom-call(bf16[640,2048]{1,0:T(8,128)(2,1)} %refs_0_.5), custom_call_target="tpu_custom_call" | custom-call | flops 268435456 | tf_op jit(solution)/shard_map/fetch/pallas_call | solution.py:294
  34.4 0.9 %collective-permute-done.6.refs_3_ = bf16[64,640]{1,0:T(8,128)(2,1)S(1)} collective-permute-done((bf16[64,640]{1,0:T(8,128)(2,1)S(1)}, bf16[64,640]{1,0:T(8,128)(2,1)S(1)}, u32[]{:S(2)}, u32[]{:S(2)}) %collective-permute-start.6) | collective-permute-done | bytes 81952 | tf_op jit(solution)/shard_map/ppermute | solution.py:551
  35.3 1.0 %project.3 = (f32[128,2048]{1,0:T(8,128)S(1)}, bf16[128,2048]{1,0:T(8,128)(2,1)S(1)}) custom-call(bf16[64,640]{1,0:T(8,128)(2,1)S(1)} %select_select_fusion.1.refs_0_, bf16[64,640]{1,0:T(8,128)(2,1)S(1)} %collective-permute-done.4.refs_1_, bf16[64,640]{1,0:T(8,128)(2,1)S(1)} %collective-permute-done.5.refs_2_, ...), custom_call_target="tpu_custom_call" | custom-call | flops 671088640 | tf_op jit(solution)/shard_map/project/pallas_call | solution.py:361
  36.3 1.3 %collective-permute-start.7 = (bf16[128,2048]{1,0:T(8,128)(2,1)S(1)}, bf16[128,2048]{1,0:T(8,128)(2,1)S(1)}, u32[]{:S(2)}, u32[]{:S(2)}) collective-permute-start(bf16[128,2048]{1,0:T(8,128)(2,1)S(1)} %get-tuple-element.27), channel_id=1, source_target_pairs={{0,4},{4,0},{1,5},{5,1},{2,6},{6,2},{3,7},{7,3},{8,12},{12,8},{9,1... | collective-permute-start | bytes 1572872 | tf_op jit(solution)/shard_map/ppermute | solution.py:562
  37.6 2.9 %fetch.5.refs_4_ = bf16[1600,2048]{1,0:T(8,128)(2,1)S(1)} custom-call(bf16[1600,2048]{1,0:T(8,128)(2,1)} %refs_0_.7), custom_call_target="tpu_custom_call" | custom-call | flops 268435456 | tf_op jit(solution)/shard_map/fetch/pallas_call | solution.py:294
  40.6 2.2 %collective-permute-done.18.refs_3_ = bf16[64,1600]{1,0:T(8,128)(2,1)S(1)} collective-permute-done((bf16[64,1600]{1,0:T(8,128)(2,1)S(1)}, bf16[64,1600]{1,0:T(8,128)(2,1)S(1)}, u32[]{:S(2)}, u32[]{:S(2)}) %collective-permute-start.18) | collective-permute-done | bytes 204832 | tf_op jit(solution)/shard_map/ppermute | solution.py:551
  42.8 1.1 %project.5 = bf16[128,2048]{1,0:T(8,128)(2,1)S(1)} custom-call(bf16[64,1600]{1,0:T(8,128)(2,1)S(1)} %select_select_fusion.refs_0_, bf16[64,1600]{1,0:T(8,128)(2,1)S(1)} %collective-permute-done.16.refs_1_, bf16[64,1600]{1,0:T(8,128)(2,1)S(1)} %collective-permute-done.17.refs_2_, bf16[64,1600]{1,0:T(8,128)(2,1)S(1)} %collective-permute-done.18.refs_3_, ...), custom_call_target="tpu_custom_call" | custom-call | flops 838860800 | tf_op jit(solution)/shard_map/project/pallas_call | solution.py:329
  44.0 0.0 copy-start
  44.0 1.4 %collective-permute-start.19 = (bf16[128,2048]{1,0:T(8,128)(2,1)S(1)}, bf16[128,2048]{1,0:T(8,128)(2,1)S(1)}, u32[]{:S(2)}, u32[]{:S(2)}) collective-permute-start(bf16[128,2048]{1,0:T(8,128)(2,1)S(1)} %project.5), channel_id=1, source_target_pairs={{0,4},{4,0},{1,5},{5,1},{2,6},{6,2},{3,7},{7,3},{8,12},{12,8},{9,1... | collective-permute-start | bytes 1572872 | tf_op jit(solution)/shard_map/ppermute | solution.py:562
  45.4 3.5 %fetch.4.weight = bf16[2048,2048]{1,0:T(8,128)(2,1)S(1)} custom-call(bf16[2048,2048]{1,0:T(8,128)(2,1)} %refs_0_.6), custom_call_target="tpu_custom_call" | custom-call | flops 268435456 | tf_op jit(solution)/shard_map/fetch/pallas_call | solution.py:294
  48.9 2.3 %collective-permute-done.7.other = bf16[128,2048]{1,0:T(8,128)(2,1)S(1)} collective-permute-done((bf16[128,2048]{1,0:T(8,128)(2,1)S(1)}, bf16[128,2048]{1,0:T(8,128)(2,1)S(1)}, u32[]{:S(2)}, u32[]{:S(2)}) %collective-permute-start.7) | collective-permute-done | bytes 524320 | tf_op jit(solution)/shard_map/ppermute | solution.py:562
  51.1 1.3 %heads.2 = (bf16[128,2048]{1,0:T(8,128)(2,1)S(1)}, f32[136,512]{1,0:T(8,128)S(1)}, bf16[136,512]{1,0:T(8,128)(2,1)S(1)}, bf16[136,512]{1,0:T(8,128)(2,1)S(1)}, bf16[136,512]{1,0:T(8,128)(2,1)S(1)}) custom-call(f32[128,2048]{1,0:T(8,128)S(1)} %get-tuple-element.26.keep, bf16[128,2048]{1,0:T(8,128)(2,1)S(1)} %collective-permute-done.7.other, ...), custom_call_target="tpu_custom_call" | custom-call | flops 1073741824 | tf_op jit(solution)/shard_map/heads/pallas_call | solution.py:404
  52.5 2.7 %collective-permute-start.25 = (bf16[128,2048]{1,0:T(8,128)(2,1)S(1)}, bf16[128,2048]{1,0:T(8,128)(2,1)S(1)}, u32[]{:S(2)}, u32[]{:S(2)}) collective-permute-start(bf16[128,2048]{1,0:T(8,128)(2,1)S(1)} %get-tuple-element.41.kept0), channel_id=1, source_target_pairs={{0,16},{8,24},{1,17},{9,25},{2,18},{10,26},{3,19},{11,27},{4,20},{... | collective-permute-start | bytes 1572872 | tf_op jit(solution)/shard_map/ppermute | solution.py:573
  55.2 1.1 %project.4.keep = f32[128,2048]{1,0:T(8,128)S(1)} custom-call(bf16[64,1600]{1,0:T(8,128)(2,1)S(1)} %select_select_fusion.refs_0_, bf16[64,1600]{1,0:T(8,128)(2,1)S(1)} %collective-permute-done.16.refs_1_, bf16[64,1600]{1,0:T(8,128)(2,1)S(1)} %collective-permute-done.17.refs_2_, bf16[64,1600]{1,0:T(8,128)(2,1)S(1)} %collective-permute-done.18.refs_3_, ...), custom_call_target="tpu_custom_call" | custom-call | flops 838860800 | tf_op jit(solution)/shard_map/project/pallas_call | solution.py:329
  56.3 0.1 collective-permute-start.8
  56.4 2.7 %collective-permute-start.9 = (bf16[136,512]{1,0:T(8,128)(2,1)S(1)}, bf16[136,512]{1,0:T(8,128)(2,1)S(1)}, u32[]{:S(2)}, u32[]{:S(2)}) collective-permute-start(bf16[136,512]{1,0:T(8,128)(2,1)S(1)} %get-tuple-element.30), channel_id=1, source_target_pairs={{0,2},{1,3},{2,0},{3,1},{4,6},{5,7},{6,4},{7,5},{8,10},{9,11},{10,... | collective-permute-start | bytes 417800 | tf_op jit(solution)/shard_map/ppermute | solution.py:571
  59.1 2.6 %collective-permute-start.10 = (bf16[136,512]{1,0:T(8,128)(2,1)S(1)}, bf16[136,512]{1,0:T(8,128)(2,1)S(1)}, u32[]{:S(2)}, u32[]{:S(2)}) collective-permute-start(bf16[136,512]{1,0:T(8,128)(2,1)S(1)} %get-tuple-element.31), channel_id=1, source_target_pairs={{0,3},{1,0},{2,1},{3,2},{4,7},{5,4},{6,5},{7,6},{8,11},{9,8},{10,9... | collective-permute-start | bytes 417800 | tf_op jit(solution)/shard_map/ppermute | solution.py:571
  61.7 1.3 %heads.3 = (bf16[128,2048]{1,0:T(8,128)(2,1)S(1)}, f32[136,512]{1,0:T(8,128)S(1)}, bf16[136,512]{1,0:T(8,128)(2,1)S(1)}, bf16[136,512]{1,0:T(8,128)(2,1)S(1)}, bf16[136,512]{1,0:T(8,128)(2,1)S(1)}) custom-call(f32[128,2048]{1,0:T(8,128)S(1)} %project.4.keep, bf16[128,2048]{1,0:T(8,128)(2,1)S(1)} %collective-permute-done.19.other, f32[2048]{0:T(1024)S(1)} %copy-done, ...), custom_call_target="tpu_custom_call" | custom-call | flops 1073741824 | tf_op jit(solution)/shard_map/heads/pallas_call | solution.py:404
  63.0 1.3 %collective-permute-start.24 = (bf16[128,2048]{1,0:T(8,128)(2,1)S(1)}, bf16[128,2048]{1,0:T(8,128)(2,1)S(1)}, u32[]{:S(2)}, u32[]{:S(2)}) collective-permute-start(bf16[128,2048]{1,0:T(8,128)(2,1)S(1)} %get-tuple-element.40.kept1), channel_id=1, source_target_pairs={{0,16},{8,24},{1,17},{9,25},{2,18},{10,26},{3,19},{11,27},{4,20},{... | collective-permute-start | bytes 1572872 | tf_op jit(solution)/shard_map/ppermute | solution.py:573
  64.4 0.2 collective-permute-start.20
  64.6 5.5 %collective-permute-done.9.refs_1_ = bf16[136,512]{1,0:T(8,128)(2,1)S(1)} collective-permute-done((bf16[136,512]{1,0:T(8,128)(2,1)S(1)}, bf16[136,512]{1,0:T(8,128)(2,1)S(1)}, u32[]{:S(2)}, u32[]{:S(2)}) %collective-permute-start.9) | collective-permute-done | bytes 139296 | tf_op jit(solution)/shard_map/ppermute | solution.py:571
  70.1 4.2 %collective-permute-start.22 = (bf16[136,512]{1,0:T(8,128)(2,1)S(1)}, bf16[136,512]{1,0:T(8,128)(2,1)S(1)}, u32[]{:S(2)}, u32[]{:S(2)}) collective-permute-start(bf16[136,512]{1,0:T(8,128)(2,1)S(1)} %get-tuple-element.39), channel_id=1, source_target_pairs={{0,3},{1,0},{2,1},{3,2},{4,7},{5,4},{6,5},{7,6},{8,11},{9,8},{10,9... | collective-permute-start | bytes 417800 | tf_op jit(solution)/shard_map/ppermute | solution.py:571
  74.3 0.2 finish.2
  74.5 3.2 %collective-permute-start.11 = (bf16[128,512]{1,0:T(8,128)(2,1)S(1)}, bf16[128,512]{1,0:T(8,128)(2,1)S(1)}, u32[]{:S(2)}, u32[]{:S(2)}) collective-permute-start(bf16[128,512]{1,0:T(8,128)(2,1)S(1)} %finish.2), channel_id=1, source_target_pairs={{0,16},{8,24},{1,17},{9,25},{2,18},{10,26},{3,19},{11,27},{4,20},{... | collective-permute-start | bytes 393224 | tf_op jit(solution)/shard_map/ppermute | solution.py:575
  77.8 1.1 %collective-permute-done.21.refs_1_ = bf16[136,512]{1,0:T(8,128)(2,1)S(1)} collective-permute-done((bf16[136,512]{1,0:T(8,128)(2,1)S(1)}, bf16[136,512]{1,0:T(8,128)(2,1)S(1)}, u32[]{:S(2)}, u32[]{:S(2)}) %collective-permute-start.21) | collective-permute-done | bytes 139296 | tf_op jit(solution)/shard_map/ppermute | solution.py:571
  78.9 0.2 finish.3
  79.1 2.3 %collective-permute-start.23 = (bf16[128,512]{1,0:T(8,128)(2,1)S(1)}, bf16[128,512]{1,0:T(8,128)(2,1)S(1)}, u32[]{:S(2)}, u32[]{:S(2)}) collective-permute-start(bf16[128,512]{1,0:T(8,128)(2,1)S(1)} %finish.3), channel_id=1, source_target_pairs={{0,16},{8,24},{1,17},{9,25},{2,18},{10,26},{3,19},{11,27},{4,20},{... | collective-permute-start | bytes 393224 | tf_op jit(solution)/shard_map/ppermute | solution.py:575
  81.4 1.4 %place.2.before = bf16[512,2048]{1,0:T(8,128)(2,1)} custom-call(bf16[128,2048]{1,0:T(8,128)(2,1)S(1)} %get-tuple-element.41.kept0, bf16[128,2048]{1,0:T(8,128)(2,1)S(1)} %get-tuple-element.40.kept1, bf16[128,2048]{1,0:T(8,128)(2,1)S(1)} %collective-permute-done.25.moved0), custom_call_target="tpu_custom_call" | custom-call | flops 67108864 | tf_op jit(solution)/shard_map/place/pallas_call | solution.py:473
  82.8 1.1 %collective-permute-done.23 = bf16[128,512]{1,0:T(8,128)(2,1)S(1)} collective-permute-done((bf16[128,512]{1,0:T(8,128)(2,1)S(1)}, bf16[128,512]{1,0:T(8,128)(2,1)S(1)}, u32[]{:S(2)}, u32[]{:S(2)}) %collective-permute-start.23) | collective-permute-done | bytes 131104 | tf_op jit(solution)/shard_map/ppermute | solution.py:575
  83.8 0.9 %maximum_select_fusion = bf16[1,512,512]{2,1,0:T(8,128)(2,1)} fusion(bf16[1,128,512]{2,1,0:T(8,128)(2,1)S(1)} %bitcast.6, bf16[1,128,512]{2,1,0:T(8,128)(2,1)S(1)} %bitcast.9, bf16[1,128,512]{2,1,0:T(8,128)(2,1)S(1)} %bitcast.5, bf16[1,128,512]{2,1,0:T(8,128)(2,1)S(1)} %bitcast.8, pred[]{:T(512)S(6)} %ge.3), kind=kLoop, calls=%fused_computation | loop fusion | flops 2359296 | bytes 1048577 | tf_op jit(solution)/shard_map/jit(_where)/select_n | solution.py:579
  (22 shorter events, 0.1 us)
Async XLA Ops:
  2.0 10.8 %collective-permute-start.12 = (bf16[64,1600]{1,0:T(8,128)(2,1)S(1)}, bf16[64,1600]{1,0:T(8,128)(2,1)S(1)}, u32[]{:S(2)}, u32[]{:S(2)}) collective-permute-start(bf16[64,1600]{1,0:T(8,128)(2,1)S(1)} %get-tuple-element.32), channel_id=1, source_target_pairs={{8,12},{12,28},{9,13},{13,29},{10,14},{14,30},{11,15},{15,31}} | collective-permute-start | bytes 614408 | tf_op jit(solution)/shard_map/ppermute | solution.py:546
  2.7 11.4 %collective-permute-start.13 = (bf16[64,1600]{1,0:T(8,128)(2,1)S(1)}, bf16[64,1600]{1,0:T(8,128)(2,1)S(1)}, u32[]{:S(2)}, u32[]{:S(2)}) collective-permute-start(bf16[64,1600]{1,0:T(8,128)(2,1)S(1)} %get-tuple-element.33), channel_id=1, source_target_pairs={{8,8},{12,24},{9,9},{13,25},{10,10},{14,26},{11,11},{15,27}} | collective-permute-start | bytes 614408 | tf_op jit(solution)/shard_map/ppermute | solution.py:546
  3.4 12.0 %collective-permute-start.14 = (bf16[64,1600]{1,0:T(8,128)(2,1)S(1)}, bf16[64,1600]{1,0:T(8,128)(2,1)S(1)}, u32[]{:S(2)}, u32[]{:S(2)}) collective-permute-start(bf16[64,1600]{1,0:T(8,128)(2,1)S(1)} %get-tuple-element.34), channel_id=1, source_target_pairs={{8,4},{12,20},{9,5},{13,21},{10,6},{14,22},{11,7},{15,23}} | collective-permute-start | bytes 614408 | tf_op jit(solution)/shard_map/ppermute | solution.py:546
  4.1 12.0 %collective-permute-start.15 = (bf16[64,1600]{1,0:T(8,128)(2,1)S(1)}, bf16[64,1600]{1,0:T(8,128)(2,1)S(1)}, u32[]{:S(2)}, u32[]{:S(2)}) collective-permute-start(bf16[64,1600]{1,0:T(8,128)(2,1)S(1)} %get-tuple-element.35), channel_id=1, source_target_pairs={{8,0},{12,16},{9,1},{13,17},{10,2},{14,18},{11,3},{15,19}} | collective-permute-start | bytes 614408 | tf_op jit(solution)/shard_map/ppermute | solution.py:546
  5.4 13.5 %collective-permute-start = (bf16[64,640]{1,0:T(8,128)(2,1)S(1)}, bf16[64,640]{1,0:T(8,128)(2,1)S(1)}, u32[]{:S(2)}, u32[]{:S(2)}) collective-permute-start(bf16[64,640]{1,0:T(8,128)(2,1)S(1)} %get-tuple-element.22), channel_id=1, source_target_pairs={{0,12},{4,28},{1,13},{5,29},{2,14},{6,30},{3,15},{7,31}} | collective-permute-start | bytes 245768 | tf_op jit(solution)/shard_map/ppermute | solution.py:546
  12.8 6.0 %collective-permute-start.1 = (bf16[64,640]{1,0:T(8,128)(2,1)S(1)}, bf16[64,640]{1,0:T(8,128)(2,1)S(1)}, u32[]{:S(2)}, u32[]{:S(2)}) collective-permute-start(bf16[64,640]{1,0:T(8,128)(2,1)S(1)} %get-tuple-element.23), channel_id=1, source_target_pairs={{0,8},{4,24},{1,9},{5,25},{2,10},{6,26},{3,11},{7,27}} | collective-permute-start | bytes 245768 | tf_op jit(solution)/shard_map/ppermute | solution.py:546
  14.1 4.7 %collective-permute-start.2 = (bf16[64,640]{1,0:T(8,128)(2,1)S(1)}, bf16[64,640]{1,0:T(8,128)(2,1)S(1)}, u32[]{:S(2)}, u32[]{:S(2)}) collective-permute-start(bf16[64,640]{1,0:T(8,128)(2,1)S(1)} %get-tuple-element.24), channel_id=1, source_target_pairs={{0,4},{4,20},{1,5},{5,21},{2,6},{6,22},{3,7},{7,23}} | collective-permute-start | bytes 245768 | tf_op jit(solution)/shard_map/ppermute | solution.py:546
  15.4 3.4 %collective-permute-start.3 = (bf16[64,640]{1,0:T(8,128)(2,1)S(1)}, bf16[64,640]{1,0:T(8,128)(2,1)S(1)}, u32[]{:S(2)}, u32[]{:S(2)}) collective-permute-start(bf16[64,640]{1,0:T(8,128)(2,1)S(1)} %get-tuple-element.25), channel_id=1, source_target_pairs={{0,0},{4,16},{1,1},{5,17},{2,2},{6,18},{3,3},{7,19}} | collective-permute-start | bytes 245768 | tf_op jit(solution)/shard_map/ppermute | solution.py:546
  16.2 15.8 %collective-permute-start.17 = (bf16[64,1600]{1,0:T(8,128)(2,1)S(1)}, bf16[64,1600]{1,0:T(8,128)(2,1)S(1)}, u32[]{:S(2)}, u32[]{:S(2)}) collective-permute-start(bf16[64,1600]{1,0:T(8,128)(2,1)S(1)} %select_select_fusion.refs_0_), channel_id=1, source_target_pairs={{0,2},{1,3},{2,0},{3,1},{4,6},{5,7},{6,4},{7,5},{8,10},{9,11},{10,... | collective-permute-start | bytes 614408 | tf_op jit(solution)/shard_map/ppermute | solution.py:551
  18.9 11.1 %collective-permute-start.5 = (bf16[64,640]{1,0:T(8,128)(2,1)S(1)}, bf16[64,640]{1,0:T(8,128)(2,1)S(1)}, u32[]{:S(2)}, u32[]{:S(2)}) collective-permute-start(bf16[64,640]{1,0:T(8,128)(2,1)S(1)} %select_select_fusion.1.refs_0_), channel_id=1, source_target_pairs={{0,2},{1,3},{2,0},{3,1},{4,6},{5,7},{6,4},{7,5},{8,10},{9,11},{10,... | collective-permute-start | bytes 245768 | tf_op jit(solution)/shard_map/ppermute | solution.py:551
  20.1 14.3 %collective-permute-start.4 = (bf16[64,640]{1,0:T(8,128)(2,1)S(1)}, bf16[64,640]{1,0:T(8,128)(2,1)S(1)}, u32[]{:S(2)}, u32[]{:S(2)}) collective-permute-start(bf16[64,640]{1,0:T(8,128)(2,1)S(1)} %select_select_fusion.1.refs_0_), channel_id=1, source_target_pairs={{0,1},{1,0},{2,3},{3,2},{4,5},{5,4},{6,7},{7,6},{8,9},{9,8},{10,11... | collective-permute-start | bytes 245768 | tf_op jit(solution)/shard_map/ppermute | solution.py:551
  30.0 5.3 %collective-permute-start.6 = (bf16[64,640]{1,0:T(8,128)(2,1)S(1)}, bf16[64,640]{1,0:T(8,128)(2,1)S(1)}, u32[]{:S(2)}, u32[]{:S(2)}) collective-permute-start(bf16[64,640]{1,0:T(8,128)(2,1)S(1)} %collective-permute-done.5.refs_2_), channel_id=1, source_target_pairs={{0,1},{1,0},{2,3},{3,2},{4,5},{5,4},{6,7},{7,6},{8,9},{9,8},{10,11... | collective-permute-start | bytes 245768 | tf_op jit(solution)/shard_map/ppermute | solution.py:551
  30.7 9.9 %collective-permute-start.16 = (bf16[64,1600]{1,0:T(8,128)(2,1)S(1)}, bf16[64,1600]{1,0:T(8,128)(2,1)S(1)}, u32[]{:S(2)}, u32[]{:S(2)}) collective-permute-start(bf16[64,1600]{1,0:T(8,128)(2,1)S(1)} %select_select_fusion.refs_0_), channel_id=1, source_target_pairs={{0,1},{1,0},{2,3},{3,2},{4,5},{5,4},{6,7},{7,6},{8,9},{9,8},{10,11... | collective-permute-start | bytes 614408 | tf_op jit(solution)/shard_map/ppermute | solution.py:551
  32.0 10.8 %collective-permute-start.18 = (bf16[64,1600]{1,0:T(8,128)(2,1)S(1)}, bf16[64,1600]{1,0:T(8,128)(2,1)S(1)}, u32[]{:S(2)}, u32[]{:S(2)}) collective-permute-start(bf16[64,1600]{1,0:T(8,128)(2,1)S(1)} %collective-permute-done.17.refs_2_), channel_id=1, source_target_pairs={{0,1},{1,0},{2,3},{3,2},{4,5},{5,4},{6,7},{7,6},{8,9},{9,8},{10,11... | collective-permute-start | bytes 614408 | tf_op jit(solution)/shard_map/ppermute | solution.py:551
  36.3 14.9 %collective-permute-start.7 = (bf16[128,2048]{1,0:T(8,128)(2,1)S(1)}, bf16[128,2048]{1,0:T(8,128)(2,1)S(1)}, u32[]{:S(2)}, u32[]{:S(2)}) collective-permute-start(bf16[128,2048]{1,0:T(8,128)(2,1)S(1)} %get-tuple-element.27), channel_id=1, source_target_pairs={{0,4},{4,0},{1,5},{5,1},{2,6},{6,2},{3,7},{7,3},{8,12},{12,8},{9,1... | collective-permute-start | bytes 1572872 | tf_op jit(solution)/shard_map/ppermute | solution.py:562
  44.0 7.2 %copy-start = (f32[2048]{0:T(1024)S(1)}, f32[2048]{0:T(1024)}, u32[]{:S(2)}) copy-start(f32[2048]{0:T(1024)} %gain.3) | copy-start | bytes 24580
  44.0 17.7 %collective-permute-start.19 = (bf16[128,2048]{1,0:T(8,128)(2,1)S(1)}, bf16[128,2048]{1,0:T(8,128)(2,1)S(1)}, u32[]{:S(2)}, u32[]{:S(2)}) collective-permute-start(bf16[128,2048]{1,0:T(8,128)(2,1)S(1)} %project.5), channel_id=1, source_target_pairs={{0,4},{4,0},{1,5},{5,1},{2,6},{6,2},{3,7},{7,3},{8,12},{12,8},{9,1... | collective-permute-start | bytes 1572872 | tf_op jit(solution)/shard_map/ppermute | solution.py:562
  52.5 28.9 %collective-permute-start.25 = (bf16[128,2048]{1,0:T(8,128)(2,1)S(1)}, bf16[128,2048]{1,0:T(8,128)(2,1)S(1)}, u32[]{:S(2)}, u32[]{:S(2)}) collective-permute-start(bf16[128,2048]{1,0:T(8,128)(2,1)S(1)} %get-tuple-element.41.kept0), channel_id=1, source_target_pairs={{0,16},{8,24},{1,17},{9,25},{2,18},{10,26},{3,19},{11,27},{4,20},{... | collective-permute-start | bytes 1572872 | tf_op jit(solution)/shard_map/ppermute | solution.py:573
  56.3 8.1 %collective-permute-start.8 = (bf16[136,512]{1,0:T(8,128)(2,1)S(1)}, bf16[136,512]{1,0:T(8,128)(2,1)S(1)}, u32[]{:S(2)}, u32[]{:S(2)}) collective-permute-start(bf16[136,512]{1,0:T(8,128)(2,1)S(1)} %get-tuple-element.29), channel_id=1, source_target_pairs={{0,1},{1,2},{2,3},{3,0},{4,5},{5,6},{6,7},{7,4},{8,9},{9,10},{10,1... | collective-permute-start | bytes 417800 | tf_op jit(solution)/shard_map/ppermute | solution.py:571
  56.4 13.8 %collective-permute-start.9 = (bf16[136,512]{1,0:T(8,128)(2,1)S(1)}, bf16[136,512]{1,0:T(8,128)(2,1)S(1)}, u32[]{:S(2)}, u32[]{:S(2)}) collective-permute-start(bf16[136,512]{1,0:T(8,128)(2,1)S(1)} %get-tuple-element.30), channel_id=1, source_target_pairs={{0,2},{1,3},{2,0},{3,1},{4,6},{5,7},{6,4},{7,5},{8,10},{9,11},{10,... | collective-permute-start | bytes 417800 | tf_op jit(solution)/shard_map/ppermute | solution.py:571
  59.1 11.1 %collective-permute-start.10 = (bf16[136,512]{1,0:T(8,128)(2,1)S(1)}, bf16[136,512]{1,0:T(8,128)(2,1)S(1)}, u32[]{:S(2)}, u32[]{:S(2)}) collective-permute-start(bf16[136,512]{1,0:T(8,128)(2,1)S(1)} %get-tuple-element.31), channel_id=1, source_target_pairs={{0,3},{1,0},{2,1},{3,2},{4,7},{5,4},{6,5},{7,6},{8,11},{9,8},{10,9... | collective-permute-start | bytes 417800 | tf_op jit(solution)/shard_map/ppermute | solution.py:571
  63.0 21.7 %collective-permute-start.24 = (bf16[128,2048]{1,0:T(8,128)(2,1)S(1)}, bf16[128,2048]{1,0:T(8,128)(2,1)S(1)}, u32[]{:S(2)}, u32[]{:S(2)}) collective-permute-start(bf16[128,2048]{1,0:T(8,128)(2,1)S(1)} %get-tuple-element.40.kept1), channel_id=1, source_target_pairs={{0,16},{8,24},{1,17},{9,25},{2,18},{10,26},{3,19},{11,27},{4,20},{... | collective-permute-start | bytes 1572872 | tf_op jit(solution)/shard_map/ppermute | solution.py:573
  64.4 10.2 %collective-permute-start.20 = (bf16[136,512]{1,0:T(8,128)(2,1)S(1)}, bf16[136,512]{1,0:T(8,128)(2,1)S(1)}, u32[]{:S(2)}, u32[]{:S(2)}) collective-permute-start(bf16[136,512]{1,0:T(8,128)(2,1)S(1)} %get-tuple-element.37), channel_id=1, source_target_pairs={{0,1},{1,2},{2,3},{3,0},{4,5},{5,6},{6,7},{7,4},{8,9},{9,10},{10,1... | collective-permute-start | bytes 417800 | tf_op jit(solution)/shard_map/ppermute | solution.py:571
  70.1 8.7 %collective-permute-start.21 = (bf16[136,512]{1,0:T(8,128)(2,1)S(1)}, bf16[136,512]{1,0:T(8,128)(2,1)S(1)}, u32[]{:S(2)}, u32[]{:S(2)}) collective-permute-start(bf16[136,512]{1,0:T(8,128)(2,1)S(1)} %get-tuple-element.38), channel_id=1, source_target_pairs={{0,2},{1,3},{2,0},{3,1},{4,6},{5,7},{6,4},{7,5},{8,10},{9,11},{10,... | collective-permute-start | bytes 417800 | tf_op jit(solution)/shard_map/ppermute | solution.py:571
  70.1 8.7 %collective-permute-start.22 = (bf16[136,512]{1,0:T(8,128)(2,1)S(1)}, bf16[136,512]{1,0:T(8,128)(2,1)S(1)}, u32[]{:S(2)}, u32[]{:S(2)}) collective-permute-start(bf16[136,512]{1,0:T(8,128)(2,1)S(1)} %get-tuple-element.39), channel_id=1, source_target_pairs={{0,3},{1,0},{2,1},{3,2},{4,7},{5,4},{6,5},{7,6},{8,11},{9,8},{10,9... | collective-permute-start | bytes 417800 | tf_op jit(solution)/shard_map/ppermute | solution.py:571
  74.5 8.2 %collective-permute-start.11 = (bf16[128,512]{1,0:T(8,128)(2,1)S(1)}, bf16[128,512]{1,0:T(8,128)(2,1)S(1)}, u32[]{:S(2)}, u32[]{:S(2)}) collective-permute-start(bf16[128,512]{1,0:T(8,128)(2,1)S(1)} %finish.2), channel_id=1, source_target_pairs={{0,16},{8,24},{1,17},{9,25},{2,18},{10,26},{3,19},{11,27},{4,20},{... | collective-permute-start | bytes 393224 | tf_op jit(solution)/shard_map/ppermute | solution.py:575
  79.1 4.8 %collective-permute-start.23 = (bf16[128,512]{1,0:T(8,128)(2,1)S(1)}, bf16[128,512]{1,0:T(8,128)(2,1)S(1)}, u32[]{:S(2)}, u32[]{:S(2)}) collective-permute-start(bf16[128,512]{1,0:T(8,128)(2,1)S(1)} %finish.3), channel_id=1, source_target_pairs={{0,16},{8,24},{1,17},{9,25},{2,18},{10,26},{3,19},{11,27},{4,20},{... | collective-permute-start | bytes 393224 | tf_op jit(solution)/shard_map/ppermute | solution.py:575

commit v7 on v6

--- a/solution.py
+++ b/solution.py
@@ -171,6 +171,7 @@
 
 
 MIB = 1 << 20
+LANES = 128
 
 
 class Place:
@@ -375,27 +376,25 @@
 def heads_kernel(mp_count, keep, other, gain, weight, tokens, own, *rest):
     meta = Place()
     sends, scaled = rest[:-1], rest[-1]
-    rows, tile = own.shape[0] - 8, own.shape[1]
+    rows, tile = tokens.shape[0], weight.shape[1] // mp_count
     rounded = (keep[...] + other[...].astype(jnp.float32)).astype(jnp.bfloat16)
     tokens[...] = rounded
     values = rounded.astype(jnp.float32)
     scaled[...] = (values * gain[...].reshape(1, -1)).astype(jnp.bfloat16)
     total = jnp.sum(values * values, axis=1, keepdims=True)
-    turned = jnp.transpose(jnp.broadcast_to(total, (rows, 128)))[:8]
+    turned = jnp.transpose(jnp.broadcast_to(total, (rows, LANES)))[:8]
     high = turned.astype(jnp.bfloat16).astype(jnp.float32)
     line = lax.broadcasted_iota(jnp.int32, turned.shape, 0)
     packed = jnp.where(line == 0, high, jnp.where(line == 1, turned - high, 0.0))
-    packed = jnp.concatenate([packed] + [jnp.zeros((8, tile - rows), jnp.float32)], axis=1)
     for shift in list(range(1, mp_count)) + [0]:
         chunk = lax.rem(meta[2] + shift, mp_count)
         columns = pl.ds(pl.multiple_of(chunk * tile, tile), tile)
         out = jnp.dot(scaled[...], weight[:, columns], preferred_element_type=jnp.float32)
-        if shift:
-            block = jnp.concatenate([out, packed], axis=0)
-            sends[shift - 1][...] = block.astype(jnp.bfloat16)
-        else:
-            own[:rows, :] = out
-            own[rows:, :] = packed
+        place = sends[shift - 1] if shift else own
+        for q in range(tile // LANES):
+            part = out[:, q * LANES : (q + 1) * LANES]
+            place[q * rows : (q + 1) * rows, :] = part.astype(place.dtype)
+        place[rows * tile // LANES :, :] = packed.astype(place.dtype)
 
 
 def heads(mp_count, keep, other, gain, weight):
@@ -408,9 +407,9 @@
         scratch_shapes=[pltpu.VMEM((rows, width), jnp.bfloat16)],
         out_shape=[
             jax.ShapeDtypeStruct((rows, width), jnp.bfloat16),
-            jax.ShapeDtypeStruct((rows + 8, tile), jnp.float32),
+            jax.ShapeDtypeStruct((rows * tile // LANES + 8, LANES), jnp.float32),
         ]
-        + [jax.ShapeDtypeStruct((rows + 8, tile), jnp.bfloat16)] * (mp_count - 1),
+        + [jax.ShapeDtypeStruct((rows * tile // LANES + 8, LANES), jnp.bfloat16)] * (mp_count - 1),
         name="heads",
         **limits_of(14, 2 * rows * width * weight.shape[1]),
     )(keep, other, gain, weight)
@@ -422,17 +421,20 @@
     total = own[...]
     for part in parts:
         total = total + part[...].astype(jnp.float32)
-    square = total[rows : rows + 1, :rows] + total[rows + 1 : rows + 2, :rows]
+    last = total.shape[0] - 8
+    square = total[last : last + 1] + total[last + 1 : last + 2]
     scale = lax.rsqrt(square / full_width + EPS_ROOT)
-    column = jnp.transpose(jnp.broadcast_to(scale, (128, rows)))[:, :1]
-    result[...] = (total[:rows] * column).astype(jnp.bfloat16)
-
-
-def finish(full_width, own, parts):
-    rows, tile = own.shape
+    column = jnp.transpose(jnp.broadcast_to(scale, (LANES, rows)))[:, :1]
+    for q in range(last // rows):
+        part = total[q * rows : (q + 1) * rows] * column
+        result[:, q * LANES : (q + 1) * LANES] = part.astype(jnp.bfloat16)
+
+
+def finish(full_width, rows, own, parts):
+    tile = (own.shape[0] - 8) // rows * LANES
     return pl.pallas_call(
         functools.partial(finish_kernel, full_width),
-        out_shape=jax.ShapeDtypeStruct((rows - 8, tile), jnp.bfloat16),
+        out_shape=jax.ShapeDtypeStruct((rows, tile), jnp.bfloat16),
         in_specs=[vmem()] * (1 + len(parts)),
         out_specs=vmem(),
         name="finish",
@@ -527,7 +529,6 @@
         spreads = [[(i, i ^ step) for i in range(mp_count)] for step in (0, 1, 2, 1)]
     swap = [(i, (i + 1) % dp_count) for i in range(dp_count)]
     up = [(0, 2), (1, 3)]
-    on_backbone = group >= 2
     full_width = input_gain.shape[0] * mp_count
     targets = 2 * dp_count
     streams = (
@@ -571,12 +572,12 @@
             sums.append(lax.ppermute(part, "mp", rings[shift]))
         kept.append(tokens)
         moved.append(lax.ppermute(tokens, "group", up))
-        values = finish(full_width, own, sums)
+        values = finish(full_width, tokens.shape[0], own, sums)
         head_parts += [lax.ppermute(values, "group", up), values]
     rows_out = place_early(kept, moved[0])
     rows_out = place_late(moved[1], rows_out)
-    heads_out = jnp.concatenate(head_parts, axis=0)
-    heads_out = jnp.where(on_backbone, heads_out, jnp.zeros_like(heads_out))
+    heads_out = place_early([head_parts[1], head_parts[3]], head_parts[0])
+    heads_out = place_late(head_parts[2], heads_out)
     return (heads_out[None], rows_out[None])
 
 

time: 85.9 us -> 97.6 us (1.14)
  waiting for transfers between devices: 21.4 us -> 30 us
  starting transfers between devices: 44.2 us -> 46.8 us
    ppermute x2, waiting for transfers between devices: 2.29 us -> 8.96 us  [shards_direct(): others.append(lax.ppermute(send, 'dp', swap))]
    ppermute x6, starting transfers between devices: 9.81 us -> 15.1 us  [shards_direct(): sums.append(lax.ppermute(part, 'mp', rings[shift]))]
    ppermute x2, starting transfers between devices: 5.47 us -> 2.59 us  [shards_direct(): head_parts += [lax.ppermute(values, 'group', up), values]]
    ppermute x6, waiting for transfers between devices: 6.65 us -> 8.02 us  [shards_direct(): sums.append(lax.ppermute(part, 'mp', rings[shift]))]
    ppermute x6, waiting for transfers between devices: 11.4 us -> 12.7 us  [shards_direct(): pieces.append(lax.ppermute(sent, 'mp', spreads[shift]))]
    pallas_call x1 -> x2, Pallas kernels: 1.39 us -> 2.24 us  [place_early(): pl.pallas_call(place_early_kernel, out_shape=pltpu.HBM((BLOCKS * rows, wi...]
  transfers between devices with their start and end apart: 26 -> 26, of which waited for: 7 -> 10; matrix products, arithmetic and copies ran while one was open for 1% -> 0% of each run, Pallas kernels for 19% -> 17%
where the time goes in v7:
time: 97.6 us; the launch traced here: 95.9 us
  starting transfers between devices  46.8 us (48%)
  waiting for transfers between devices  30 us (31%)
  Pallas kernels  18.1 us (19%)
  between operations  0.98 us (1%)
    ppermute x6, starting transfers between devices, shards_direct(): sums.append(lax.ppermute(part, 'mp', rings[shift]))  15.1 us
    ppermute x8, starting transfers between devices, shards_direct(): lax.ppermute(messages[stream * targets + index], ('group', 'dp'), pairs)  14 us
    ppermute x6, waiting for transfers between devices, shards_direct(): pieces.append(lax.ppermute(sent, 'mp', spreads[shift]))  12.7 us
    ppermute x2, waiting for transfers between devices, shards_direct(): others.append(lax.ppermute(send, 'dp', swap))  8.96 us
    pallas_call x3, Pallas kernels, fetch(): pl.pallas_call(functools.partial(fetch_kernel, cuts), out_shape=[pltpu.VM...  8.13 us
    ppermute x6, waiting for transfers between devices, shards_direct(): sums.append(lax.ppermute(part, 'mp', rings[shift]))  8.02 us
    ppermute x6, starting transfers between devices, shards_direct(): pieces.append(lax.ppermute(sent, 'mp', spreads[shift]))  7.54 us
    ppermute x2, starting transfers between devices, shards_direct(): moved.append(lax.ppermute(tokens, 'group', up))  4.91 us
  transfers between devices with their start and end apart: 26, of which 10 were waited for; matrix products, arithmetic and copies ran while one was open for 0% of the time, Pallas kernels for 17%

profile of v7, /device:TPU:0, one launch (start us, length us, event | category | flops | bytes accessed | tf_op | source)
XLA Modules:
  0.0 95.9 jit_solution(10478005373276666473)
XLA Ops:
  0.6 1.4 %encode.1 = (bf16[64,640]{1,0:T(8,128)(2,1)S(1)}, bf16[64,640]{1,0:T(8,128)(2,1)S(1)}, bf16[64,640]{1,0:T(8,128)(2,1)S(1)}, bf16[64,640]{1,0:T(8,128)(2,1)S(1)},...) custom-call(s32[2,2,4]{2,1,0:T(2,128)} %dest.1, ...), custom_call_target="tpu_custom_call" | custom-call | flops 268435456 | tf_op jit(solution)/shard_map/encode/pallas_call | solution.py:266
  2.0 0.7 collective-permute-start
  2.7 0.7 collective-permute-start.1
  3.4 0.7 collective-permute-start.2
  4.1 1.3 %collective-permute-start.3 = (bf16[64,1600]{1,0:T(8,128)(2,1)S(1)}, bf16[64,1600]{1,0:T(8,128)(2,1)S(1)}, u32[]{:S(2)}, u32[]{:S(2)}) collective-permute-start(bf16[64,1600]{1,0:T(8,128)(2,1)S(1)} %get-tuple-element.25), channel_id=1, source_target_pairs={{8,0},{12,16},{9,1},{13,17},{10,2},{14,18},{11,3},{15,19}} | collective-permute-start | bytes 614408 | tf_op jit(solution)/shard_map/ppermute | solution.py:547
  5.4 7.4 %collective-permute-start.12 = (bf16[64,640]{1,0:T(8,128)(2,1)S(1)}, bf16[64,640]{1,0:T(8,128)(2,1)S(1)}, u32[]{:S(2)}, u32[]{:S(2)}) collective-permute-start(bf16[64,640]{1,0:T(8,128)(2,1)S(1)} %get-tuple-element.30), channel_id=1, source_target_pairs={{0,12},{4,28},{1,13},{5,29},{2,14},{6,30},{3,15},{7,31}} | collective-permute-start | bytes 245768 | tf_op jit(solution)/shard_map/ppermute | solution.py:547
  12.8 1.3 %collective-permute-start.13 = (bf16[64,640]{1,0:T(8,128)(2,1)S(1)}, bf16[64,640]{1,0:T(8,128)(2,1)S(1)}, u32[]{:S(2)}, u32[]{:S(2)}) collective-permute-start(bf16[64,640]{1,0:T(8,128)(2,1)S(1)} %get-tuple-element.31), channel_id=1, source_target_pairs={{0,8},{4,24},{1,9},{5,25},{2,10},{6,26},{3,11},{7,27}} | collective-permute-start | bytes 245768 | tf_op jit(solution)/shard_map/ppermute | solution.py:547
  14.1 1.3 %collective-permute-start.14 = (bf16[64,640]{1,0:T(8,128)(2,1)S(1)}, bf16[64,640]{1,0:T(8,128)(2,1)S(1)}, u32[]{:S(2)}, u32[]{:S(2)}) collective-permute-start(bf16[64,640]{1,0:T(8,128)(2,1)S(1)} %get-tuple-element.32), channel_id=1, source_target_pairs={{0,4},{4,20},{1,5},{5,21},{2,6},{6,22},{3,7},{7,23}} | collective-permute-start | bytes 245768 | tf_op jit(solution)/shard_map/ppermute | solution.py:547
  15.4 0.7 collective-permute-start.15
  16.2 2.7 %collective-permute-start.5 = (bf16[64,1600]{1,0:T(8,128)(2,1)S(1)}, bf16[64,1600]{1,0:T(8,128)(2,1)S(1)}, u32[]{:S(2)}, u32[]{:S(2)}) collective-permute-start(bf16[64,1600]{1,0:T(8,128)(2,1)S(1)} %select_select_fusion.refs_0_), channel_id=1, source_target_pairs={{0,2},{1,3},{2,0},{3,1},{4,6},{5,7},{6,4},{7,5},{8,10},{9,11},{10,... | collective-permute-start | bytes 614408 | tf_op jit(solution)/shard_map/ppermute | solution.py:552
  18.9 1.3 %collective-permute-start.17 = (bf16[64,640]{1,0:T(8,128)(2,1)S(1)}, bf16[64,640]{1,0:T(8,128)(2,1)S(1)}, u32[]{:S(2)}, u32[]{:S(2)}) collective-permute-start(bf16[64,640]{1,0:T(8,128)(2,1)S(1)} %select_select_fusion.1.refs_0_), channel_id=1, source_target_pairs={{0,2},{1,3},{2,0},{3,1},{4,6},{5,7},{6,4},{7,5},{8,10},{9,11},{10,... | collective-permute-start | bytes 245768 | tf_op jit(solution)/shard_map/ppermute | solution.py:552
  20.1 1.6 %collective-permute-start.4 = (bf16[64,1600]{1,0:T(8,128)(2,1)S(1)}, bf16[64,1600]{1,0:T(8,128)(2,1)S(1)}, u32[]{:S(2)}, u32[]{:S(2)}) collective-permute-start(bf16[64,1600]{1,0:T(8,128)(2,1)S(1)} %select_select_fusion.refs_0_), channel_id=1, source_target_pairs={{0,1},{1,0},{2,3},{3,2},{4,5},{5,4},{6,7},{7,6},{8,9},{9,8},{10,11... | collective-permute-start | bytes 614408 | tf_op jit(solution)/shard_map/ppermute | solution.py:552
  21.7 7.5 %collective-permute-done.5.refs_2_ = bf16[64,1600]{1,0:T(8,128)(2,1)S(1)} collective-permute-done((bf16[64,1600]{1,0:T(8,128)(2,1)S(1)}, bf16[64,1600]{1,0:T(8,128)(2,1)S(1)}, u32[]{:S(2)}, u32[]{:S(2)}) %collective-permute-start.5) | collective-permute-done | bytes 204832 | tf_op jit(solution)/shard_map/ppermute | solution.py:552
  29.2 2.0 %collective-permute-start.16 = (bf16[64,640]{1,0:T(8,128)(2,1)S(1)}, bf16[64,640]{1,0:T(8,128)(2,1)S(1)}, u32[]{:S(2)}, u32[]{:S(2)}) collective-permute-start(bf16[64,640]{1,0:T(8,128)(2,1)S(1)} %select_select_fusion.1.refs_0_), channel_id=1, source_target_pairs={{0,1},{1,0},{2,3},{3,2},{4,5},{5,4},{6,7},{7,6},{8,9},{9,8},{10,11... | collective-permute-start | bytes 245768 | tf_op jit(solution)/shard_map/ppermute | solution.py:552
  31.2 0.0 collective-permute-start.18
  31.3 1.7 %fetch.5.refs_4_ = bf16[640,2048]{1,0:T(8,128)(2,1)S(1)} custom-call(bf16[640,2048]{1,0:T(8,128)(2,1)} %refs_0_.7), custom_call_target="tpu_custom_call" | custom-call | flops 268435456 | tf_op jit(solution)/shard_map/fetch/pallas_call | solution.py:295
  33.0 4.4 %collective-permute-done.16.refs_1_ = bf16[64,640]{1,0:T(8,128)(2,1)S(1)} collective-permute-done((bf16[64,640]{1,0:T(8,128)(2,1)S(1)}, bf16[64,640]{1,0:T(8,128)(2,1)S(1)}, u32[]{:S(2)}, u32[]{:S(2)}) %collective-permute-start.16) | collective-permute-done | bytes 81952 | tf_op jit(solution)/shard_map/ppermute | solution.py:552
  37.3 0.9 collective-permute-done.18.refs_3_
  38.2 1.0 %project.5 = (f32[128,2048]{1,0:T(8,128)S(1)}, bf16[128,2048]{1,0:T(8,128)(2,1)S(1)}) custom-call(bf16[64,640]{1,0:T(8,128)(2,1)S(1)} %select_select_fusion.1.refs_0_, bf16[64,640]{1,0:T(8,128)(2,1)S(1)} %collective-permute-done.16.refs_1_, bf16[64,640]{1,0:T(8,128)(2,1)S(1)} %collective-permute-done.17.refs_2_, ...), custom_call_target="tpu_custom_call" | custom-call | flops 671088640 | tf_op jit(solution)/shard_map/project/pallas_call | solution.py:362
  39.2 2.6 %collective-permute-start.19 = (bf16[128,2048]{1,0:T(8,128)(2,1)S(1)}, bf16[128,2048]{1,0:T(8,128)(2,1)S(1)}, u32[]{:S(2)}, u32[]{:S(2)}) collective-permute-start(bf16[128,2048]{1,0:T(8,128)(2,1)S(1)} %get-tuple-element.35), channel_id=1, source_target_pairs={{0,4},{4,0},{1,5},{5,1},{2,6},{6,2},{3,7},{7,3},{8,12},{12,8},{9,1... | collective-permute-start | bytes 1572872 | tf_op jit(solution)/shard_map/ppermute | solution.py:563
  41.8 2.9 %fetch.3.refs_4_ = bf16[1600,2048]{1,0:T(8,128)(2,1)S(1)} custom-call(bf16[1600,2048]{1,0:T(8,128)(2,1)} %refs_0_.5), custom_call_target="tpu_custom_call" | custom-call | flops 268435456 | tf_op jit(solution)/shard_map/fetch/pallas_call | solution.py:295
  44.7 1.2 %project.4 = bf16[128,2048]{1,0:T(8,128)(2,1)S(1)} custom-call(bf16[64,1600]{1,0:T(8,128)(2,1)S(1)} %select_select_fusion.refs_0_, bf16[64,1600]{1,0:T(8,128)(2,1)S(1)} %collective-permute-done.4.refs_1_, bf16[64,1600]{1,0:T(8,128)(2,1)S(1)} %collective-permute-done.5.refs_2_, bf16[64,1600]{1,0:T(8,128)(2,1)S(1)} %collective-permute-done.6.refs_3_, ...), custom_call_target="tpu_custom_call" | custom-call | flops 838860800 | tf_op jit(solution)/shard_map/project/pallas_call | solution.py:330
  45.9 0.1 collective-permute-start.7
  46.0 3.5 %fetch.4.weight = bf16[2048,2048]{1,0:T(8,128)(2,1)S(1)} custom-call(bf16[2048,2048]{1,0:T(8,128)(2,1)} %refs_0_.6), custom_call_target="tpu_custom_call" | custom-call | flops 268435456 | tf_op jit(solution)/shard_map/fetch/pallas_call | solution.py:295
  49.5 0.0 copy-start
  49.5 1.2 %project.3.keep = f32[128,2048]{1,0:T(8,128)S(1)} custom-call(bf16[64,1600]{1,0:T(8,128)(2,1)S(1)} %select_select_fusion.refs_0_, bf16[64,1600]{1,0:T(8,128)(2,1)S(1)} %collective-permute-done.4.refs_1_, bf16[64,1600]{1,0:T(8,128)(2,1)S(1)} %collective-permute-done.5.refs_2_, bf16[64,1600]{1,0:T(8,128)(2,1)S(1)} %collective-permute-done.6.refs_3_, ...), custom_call_target="tpu_custom_call" | custom-call | flops 838860800 | tf_op jit(solution)/shard_map/project/pallas_call | solution.py:330
  50.7 3.9 %collective-permute-done.19.other = bf16[128,2048]{1,0:T(8,128)(2,1)S(1)} collective-permute-done((bf16[128,2048]{1,0:T(8,128)(2,1)S(1)}, bf16[128,2048]{1,0:T(8,128)(2,1)S(1)}, u32[]{:S(2)}, u32[]{:S(2)}) %collective-permute-start.19) | collective-permute-done | bytes 524320 | tf_op jit(solution)/shard_map/ppermute | solution.py:563
  54.5 1.3 %heads.3 = (bf16[128,2048]{1,0:T(8,128)(2,1)S(1)}, f32[520,128]{1,0:T(8,128)S(1)}, bf16[520,128]{1,0:T(8,128)(2,1)S(1)}, bf16[520,128]{1,0:T(8,128)(2,1)S(1)}, bf16[520,128]{1,0:T(8,128)(2,1)S(1)}) custom-call(f32[128,2048]{1,0:T(8,128)S(1)} %get-tuple-element.34.keep, bf16[128,2048]{1,0:T(8,128)(2,1)S(1)} %collective-permute-done.19.other, ...), custom_call_target="tpu_custom_call" | custom-call | flops 1073741824 | tf_op jit(solution)/shard_map/heads/pallas_call | solution.py:403
  55.9 2.8 %collective-permute-start.25 = (bf16[128,2048]{1,0:T(8,128)(2,1)S(1)}, bf16[128,2048]{1,0:T(8,128)(2,1)S(1)}, u32[]{:S(2)}, u32[]{:S(2)}) collective-permute-start(bf16[128,2048]{1,0:T(8,128)(2,1)S(1)} %get-tuple-element.41.kept0), channel_id=1, source_target_pairs={{0,16},{8,24},{1,17},{9,25},{2,18},{10,26},{3,19},{11,27},{4,20},{... | collective-permute-start | bytes 1572872 | tf_op jit(solution)/shard_map/ppermute | solution.py:574
  58.7 5.1 %collective-permute-done.7.other = bf16[128,2048]{1,0:T(8,128)(2,1)S(1)} collective-permute-done((bf16[128,2048]{1,0:T(8,128)(2,1)S(1)}, bf16[128,2048]{1,0:T(8,128)(2,1)S(1)}, u32[]{:S(2)}, u32[]{:S(2)}) %collective-permute-start.7) | collective-permute-done | bytes 524320 | tf_op jit(solution)/shard_map/ppermute | solution.py:563
  63.8 1.3 %heads.2 = (bf16[128,2048]{1,0:T(8,128)(2,1)S(1)}, f32[520,128]{1,0:T(8,128)S(1)}, bf16[520,128]{1,0:T(8,128)(2,1)S(1)}, bf16[520,128]{1,0:T(8,128)(2,1)S(1)}, bf16[520,128]{1,0:T(8,128)(2,1)S(1)}) custom-call(f32[128,2048]{1,0:T(8,128)S(1)} %project.3.keep, bf16[128,2048]{1,0:T(8,128)(2,1)S(1)} %collective-permute-done.7.other, f32[2048]{0:T(1024)S(1)} %copy-done, ...), custom_call_target="tpu_custom_call" | custom-call | flops 1073741824 | tf_op jit(solution)/shard_map/heads/pallas_call | solution.py:403
  65.1 2.1 %collective-permute-start.24 = (bf16[128,2048]{1,0:T(8,128)(2,1)S(1)}, bf16[128,2048]{1,0:T(8,128)(2,1)S(1)}, u32[]{:S(2)}, u32[]{:S(2)}) collective-permute-start(bf16[128,2048]{1,0:T(8,128)(2,1)S(1)} %get-tuple-element.40.kept1), channel_id=1, source_target_pairs={{0,16},{8,24},{1,17},{9,25},{2,18},{10,26},{3,19},{11,27},{4,20},{... | collective-permute-start | bytes 1572872 | tf_op jit(solution)/shard_map/ppermute | solution.py:574
  67.2 1.3 %collective-permute-start.20 = (bf16[520,128]{1,0:T(8,128)(2,1)S(1)}, bf16[520,128]{1,0:T(8,128)(2,1)S(1)}, u32[]{:S(2)}, u32[]{:S(2)}) collective-permute-start(bf16[520,128]{1,0:T(8,128)(2,1)S(1)} %get-tuple-element.37), channel_id=1, source_target_pairs={{0,1},{1,2},{2,3},{3,0},{4,5},{5,6},{6,7},{7,4},{8,9},{9,10},{10,1... | collective-permute-start | bytes 399368 | tf_op jit(solution)/shard_map/ppermute | solution.py:572
  68.5 3.4 %collective-permute-start.21 = (bf16[520,128]{1,0:T(8,128)(2,1)S(1)}, bf16[520,128]{1,0:T(8,128)(2,1)S(1)}, u32[]{:S(2)}, u32[]{:S(2)}) collective-permute-start(bf16[520,128]{1,0:T(8,128)(2,1)S(1)} %get-tuple-element.38), channel_id=1, source_target_pairs={{0,2},{1,3},{2,0},{3,1},{4,6},{5,7},{6,4},{7,5},{8,10},{9,11},{10,... | collective-permute-start | bytes 399368 | tf_op jit(solution)/shard_map/ppermute | solution.py:572
  71.9 1.4 %collective-permute-start.22 = (bf16[520,128]{1,0:T(8,128)(2,1)S(1)}, bf16[520,128]{1,0:T(8,128)(2,1)S(1)}, u32[]{:S(2)}, u32[]{:S(2)}) collective-permute-start(bf16[520,128]{1,0:T(8,128)(2,1)S(1)} %get-tuple-element.39), channel_id=1, source_target_pairs={{0,3},{1,0},{2,1},{3,2},{4,7},{5,4},{6,5},{7,6},{8,11},{9,8},{10,9... | collective-permute-start | bytes 399368 | tf_op jit(solution)/shard_map/ppermute | solution.py:572
  73.3 2.5 %collective-permute-done.20.refs_0_ = bf16[520,128]{1,0:T(8,128)(2,1)S(1)} collective-permute-done((bf16[520,128]{1,0:T(8,128)(2,1)S(1)}, bf16[520,128]{1,0:T(8,128)(2,1)S(1)}, u32[]{:S(2)}, u32[]{:S(2)}) %collective-permute-start.20) | collective-permute-done | bytes 133152 | tf_op jit(solution)/shard_map/ppermute | solution.py:572
  75.8 4.0 %collective-permute-start.8 = (bf16[520,128]{1,0:T(8,128)(2,1)S(1)}, bf16[520,128]{1,0:T(8,128)(2,1)S(1)}, u32[]{:S(2)}, u32[]{:S(2)}) collective-permute-start(bf16[520,128]{1,0:T(8,128)(2,1)S(1)} %get-tuple-element.27), channel_id=1, source_target_pairs={{0,1},{1,2},{2,3},{3,0},{4,5},{5,6},{6,7},{7,4},{8,9},{9,10},{10,1... | collective-permute-start | bytes 399368 | tf_op jit(solution)/shard_map/ppermute | solution.py:572
  79.8 3.3 %collective-permute-done.21.refs_1_ = bf16[520,128]{1,0:T(8,128)(2,1)S(1)} collective-permute-done((bf16[520,128]{1,0:T(8,128)(2,1)S(1)}, bf16[520,128]{1,0:T(8,128)(2,1)S(1)}, u32[]{:S(2)}, u32[]{:S(2)}) %collective-permute-start.21) | collective-permute-done | bytes 133152 | tf_op jit(solution)/shard_map/ppermute | solution.py:572
  83.1 4.9 %collective-permute-start.10 = (bf16[520,128]{1,0:T(8,128)(2,1)S(1)}, bf16[520,128]{1,0:T(8,128)(2,1)S(1)}, u32[]{:S(2)}, u32[]{:S(2)}) collective-permute-start(bf16[520,128]{1,0:T(8,128)(2,1)S(1)} %get-tuple-element.29), channel_id=1, source_target_pairs={{0,3},{1,0},{2,1},{3,2},{4,7},{5,4},{6,5},{7,6},{8,11},{9,8},{10,9... | collective-permute-start | bytes 399368 | tf_op jit(solution)/shard_map/ppermute | solution.py:572
  88.1 0.2 finish.3.kept0
  88.3 1.3 %collective-permute-start.23 = (bf16[128,512]{1,0:T(8,128)(2,1)S(1)}, bf16[128,512]{1,0:T(8,128)(2,1)S(1)}, u32[]{:S(2)}, u32[]{:S(2)}) collective-permute-start(bf16[128,512]{1,0:T(8,128)(2,1)S(1)} %finish.3.kept0), channel_id=1, source_target_pairs={{0,16},{8,24},{1,17},{9,25},{2,18},{10,26},{3,19},{11,27},{4,20},{... | collective-permute-start | bytes 393224 | tf_op jit(solution)/shard_map/ppermute | solution.py:576
  89.6 2.0 %collective-permute-done.9.refs_1_ = bf16[520,128]{1,0:T(8,128)(2,1)S(1)} collective-permute-done((bf16[520,128]{1,0:T(8,128)(2,1)S(1)}, bf16[520,128]{1,0:T(8,128)(2,1)S(1)}, u32[]{:S(2)}, u32[]{:S(2)}) %collective-permute-start.9) | collective-permute-done | bytes 133152 | tf_op jit(solution)/shard_map/ppermute | solution.py:572
  91.6 0.2 collective-permute-done.10.refs_2_
  91.8 0.2 finish.2.kept1
  92.0 1.3 %collective-permute-start.11 = (bf16[128,512]{1,0:T(8,128)(2,1)S(1)}, bf16[128,512]{1,0:T(8,128)(2,1)S(1)}, u32[]{:S(2)}, u32[]{:S(2)}) collective-permute-start(bf16[128,512]{1,0:T(8,128)(2,1)S(1)} %finish.2.kept1), channel_id=1, source_target_pairs={{0,16},{8,24},{1,17},{9,25},{2,18},{10,26},{3,19},{11,27},{4,20},{... | collective-permute-start | bytes 393224 | tf_op jit(solution)/shard_map/ppermute | solution.py:576
  93.3 0.8 place.4.before
  94.2 1.4 %place.6.before = bf16[512,2048]{1,0:T(8,128)(2,1)} custom-call(bf16[128,2048]{1,0:T(8,128)(2,1)S(1)} %get-tuple-element.41.kept0, bf16[128,2048]{1,0:T(8,128)(2,1)S(1)} %get-tuple-element.40.kept1, bf16[128,2048]{1,0:T(8,128)(2,1)S(1)} %collective-permute-done.25.moved0), custom_call_target="tpu_custom_call" | custom-call | flops 67108864 | tf_op jit(solution)/shard_map/place/pallas_call | solution.py:475
  95.6 0.2 collective-permute-done.11.moved1
  (23 shorter events, 0.2 us)
Async XLA Ops:
  2.0 10.8 %collective-permute-start = (bf16[64,1600]{1,0:T(8,128)(2,1)S(1)}, bf16[64,1600]{1,0:T(8,128)(2,1)S(1)}, u32[]{:S(2)}, u32[]{:S(2)}) collective-permute-start(bf16[64,1600]{1,0:T(8,128)(2,1)S(1)} %get-tuple-element.22), channel_id=1, source_target_pairs={{8,12},{12,28},{9,13},{13,29},{10,14},{14,30},{11,15},{15,31}} | collective-permute-start | bytes 614408 | tf_op jit(solution)/shard_map/ppermute | solution.py:547
  2.7 11.4 %collective-permute-start.1 = (bf16[64,1600]{1,0:T(8,128)(2,1)S(1)}, bf16[64,1600]{1,0:T(8,128)(2,1)S(1)}, u32[]{:S(2)}, u32[]{:S(2)}) collective-permute-start(bf16[64,1600]{1,0:T(8,128)(2,1)S(1)} %get-tuple-element.23), channel_id=1, source_target_pairs={{8,8},{12,24},{9,9},{13,25},{10,10},{14,26},{11,11},{15,27}} | collective-permute-start | bytes 614408 | tf_op jit(solution)/shard_map/ppermute | solution.py:547
  3.4 12.0 %collective-permute-start.2 = (bf16[64,1600]{1,0:T(8,128)(2,1)S(1)}, bf16[64,1600]{1,0:T(8,128)(2,1)S(1)}, u32[]{:S(2)}, u32[]{:S(2)}) collective-permute-start(bf16[64,1600]{1,0:T(8,128)(2,1)S(1)} %get-tuple-element.24), channel_id=1, source_target_pairs={{8,4},{12,20},{9,5},{13,21},{10,6},{14,22},{11,7},{15,23}} | collective-permute-start | bytes 614408 | tf_op jit(solution)/shard_map/ppermute | solution.py:547
  4.1 12.0 %collective-permute-start.3 = (bf16[64,1600]{1,0:T(8,128)(2,1)S(1)}, bf16[64,1600]{1,0:T(8,128)(2,1)S(1)}, u32[]{:S(2)}, u32[]{:S(2)}) collective-permute-start(bf16[64,1600]{1,0:T(8,128)(2,1)S(1)} %get-tuple-element.25), channel_id=1, source_target_pairs={{8,0},{12,16},{9,1},{13,17},{10,2},{14,18},{11,3},{15,19}} | collective-permute-start | bytes 614408 | tf_op jit(solution)/shard_map/ppermute | solution.py:547
  5.4 13.5 %collective-permute-start.12 = (bf16[64,640]{1,0:T(8,128)(2,1)S(1)}, bf16[64,640]{1,0:T(8,128)(2,1)S(1)}, u32[]{:S(2)}, u32[]{:S(2)}) collective-permute-start(bf16[64,640]{1,0:T(8,128)(2,1)S(1)} %get-tuple-element.30), channel_id=1, source_target_pairs={{0,12},{4,28},{1,13},{5,29},{2,14},{6,30},{3,15},{7,31}} | collective-permute-start | bytes 245768 | tf_op jit(solution)/shard_map/ppermute | solution.py:547
  12.8 6.0 %collective-permute-start.13 = (bf16[64,640]{1,0:T(8,128)(2,1)S(1)}, bf16[64,640]{1,0:T(8,128)(2,1)S(1)}, u32[]{:S(2)}, u32[]{:S(2)}) collective-permute-start(bf16[64,640]{1,0:T(8,128)(2,1)S(1)} %get-tuple-element.31), channel_id=1, source_target_pairs={{0,8},{4,24},{1,9},{5,25},{2,10},{6,26},{3,11},{7,27}} | collective-permute-start | bytes 245768 | tf_op jit(solution)/shard_map/ppermute | solution.py:547
  14.1 4.7 %collective-permute-start.14 = (bf16[64,640]{1,0:T(8,128)(2,1)S(1)}, bf16[64,640]{1,0:T(8,128)(2,1)S(1)}, u32[]{:S(2)}, u32[]{:S(2)}) collective-permute-start(bf16[64,640]{1,0:T(8,128)(2,1)S(1)} %get-tuple-element.32), channel_id=1, source_target_pairs={{0,4},{4,20},{1,5},{5,21},{2,6},{6,22},{3,7},{7,23}} | collective-permute-start | bytes 245768 | tf_op jit(solution)/shard_map/ppermute | solution.py:547
  15.4 3.4 %collective-permute-start.15 = (bf16[64,640]{1,0:T(8,128)(2,1)S(1)}, bf16[64,640]{1,0:T(8,128)(2,1)S(1)}, u32[]{:S(2)}, u32[]{:S(2)}) collective-permute-start(bf16[64,640]{1,0:T(8,128)(2,1)S(1)} %get-tuple-element.33), channel_id=1, source_target_pairs={{0,0},{4,16},{1,1},{5,17},{2,2},{6,18},{3,3},{7,19}} | collective-permute-start | bytes 245768 | tf_op jit(solution)/shard_map/ppermute | solution.py:547
  16.2 13.0 %collective-permute-start.5 = (bf16[64,1600]{1,0:T(8,128)(2,1)S(1)}, bf16[64,1600]{1,0:T(8,128)(2,1)S(1)}, u32[]{:S(2)}, u32[]{:S(2)}) collective-permute-start(bf16[64,1600]{1,0:T(8,128)(2,1)S(1)} %select_select_fusion.refs_0_), channel_id=1, source_target_pairs={{0,2},{1,3},{2,0},{3,1},{4,6},{5,7},{6,4},{7,5},{8,10},{9,11},{10,... | collective-permute-start | bytes 614408 | tf_op jit(solution)/shard_map/ppermute | solution.py:552
  18.9 12.4 %collective-permute-start.17 = (bf16[64,640]{1,0:T(8,128)(2,1)S(1)}, bf16[64,640]{1,0:T(8,128)(2,1)S(1)}, u32[]{:S(2)}, u32[]{:S(2)}) collective-permute-start(bf16[64,640]{1,0:T(8,128)(2,1)S(1)} %select_select_fusion.1.refs_0_), channel_id=1, source_target_pairs={{0,2},{1,3},{2,0},{3,1},{4,6},{5,7},{6,4},{7,5},{8,10},{9,11},{10,... | collective-permute-start | bytes 245768 | tf_op jit(solution)/shard_map/ppermute | solution.py:552
  20.1 24.6 %collective-permute-start.4 = (bf16[64,1600]{1,0:T(8,128)(2,1)S(1)}, bf16[64,1600]{1,0:T(8,128)(2,1)S(1)}, u32[]{:S(2)}, u32[]{:S(2)}) collective-permute-start(bf16[64,1600]{1,0:T(8,128)(2,1)S(1)} %select_select_fusion.refs_0_), channel_id=1, source_target_pairs={{0,1},{1,0},{2,3},{3,2},{4,5},{5,4},{6,7},{7,6},{8,9},{9,8},{10,11... | collective-permute-start | bytes 614408 | tf_op jit(solution)/shard_map/ppermute | solution.py:552
  29.2 15.5 %collective-permute-start.6 = (bf16[64,1600]{1,0:T(8,128)(2,1)S(1)}, bf16[64,1600]{1,0:T(8,128)(2,1)S(1)}, u32[]{:S(2)}, u32[]{:S(2)}) collective-permute-start(bf16[64,1600]{1,0:T(8,128)(2,1)S(1)} %collective-permute-done.5.refs_2_), channel_id=1, source_target_pairs={{0,1},{1,0},{2,3},{3,2},{4,5},{5,4},{6,7},{7,6},{8,9},{9,8},{10,11... | collective-permute-start | bytes 614408 | tf_op jit(solution)/shard_map/ppermute | solution.py:552
  29.2 8.1 %collective-permute-start.16 = (bf16[64,640]{1,0:T(8,128)(2,1)S(1)}, bf16[64,640]{1,0:T(8,128)(2,1)S(1)}, u32[]{:S(2)}, u32[]{:S(2)}) collective-permute-start(bf16[64,640]{1,0:T(8,128)(2,1)S(1)} %select_select_fusion.1.refs_0_), channel_id=1, source_target_pairs={{0,1},{1,0},{2,3},{3,2},{4,5},{5,4},{6,7},{7,6},{8,9},{9,8},{10,11... | collective-permute-start | bytes 245768 | tf_op jit(solution)/shard_map/ppermute | solution.py:552
  31.2 7.0 %collective-permute-start.18 = (bf16[64,640]{1,0:T(8,128)(2,1)S(1)}, bf16[64,640]{1,0:T(8,128)(2,1)S(1)}, u32[]{:S(2)}, u32[]{:S(2)}) collective-permute-start(bf16[64,640]{1,0:T(8,128)(2,1)S(1)} %collective-permute-done.17.refs_2_), channel_id=1, source_target_pairs={{0,1},{1,0},{2,3},{3,2},{4,5},{5,4},{6,7},{7,6},{8,9},{9,8},{10,11... | collective-permute-start | bytes 245768 | tf_op jit(solution)/shard_map/ppermute | solution.py:552
  39.2 15.3 %collective-permute-start.19 = (bf16[128,2048]{1,0:T(8,128)(2,1)S(1)}, bf16[128,2048]{1,0:T(8,128)(2,1)S(1)}, u32[]{:S(2)}, u32[]{:S(2)}) collective-permute-start(bf16[128,2048]{1,0:T(8,128)(2,1)S(1)} %get-tuple-element.35), channel_id=1, source_target_pairs={{0,4},{4,0},{1,5},{5,1},{2,6},{6,2},{3,7},{7,3},{8,12},{12,8},{9,1... | collective-permute-start | bytes 1572872 | tf_op jit(solution)/shard_map/ppermute | solution.py:563
  45.9 17.9 %collective-permute-start.7 = (bf16[128,2048]{1,0:T(8,128)(2,1)S(1)}, bf16[128,2048]{1,0:T(8,128)(2,1)S(1)}, u32[]{:S(2)}, u32[]{:S(2)}) collective-permute-start(bf16[128,2048]{1,0:T(8,128)(2,1)S(1)} %project.4), channel_id=1, source_target_pairs={{0,4},{4,0},{1,5},{5,1},{2,6},{6,2},{3,7},{7,3},{8,12},{12,8},{9,1... | collective-permute-start | bytes 1572872 | tf_op jit(solution)/shard_map/ppermute | solution.py:563
  49.5 5.1 %copy-start = (f32[2048]{0:T(1024)S(1)}, f32[2048]{0:T(1024)}, u32[]{:S(2)}) copy-start(f32[2048]{0:T(1024)} %gain.3) | copy-start | bytes 24580
  55.9 38.3 %collective-permute-start.25 = (bf16[128,2048]{1,0:T(8,128)(2,1)S(1)}, bf16[128,2048]{1,0:T(8,128)(2,1)S(1)}, u32[]{:S(2)}, u32[]{:S(2)}) collective-permute-start(bf16[128,2048]{1,0:T(8,128)(2,1)S(1)} %get-tuple-element.41.kept0), channel_id=1, source_target_pairs={{0,16},{8,24},{1,17},{9,25},{2,18},{10,26},{3,19},{11,27},{4,20},{... | collective-permute-start | bytes 1572872 | tf_op jit(solution)/shard_map/ppermute | solution.py:574
  65.1 30.7 %collective-permute-start.24 = (bf16[128,2048]{1,0:T(8,128)(2,1)S(1)}, bf16[128,2048]{1,0:T(8,128)(2,1)S(1)}, u32[]{:S(2)}, u32[]{:S(2)}) collective-permute-start(bf16[128,2048]{1,0:T(8,128)(2,1)S(1)} %get-tuple-element.40.kept1), channel_id=1, source_target_pairs={{0,16},{8,24},{1,17},{9,25},{2,18},{10,26},{3,19},{11,27},{4,20},{... | collective-permute-start | bytes 1572872 | tf_op jit(solution)/shard_map/ppermute | solution.py:574
  67.2 8.6 %collective-permute-start.20 = (bf16[520,128]{1,0:T(8,128)(2,1)S(1)}, bf16[520,128]{1,0:T(8,128)(2,1)S(1)}, u32[]{:S(2)}, u32[]{:S(2)}) collective-permute-start(bf16[520,128]{1,0:T(8,128)(2,1)S(1)} %get-tuple-element.37), channel_id=1, source_target_pairs={{0,1},{1,2},{2,3},{3,0},{4,5},{5,6},{6,7},{7,4},{8,9},{9,10},{10,1... | collective-permute-start | bytes 399368 | tf_op jit(solution)/shard_map/ppermute | solution.py:572
  68.5 14.7 %collective-permute-start.21 = (bf16[520,128]{1,0:T(8,128)(2,1)S(1)}, bf16[520,128]{1,0:T(8,128)(2,1)S(1)}, u32[]{:S(2)}, u32[]{:S(2)}) collective-permute-start(bf16[520,128]{1,0:T(8,128)(2,1)S(1)} %get-tuple-element.38), channel_id=1, source_target_pairs={{0,2},{1,3},{2,0},{3,1},{4,6},{5,7},{6,4},{7,5},{8,10},{9,11},{10,... | collective-permute-start | bytes 399368 | tf_op jit(solution)/shard_map/ppermute | solution.py:572
  71.9 11.3 %collective-permute-start.22 = (bf16[520,128]{1,0:T(8,128)(2,1)S(1)}, bf16[520,128]{1,0:T(8,128)(2,1)S(1)}, u32[]{:S(2)}, u32[]{:S(2)}) collective-permute-start(bf16[520,128]{1,0:T(8,128)(2,1)S(1)} %get-tuple-element.39), channel_id=1, source_target_pairs={{0,3},{1,0},{2,1},{3,2},{4,7},{5,4},{6,5},{7,6},{8,11},{9,8},{10,9... | collective-permute-start | bytes 399368 | tf_op jit(solution)/shard_map/ppermute | solution.py:572
  75.8 12.5 %collective-permute-start.8 = (bf16[520,128]{1,0:T(8,128)(2,1)S(1)}, bf16[520,128]{1,0:T(8,128)(2,1)S(1)}, u32[]{:S(2)}, u32[]{:S(2)}) collective-permute-start(bf16[520,128]{1,0:T(8,128)(2,1)S(1)} %get-tuple-element.27), channel_id=1, source_target_pairs={{0,1},{1,2},{2,3},{3,0},{4,5},{5,6},{6,7},{7,4},{8,9},{9,10},{10,1... | collective-permute-start | bytes 399368 | tf_op jit(solution)/shard_map/ppermute | solution.py:572
  83.1 8.5 %collective-permute-start.9 = (bf16[520,128]{1,0:T(8,128)(2,1)S(1)}, bf16[520,128]{1,0:T(8,128)(2,1)S(1)}, u32[]{:S(2)}, u32[]{:S(2)}) collective-permute-start(bf16[520,128]{1,0:T(8,128)(2,1)S(1)} %get-tuple-element.28), channel_id=1, source_target_pairs={{0,2},{1,3},{2,0},{3,1},{4,6},{5,7},{6,4},{7,5},{8,10},{9,11},{10,... | collective-permute-start | bytes 399368 | tf_op jit(solution)/shard_map/ppermute | solution.py:572
  83.1 8.7 %collective-permute-start.10 = (bf16[520,128]{1,0:T(8,128)(2,1)S(1)}, bf16[520,128]{1,0:T(8,128)(2,1)S(1)}, u32[]{:S(2)}, u32[]{:S(2)}) collective-permute-start(bf16[520,128]{1,0:T(8,128)(2,1)S(1)} %get-tuple-element.29), channel_id=1, source_target_pairs={{0,3},{1,0},{2,1},{3,2},{4,7},{5,4},{6,5},{7,6},{8,11},{9,8},{10,9... | collective-permute-start | bytes 399368 | tf_op jit(solution)/shard_map/ppermute | solution.py:572
  88.3 5.1 %collective-permute-start.23 = (bf16[128,512]{1,0:T(8,128)(2,1)S(1)}, bf16[128,512]{1,0:T(8,128)(2,1)S(1)}, u32[]{:S(2)}, u32[]{:S(2)}) collective-permute-start(bf16[128,512]{1,0:T(8,128)(2,1)S(1)} %finish.3.kept0), channel_id=1, source_target_pairs={{0,16},{8,24},{1,17},{9,25},{2,18},{10,26},{3,19},{11,27},{4,20},{... | collective-permute-start | bytes 393224 | tf_op jit(solution)/shard_map/ppermute | solution.py:576
  92.0 3.8 %collective-permute-start.11 = (bf16[128,512]{1,0:T(8,128)(2,1)S(1)}, bf16[128,512]{1,0:T(8,128)(2,1)S(1)}, u32[]{:S(2)}, u32[]{:S(2)}) collective-permute-start(bf16[128,512]{1,0:T(8,128)(2,1)S(1)} %finish.2.kept1), channel_id=1, source_target_pairs={{0,16},{8,24},{1,17},{9,25},{2,18},{10,26},{3,19},{11,27},{4,20},{... | collective-permute-start | bytes 393224 | tf_op jit(solution)/shard_map/ppermute | solution.py:576
